TPU v7x, 32 devices: a whole 2x2x4 slice. The times are simulated.
32 devices in a mesh: dp: 16 (over z, x, core), mp: 2 (over y).
Axes of the slice: x: 2, y: 2, z: 4, core: 2. Of those that a mesh axis runs over, the one named last changes fastest.
Arguments:
- node_feats: bfloat16 [256, 32768], P('mp', 'dp'), may hold values from -6 to 6
- proj_weight: bfloat16 [256, 256], P('mp'), may hold values from -0.375 to 0.375
- att_src: float32 [256], P('mp'), may hold values from -32 to 32
- att_dst: float32 [256], P('mp'), may hold values from -32 to 32
- out_bias: float32 [256], P('mp'), may hold values from -3 to 3
- tile_rows: int32 [512], P('dp'), may hold values from 0 to 255, as said below
- tile_cols: int32 [512], P('dp'), may hold values from 0 to 255, as said below
- tile_masks: int32 [512, 4, 128], P('dp'), may hold values from -2147483648 to 2147483646
Outputs:
- node_out: bfloat16 [256, 32768], P('mp', 'dp')
Inputs may be any that keep to these rules, and one draw needn't show every extreme that they name: `tile_rows`: block b holds nodes 128 b to 128 b + 127 and belongs to index b // 16 of dp. Among the 32 tiles of one index of dp, no owner's blocks are named more than 4 times; on every index one owner's blocks are named exactly 4 times. `tile_cols`: the same bound holds for source blocks: among the 32 tiles of one index of dp, no owner's blocks are named more than 4 times, and one owner's exactly 4 times on every index.
All inputs are finite; a program needn't handle non-finite values.
Results may differ from a plain program's by a relative error of at most 0.0034.
Values may be sent and summed in bfloat16 or wider, within the bound.
No kernel may reach another device: no remote copies, remote signals or barrier semaphores. Data moves between devices by JAX's collectives and lax.ppermute only.
A program may use at most 64 MiB of HBM per device.

v0:
```python
import functools

import jax
import jax.numpy as jnp
from jax import lax
from jax.experimental import pallas as pl
from jax.experimental.pallas import tpu as pltpu
from jax.sharding import PartitionSpec as P


HD = 32
LOG2E = 1.4426950408889634
FAR = -1e30
F32 = jnp.float32
BF16 = jnp.bfloat16


GROUP = 2
LIMIT = 16 * 1024 * 1024

VMEM = pl.BlockSpec(memory_space=pltpu.VMEM)
SMEM = pl.BlockSpec(memory_space=pltpu.SMEM)


def split(value, size):
    if size & (size - 1) == 0:
        return value >> (size.bit_length() - 1), value & (size - 1)
    return lax.div(value, jnp.int32(size)), lax.rem(value, jnp.int32(size))


def pad8(count):
    return -(-count // 8) * 8


def leaky(scores):
    return jnp.maximum(scores, 0.2 * scores)


def head_sums(rows):
    return jnp.sum(rows.reshape(rows.shape[0] // HD, HD, rows.shape[1]), axis=1)


def stack_rows(pieces, total):
    have = sum(p.shape[0] for p in pieces)
    if have < total:
        pieces = pieces + [jnp.zeros((total - have, pieces[0].shape[1]), F32)]
    return jnp.concatenate(pieces, axis=0)


def ring_order(chips):
    columns = max(1, chips // 4)
    rows = chips // columns
    if columns == 1:
        return list(range(chips))
    order = [row * columns for row in range(rows)]
    for row in reversed(range(rows)):
        inner = list(range(1, columns))
        order += [row * columns + col for col in (inner if (rows - 1 - row) % 2 == 0 else inner[::-1])]
    return order


def project_kernel(parts, mp_ref, w_ref, att_ref, *refs):
    x_refs, (pay_ref, sc_ref) = refs[:parts], refs[parts:]
    me = mp_ref[0]
    depth = w_ref.shape[1] // parts
    total = None
    for k in range(parts):
        at = pl.multiple_of((me ^ k) * depth, depth) if parts > 1 else 0
        term = jnp.dot(w_ref[:, pl.ds(at, depth)], x_refs[k][...], preferred_element_type=F32)
        total = term if total is None else total + term
    rounded = total.astype(BF16)
    a_src, a_dst = att_ref[:, 0:1], att_ref[:, 1:2]
    source = head_sums(total * a_src)
    target = head_sums(total * a_dst)
    rest = source - head_sums(rounded.astype(F32) * a_src)
    rest_hi = rest.astype(BF16).astype(F32)
    extra = stack_rows([rest_hi, rest - rest_hi], pay_ref.shape[1] - rounded.shape[0]).astype(BF16)
    scores = stack_rows([target, leaky(source + target)], sc_ref.shape[1])
    dims, tile = rounded.shape[0], pay_ref.shape[2]
    for b in range(pay_ref.shape[0]):
        at = slice(b * tile, (b + 1) * tile)
        pay_ref[b, :dims, :] = rounded[:, at]
        pay_ref[b, dims:, :] = extra[:, at]
        sc_ref[b] = scores[:, at]


def pack_kernel(blocks, chips, groups, rows_ref, cols_ref, place_ref, masks_ref, out_ref, count):
    devices, slots = out_ref.shape[0], out_ref.shape[1] - 1
    words = out_ref.shape[2:]
    half = blocks // 2
    lane = lax.broadcasted_iota(jnp.int32, words, 1)
    for d in range(devices):
        count[d] = 0
        out_ref[d, slots] = jnp.zeros(words, jnp.int32)

    def body(t, carry):
        row, col = rows_ref[t], cols_ref[t]
        owner, row_at = split(row, blocks)
        holder, col_at = split(col, blocks)
        parity = holder & 1
        other = (owner ^ parity) & 1
        goal = (owner & -2) + parity
        at = count[goal]
        count[goal] = at + 1
        out_ref[goal, at] = masks_ref[t]
        back = place_ref[owner >> 1] - place_ref[holder >> 1]
        back = jnp.where(back < 0, back + chips, back)
        step = jnp.minimum(back, chips - back)
        part, j = split(col_at, half)
        far = 2 * back == chips
        buf = part + jnp.where((back > step) & ~far, 2, 0)
        group = step + jnp.where(far & (other == 0), 1, 0)
        code = (((row_at + other * blocks) * 4 + buf) * half + j) * groups + group
        here = out_ref[goal, slots]
        here = jnp.where(lane == at, code, jnp.where(lane == slots, at + 1, here))
        out_ref[goal, slots] = here
        return carry

    lax.fori_loop(0, rows_ref.shape[0], body, 0)


def list_kernel(devices, slots, groups, ids_ref, list_ref, count_ref):
    total = list_ref.shape[0] // groups
    for g in range(groups):
        count_ref[g] = 0

    for d in range(devices):
        def body(n, carry, d=d):
            code, group = split(ids_ref[d * (slots + 1) + n], groups)
            at = count_ref[group]
            list_ref[group * total + at] = (code * (devices * (slots + 1)) + d * (slots + 1) + n) * 2 + 1
            count_ref[group] = at + 1
            return carry

        lax.fori_loop(0, ids_ref[d * (slots + 1) + slots], body, 0)
    for g in range(groups):
        at = count_ref[g]
        for k in range(GROUP - 1):
            list_ref[g * total + at + k] = 0
        count_ref[g] = lax.div(at + GROUP - 1, jnp.int32(GROUP))


def tile_bundle(entries, masks_total, half, dims, masks_ref, tscore, att, buf, state):
    heads = dims // HD
    tile = masks_ref.shape[2]
    up = 31 - lax.broadcasted_iota(jnp.int32, (32, tile), 0)
    work = []
    for entry in entries:
        valid = -(entry & 1)
        code, slot = split(entry >> 1, masks_total)
        code, at = split(code, half)
        row, which = split(code, 4)
        packed = masks_ref[slot] & valid
        block = [
            jnp.where((jnp.broadcast_to(packed[w : w + 1], (32, tile)) << up) < 0, 0.0, FAR)
            for w in range(packed.shape[0])
        ]
        block = jnp.concatenate(block, axis=0)
        feats = buf[which, at, :dims, :]
        extra = buf[which, at, dims:, :].astype(F32)
        source = head_sums(feats.astype(F32) * att) + extra[:heads] + extra[heads : 2 * heads]
        columns = jnp.transpose(stack_rows([source], pad8(heads)))
        tops = [
            jnp.max(jnp.broadcast_to(columns[:, h : h + 1], (tile, tile)) + block, axis=0, keepdims=True)
            for h in range(heads)
        ]
        work.append((row, feats, block, columns, jnp.concatenate(tops, axis=0)))
    moved = []
    for row, _, _, _, tops in work:
        target = tscore[row, :heads, :]
        old = state[row, dims : dims + heads, :]
        new = jnp.maximum(old, leaky(target + tops))
        state[row, dims : dims + heads, :] = new
        moved.append((jnp.exp2(old - new), target - new, 0.2 * target - new))
    sums = []
    for (row, feats, block, columns, _), (alpha, up1, up2) in zip(work, moved):
        masses, values = [], []
        for h in range(heads):
            col = jnp.broadcast_to(columns[:, h : h + 1], (tile, tile))
            low = jnp.broadcast_to(0.2 * columns[:, h : h + 1], (tile, tile))
            raw = jnp.maximum(col + up1[h : h + 1], low + up2[h : h + 1])
            weight = jnp.exp2(raw + block)
            masses.append(jnp.sum(weight, axis=0, keepdims=True))
            values.append(
                jnp.dot(
                    feats[h * HD : (h + 1) * HD], weight.astype(BF16), preferred_element_type=F32
                )
            )
        sums.append((jnp.concatenate(masses, axis=0), values))
    for (row, _, _, _, _), (alpha, _, _), (mass, values) in zip(work, moved, sums):
        at = slice(dims + heads, dims + 2 * heads)
        state[row, at, :] = state[row, at, :] * alpha + mass
        for h in range(heads):
            at = slice(h * HD, (h + 1) * HD)
            state[row, at, :] = state[row, at, :] * alpha[h : h + 1] + values[h]


def stage_kernel(group, groups, first, hand, list_ref, count_ref, masks_ref, own_sc, other_sc, att_ref, *refs):
    if hand:
        *refs, other_out, tscore, buf = refs
        refs = [*refs, tscore, buf]
    if first:
        *pays, state, tscore, buf = refs
    else:
        *pays, _, state, tscore, buf = refs
    total = list_ref.shape[0] // groups
    blocks, dims = own_sc.shape[0], att_ref.shape[0]
    half = buf.shape[1]
    heads = dims // HD
    for k, pay in enumerate(pays):
        buf[k] = pay[...]
    tscore[:blocks] = own_sc[...]
    tscore[blocks:] = other_sc[...]
    if first:
        tile = state.shape[2]
        rest = state.shape[1] - dims - 2 * heads
        for b in range(blocks):
            state[b, :dims] = pays[b // half][b % half, :dims].astype(F32)
            state[b, dims : dims + heads] = own_sc[b, heads : 2 * heads]
            state[b, dims + heads : dims + 2 * heads] = jnp.ones((heads, tile), F32)
            state[blocks + b, :dims] = jnp.zeros((dims, tile), F32)
            state[blocks + b, dims : dims + heads] = jnp.full((heads, tile), FAR, F32)
            state[blocks + b, dims + heads :] = jnp.zeros((heads + rest, tile), F32)
            if rest:
                state[b, dims + 2 * heads :] = jnp.zeros((rest, tile), F32)
    att = att_ref[:, 0:1]

    def body(i, carry):
        at = group * total + i * GROUP
        entries = [list_ref[at + k] for k in range(GROUP)]
        tile_bundle(entries, masks_ref.shape[0], half, dims, masks_ref, tscore, att, buf, state)
        return carry

    lax.fori_loop(0, count_ref[group], body, 0)
    if hand:
        other_out[...] = state[blocks:]


def merge_kernel(state_ref, other_ref, x_ref, bias_ref, out_ref):
    blocks, dims, tile = other_ref.shape[0], x_ref.shape[0], other_ref.shape[2]
    heads = dims // HD
    bias = bias_ref[...]
    for b in range(blocks):
        m1, m2 = state_ref[b, dims : dims + heads], other_ref[b, dims : dims + heads]
        l1 = state_ref[b, dims + heads : dims + 2 * heads]
        l2 = other_ref[b, dims + heads : dims + 2 * heads]
        best = jnp.maximum(m1, m2)
        c1, c2 = jnp.exp2(m1 - best), jnp.exp2(m2 - best)
        scale = 1.0 / (l1 * c1 + l2 * c2)
        c1, c2 = (c1 * scale)[:, None, :], (c2 * scale)[:, None, :]
        mixed = state_ref[b, :dims].reshape(heads, HD, tile) * c1
        mixed = mixed + other_ref[b, :dims].reshape(heads, HD, tile) * c2
        at = slice(b * tile, (b + 1) * tile)
        v = mixed.reshape(dims, tile) + x_ref[:, at].astype(F32) + bias
        out_ref[:, at] = jnp.where(v > 0, v, jnp.exp(jnp.minimum(v, 0.0)) - 1.0).astype(BF16)


def call(kernel, outs, args, in_specs=None, out_specs=VMEM, scratch=(), aliases=None, flops=1000000):
    return pl.pallas_call(
        kernel,
        out_shape=outs,
        in_specs=in_specs or [VMEM] * len(args),
        out_specs=out_specs,
        scratch_shapes=list(scratch),
        input_output_aliases=aliases or {},
        compiler_params=pltpu.CompilerParams(vmem_limit_bytes=LIMIT),
        cost_estimate=pl.CostEstimate(flops=flops, bytes_accessed=0, transcendentals=0),
    )(*args)


def near(x):
    return pltpu.with_memory_space_constraint(x, pltpu.VMEM)


def local(node_feats, proj_weight, att_src, att_dst, out_bias, tile_rows, tile_cols, tile_masks):
    nodes = node_feats.shape[1]
    dims = proj_weight.shape[0]
    heads = dims // HD
    words, tile = tile_masks.shape[1:]
    blocks = nodes // tile
    tiles = tile_rows.shape[0]
    n_dp, n_mp = lax.axis_size("dp"), lax.axis_size("mp")
    chips = n_dp // 2
    slots = 2 * max(2, 2 * tiles // n_dp)
    half = blocks // 2
    extra = pad8(2 * heads)
    order = ring_order(chips)
    place = [order.index(c) for c in range(chips)]
    me_mp = lax.axis_index("mp")
    steps = chips // 2
    groups = 8
    while groups < steps + 2:
        groups *= 2

    def hop(step):
        pairs = []
        for p, c in enumerate(order):
            to = order[(p + step) % chips]
            pairs += [(2 * c, 2 * to), (2 * c + 1, 2 * to + 1)]
        return sorted(pairs)

    right, left = hop(1), hop(-1)
    swap = [(i, i ^ 1) for i in range(n_dp)]

    mine = jnp.full((1,), me_mp, jnp.int32)
    if n_mp == 2:
        flip = [(0, 1), (1, 0)]
        halves = [node_feats[:, k * (nodes // 2) : (k + 1) * (nodes // 2)] for k in range(2)]
        inputs = [[x, lax.ppermute(x, "mp", flip)] for x in halves]
    else:
        whole = lax.all_gather(node_feats, "mp", axis=0, tiled=True)
        inputs = [[whole[:, k * (nodes // 2) : (k + 1) * (nodes // 2)]] for k in range(2)]
    att = jnp.stack([att_src, att_dst], axis=1) * LOG2E

    packed = call(
        functools.partial(pack_kernel, blocks, chips, groups),
        pltpu.VMEM((n_dp, slots + 1, words, tile), jnp.int32),
        (tile_rows, tile_cols, jnp.array(place, jnp.int32), tile_masks),
        in_specs=[SMEM, SMEM, SMEM, VMEM],
        scratch=[pltpu.SMEM((n_dp,), jnp.int32)],
    )
    got = lax.all_to_all(packed, "dp", split_axis=0, concat_axis=0, tiled=True)

    pays, scs = [], []
    for xs in inputs:
        pay, sc = call(
            functools.partial(project_kernel, len(xs)),
            (pltpu.VMEM((half, dims + extra, tile), BF16), pltpu.VMEM((half, extra, tile), F32)),
            (mine, proj_weight, att, *[near(x) for x in xs]),
            in_specs=[SMEM] + [VMEM] * (2 + len(xs)),
            out_specs=(VMEM, VMEM),
        )
        pays.append(pay)
        scs.append(sc)
    own_sc = jnp.concatenate(scs, axis=0)
    other_sc = lax.ppermute(own_sc, "dp", swap)

    arrivals = [list(pays)]
    going = {w + p: pays["AB".index(p)] for w in "rl" for p in "AB"}
    for k in range(1, steps + 1):
        far = 2 * k == chips
        for way in ("rA", "lB") if far else ("rA", "lA", "rB", "lB"):
            pairs = right if way[0] == "r" else left
            going[way] = lax.ppermute(going[way], "dp", pairs)
        names = ("rA", "lB") if far else ("rA", "rB", "lA", "lB")
        arrivals.append([going[w] for w in names])

    ids = got[:, slots, 0, : slots + 1].reshape(n_dp * (slots + 1))
    total = n_dp * slots + GROUP
    lists, counts = call(
        functools.partial(list_kernel, n_dp, slots, groups),
        (
            jax.ShapeDtypeStruct((groups * total,), jnp.int32),
            jax.ShapeDtypeStruct((groups,), jnp.int32),
        ),
        (ids,),
        in_specs=[SMEM],
        out_specs=(SMEM, SMEM),
    )

    masks = near(got.reshape(n_dp * (slots + 1), words, tile))
    near_sc = (near(own_sc), near(other_sc))
    state_shape = pltpu.VMEM((2 * blocks, dims + extra, tile), F32)

    half_shape = pltpu.VMEM((blocks, dims + extra, tile), F32)

    def stage(g, bufs, state, hand=False):
        args = [lists, counts, masks, *near_sc, att, *[near(b) for b in bufs]]
        if state is not None:
            args.append(near(state))
        return call(
            functools.partial(stage_kernel, g, groups, state is None, hand),
            (state_shape, half_shape) if hand else state_shape,
            args,
            out_specs=(VMEM, VMEM) if hand else VMEM,
            in_specs=[SMEM, SMEM] + [VMEM] * (len(args) - 2),
            scratch=[
                pltpu.VMEM((2 * blocks, extra, tile), F32),
                pltpu.VMEM((len(bufs), half, dims + extra, tile), BF16),
            ],
            aliases={} if state is None else {len(args) - 1: 0},
            flops=8000000000,
        )

    state = None
    for g, bufs in enumerate(arrivals):
        state = stage(g, bufs, state, g == steps)
    state, other = state
    back = lax.ppermute(other, "dp", swap)
    state = stage(steps + 1, arrivals[-1], state)
    return call(
        merge_kernel,
        jax.ShapeDtypeStruct((dims, nodes), BF16),
        (near(state), near(back), node_feats, out_bias[:, None]),
    )


def solution(mesh):
    return jax.shard_map(
        local,
        mesh=mesh,
        in_specs=(
            P("mp", "dp"),
            P("mp", None),
            P("mp"),
            P("mp"),
            P("mp"),
            P("dp"),
            P("dp"),
            P("dp", None, None),
        ),
        out_specs=P("mp", "dp"),
        check_vma=False,
    )
```

profile of v0, /device:TPU:11, one launch (start us, length us, event | category | flops | bytes accessed | tf_op | source)
XLA Modules:
  0.0 81.5 jit_solution(9839101707137343302)
XLA Ops:
  0.0 1.1 %fusion = (bf16[128,1024]{1,0:T(8,128)(2,1)S(1)}, bf16[128,1024]{1,0:T(8,128)(2,1)S(1)}) fusion(bf16[128,2048]{1,0:T(8,128)(2,1)} %x_ref.1), kind=kLoop, calls=%fused_computation.5 | loop fusion | bytes 1048576 | tf_op jit(solution)/shard_map/slice | solution.py:308
  1.1 1.3 %collective-permute-start.1 = (bf16[128,1024]{1,0:T(8,128)(2,1)S(1)}, bf16[128,1024]{1,0:T(8,128)(2,1)S(1)}, u32[]{:S(2)}, u32[]{:S(2)}) collective-permute-start(bf16[128,1024]{1,0:T(8,128)(2,1)S(1)} %get-tuple-element.21.refs_0_), channel_id=1, source_target_pairs={{0,1},{1,0},{2,3},{3,2},{4,5},{5,4},{6,7},{7,6},{8,9},{9,8},{10,11... | collective-permute-start | bytes 786440 | tf_op jit(solution)/shard_map/ppermute | solution.py:309
  2.6 0.8 %copy-done.4 = s32[32,4,128]{2,1,0:T(4,128)S(1)} copy-done((s32[32,4,128]{2,1,0:T(4,128)S(1)}, s32[32,4,128]{2,1,0:T(4,128)}, u32[]{:S(2)}) %copy-start.4) | copy-done | bytes 65560
  5.4 2.0 %shard_map.91 = s32[16,9,4,128]{3,2,1,0:T(4,128)} custom-call(s32[32]{0:T(128)S(1)} %copy-done.5, s32[32]{0:T(128)S(1)} %copy-done.6, s32[8]{0:T(128)S(1)} %copy-done.7, s32[32,4,128]{2,1,0:T(4,128)S(1)} %copy-done.4), custom_call_target="tpu_custom_call" | custom-call | flops 1000000 | tf_op jit(solution)/shard_map/pallas_call | solution.py:259
  7.4 7.1 %all-to-all-start = ((s32[16,9,4,128]{3,2,1,0:T(4,128)}), s32[16,9,4,128]{3,2,1,0:T(4,128)S(1)}, u32[]{:S(2)}, u32[]{:S(2)}) async-start(s32[16,9,4,128]{3,2,1,0:T(4,128)} %shard_map.91), calls=%async_computation | async-start | bytes 589824 | tf_op jit(solution)/shard_map/all_to_all | solution.py:322
  16.1 1.2 %collective-permute-start.7 = (bf16[8,136,128]{2,1,0:T(8,128)(2,1)S(1)}, bf16[8,136,128]{2,1,0:T(8,128)(2,1)}, u32[]{:S(2)}, u32[]{:S(2)}) collective-permute-start(bf16[8,136,128]{2,1,0:T(8,128)(2,1)S(1)} %get-tuple-element.18.refs_1_), channel_id=1, source_target_pairs={{0,4},{2,6},{4,12},{6,14},{8,0},{10,2},{12,20},{14,22},{16,8},{18,... | collective-permute-start | bytes 835592 | tf_op jit(solution)/shard_map/ppermute | solution.py:344
  17.8 1.2 %collective-permute-start.14 = (bf16[8,136,128]{2,1,0:T(8,128)(2,1)S(1)}, bf16[8,136,128]{2,1,0:T(8,128)(2,1)S(1)}, u32[]{:S(2)}, u32[]{:S(2)}) collective-permute-start(bf16[8,136,128]{2,1,0:T(8,128)(2,1)S(1)} %get-tuple-element.17.refs_0_), channel_id=1, source_target_pairs={{0,4},{2,6},{4,12},{6,14},{8,0},{10,2},{12,20},{14,22},{16,8},{18,... | collective-permute-start | bytes 835592 | tf_op jit(solution)/shard_map/ppermute | solution.py:344
  20.0 1.6 %collective-permute-start.2 = (f32[16,8,128]{2,1,0:T(8,128)S(1)}, f32[16,8,128]{2,1,0:T(8,128)S(1)}, u32[]{:S(2)}, u32[]{:S(2)}) collective-permute-start(f32[16,8,128]{2,1,0:T(8,128)S(1)} %constant_dynamic-update-slice_fusion.own_sc), channel_id=1, source_target_pairs={{0,2},{2,0},{4,6},{6,4},{8,10},{10,8},{12,14},{14,12},{16,18},{18,... | collective-permute-start | bytes 196616 | tf_op jit(solution)/shard_map/ppermute | solution.py:336
  21.6 7.3 %collective-permute-done.11.refs_1_ = bf16[8,136,128]{2,1,0:T(8,128)(2,1)} collective-permute-done((bf16[8,136,128]{2,1,0:T(8,128)(2,1)S(1)}, bf16[8,136,128]{2,1,0:T(8,128)(2,1)}, u32[]{:S(2)}, u32[]{:S(2)}) %collective-permute-start.11) | collective-permute-done | bytes 278560 | tf_op jit(solution)/shard_map/ppermute | solution.py:344
  28.9 1.5 %collective-permute-start.8 = (bf16[8,136,128]{2,1,0:T(8,128)(2,1)}, bf16[8,136,128]{2,1,0:T(8,128)(2,1)}, u32[]{:S(2)}, u32[]{:S(2)}) collective-permute-start(bf16[8,136,128]{2,1,0:T(8,128)(2,1)} %collective-permute-done.7.refs_3_), channel_id=1, source_target_pairs={{0,4},{2,6},{4,12},{6,14},{8,0},{10,2},{12,20},{14,22},{16,8},{18,... | collective-permute-start | bytes 835592 | tf_op jit(solution)/shard_map/ppermute | solution.py:344
  30.4 2.8 %collective-permute-done.14.refs_2_ = bf16[8,136,128]{2,1,0:T(8,128)(2,1)S(1)} collective-permute-done((bf16[8,136,128]{2,1,0:T(8,128)(2,1)S(1)}, bf16[8,136,128]{2,1,0:T(8,128)(2,1)S(1)}, u32[]{:S(2)}, u32[]{:S(2)}) %collective-permute-start.14) | collective-permute-done | bytes 278560 | tf_op jit(solution)/shard_map/ppermute | solution.py:344
  33.2 2.3 %collective-permute-start.15 = (bf16[8,136,128]{2,1,0:T(8,128)(2,1)S(1)}, bf16[8,136,128]{2,1,0:T(8,128)(2,1)}, u32[]{:S(2)}, u32[]{:S(2)}) collective-permute-start(bf16[8,136,128]{2,1,0:T(8,128)(2,1)S(1)} %collective-permute-done.14.refs_2_), channel_id=1, source_target_pairs={{0,4},{2,6},{4,12},{6,14},{8,0},{10,2},{12,20},{14,22},{16,8},{18,... | collective-permute-start | bytes 835592 | tf_op jit(solution)/shard_map/ppermute | solution.py:344
  35.6 1.6 %shard_map.92 = (s32[1040]{0:T(1024)S(1)}, s32[8]{0:T(128)S(1)}) custom-call(s32[144]{0:T(256)S(1)} %reshape_squeeze.3.ids_ref), custom_call_target="tpu_custom_call" | custom-call | flops 1000000 | tf_op jit(solution)/shard_map/pallas_call | solution.py:259
  37.3 1.0 %copy-done.9 = bf16[8,136,128]{2,1,0:T(8,128)(2,1)S(1)} copy-done((bf16[8,136,128]{2,1,0:T(8,128)(2,1)S(1)}, bf16[8,136,128]{2,1,0:T(8,128)(2,1)}, u32[]{:S(2)}) %copy-start.9) | copy-done | bytes 278552
  38.2 1.0 %copy-done.11 = bf16[8,136,128]{2,1,0:T(8,128)(2,1)S(1)} copy-done((bf16[8,136,128]{2,1,0:T(8,128)(2,1)S(1)}, bf16[8,136,128]{2,1,0:T(8,128)(2,1)}, u32[]{:S(2)}) %copy-start.11) | copy-done | bytes 278552
  39.2 2.4 %shard_map.95.refs_4_ = f32[32,136,128]{2,1,0:T(8,128)S(1)} custom-call(s32[1040]{0:T(1024)S(1)} %get-tuple-element.13.list_ref, s32[8]{0:T(128)S(1)} %get-tuple-element.14.count_ref, s32[144,4,128]{2,1,0:T(4,128)S(1)} %bitcast.5, f32[16,8,128]{2,1,0:T(8,128)S(1)} %constant_dynamic-update-slice_fusion.own_sc, ...), custom_call_target="tpu_custom_call" | custom-call | flops 8000000000 | tf_op jit(solution)/shard_map/pallas_call | solution.py:259
  41.6 3.6 %shard_map.96.refs_4_ = f32[32,136,128]{2,1,0:T(8,128)S(1)} custom-call(s32[1040]{0:T(1024)S(1)} %get-tuple-element.13.list_ref, s32[8]{0:T(128)S(1)} %get-tuple-element.14.count_ref, s32[144,4,128]{2,1,0:T(4,128)S(1)} %bitcast.6, f32[16,8,128]{2,1,0:T(8,128)S(1)} %constant_dynamic-update-slice_fusion.own_sc, ...), custom_call_target="tpu_custom_call", output_to_operand_aliasing={{}: (10, {})} | custom-call | flops 8000000000 | tf_op jit(solution)/shard_map/pallas_call | solution.py:259
  45.3 2.4 %collective-permute-start.9 = (bf16[8,136,128]{2,1,0:T(8,128)(2,1)}, bf16[8,136,128]{2,1,0:T(8,128)(2,1)S(1)}, u32[]{:S(2)}, u32[]{:S(2)}) collective-permute-start(bf16[8,136,128]{2,1,0:T(8,128)(2,1)} %collective-permute-done.8.refs_3_), channel_id=1, source_target_pairs={{0,4},{2,6},{4,12},{6,14},{8,0},{10,2},{12,20},{14,22},{16,8},{18,... | collective-permute-start | bytes 835592 | tf_op jit(solution)/shard_map/ppermute | solution.py:344
  47.7 1.4 %collective-permute-start.16 = (bf16[8,136,128]{2,1,0:T(8,128)(2,1)}, bf16[8,136,128]{2,1,0:T(8,128)(2,1)S(1)}, u32[]{:S(2)}, u32[]{:S(2)}) collective-permute-start(bf16[8,136,128]{2,1,0:T(8,128)(2,1)} %collective-permute-done.15.refs_2_), channel_id=1, source_target_pairs={{0,4},{2,6},{4,12},{6,14},{8,0},{10,2},{12,20},{14,22},{16,8},{18,... | collective-permute-start | bytes 835592 | tf_op jit(solution)/shard_map/ppermute | solution.py:344
  49.2 3.6 %shard_map.97.refs_4_ = f32[32,136,128]{2,1,0:T(8,128)S(1)} custom-call(s32[1040]{0:T(1024)S(1)} %get-tuple-element.13.list_ref, s32[8]{0:T(128)S(1)} %get-tuple-element.14.count_ref, s32[144,4,128]{2,1,0:T(4,128)S(1)} %bitcast.7, f32[16,8,128]{2,1,0:T(8,128)S(1)} %constant_dynamic-update-slice_fusion.own_sc, ...), custom_call_target="tpu_custom_call", output_to_operand_aliasing={{}: (10, {})} | custom-call | flops 8000000000 | tf_op jit(solution)/shard_map/pallas_call | solution.py:259
  52.8 2.3 %collective-permute-start.10 = (bf16[8,136,128]{2,1,0:T(8,128)(2,1)S(1)}, bf16[8,136,128]{2,1,0:T(8,128)(2,1)S(1)}, u32[]{:S(2)}, u32[]{:S(2)}) collective-permute-start(bf16[8,136,128]{2,1,0:T(8,128)(2,1)S(1)} %collective-permute-done.9.refs_3_), channel_id=1, source_target_pairs={{0,4},{2,6},{4,12},{6,14},{8,0},{10,2},{12,20},{14,22},{16,8},{18,... | collective-permute-start | bytes 835592 | tf_op jit(solution)/shard_map/ppermute | solution.py:344
  55.1 5.2 %collective-permute-done.13.refs_1_ = bf16[8,136,128]{2,1,0:T(8,128)(2,1)S(1)} collective-permute-done((bf16[8,136,128]{2,1,0:T(8,128)(2,1)S(1)}, bf16[8,136,128]{2,1,0:T(8,128)(2,1)S(1)}, u32[]{:S(2)}, u32[]{:S(2)}) %collective-permute-start.13) | collective-permute-done | bytes 278560 | tf_op jit(solution)/shard_map/ppermute | solution.py:344
  60.3 3.9 %shard_map.98.refs_2_ = f32[32,136,128]{2,1,0:T(8,128)S(1)} custom-call(s32[1040]{0:T(1024)S(1)} %get-tuple-element.13.list_ref, s32[8]{0:T(128)S(1)} %get-tuple-element.14.count_ref, s32[144,4,128]{2,1,0:T(4,128)S(1)} %bitcast.8, f32[16,8,128]{2,1,0:T(8,128)S(1)} %constant_dynamic-update-slice_fusion.own_sc, ...), custom_call_target="tpu_custom_call", output_to_operand_aliasing={{}: (10, {})} | custom-call | flops 8000000000 | tf_op jit(solution)/shard_map/pallas_call | solution.py:259
  64.4 1.1 %collective-permute-done.6.refs_0_ = bf16[8,136,128]{2,1,0:T(8,128)(2,1)S(1)} collective-permute-done((bf16[8,136,128]{2,1,0:T(8,128)(2,1)S(1)}, bf16[8,136,128]{2,1,0:T(8,128)(2,1)S(1)}, u32[]{:S(2)}, u32[]{:S(2)}) %collective-permute-start.6) | collective-permute-done | bytes 278560 | tf_op jit(solution)/shard_map/ppermute | solution.py:344
  65.5 2.6 %shard_map.99 = (f32[32,136,128]{2,1,0:T(8,128)S(1)}, f32[16,136,128]{2,1,0:T(8,128)}) custom-call(s32[1040]{0:T(1024)S(1)} %get-tuple-element.13.list_ref, s32[8]{0:T(128)S(1)} %get-tuple-element.14.count_ref, s32[144,4,128]{2,1,0:T(4,128)S(1)} %bitcast.9, ...), custom_call_target="tpu_custom_call", output_to_operand_aliasing={{0}: (8, {})} | custom-call | flops 8000000000 | tf_op jit(solution)/shard_map/pallas_call | solution.py:259
  68.0 6.8 %collective-permute-start.17 = (f32[16,136,128]{2,1,0:T(8,128)}, f32[16,136,128]{2,1,0:T(8,128)S(1)}, u32[]{:S(2)}, u32[]{:S(2)}) collective-permute-start(f32[16,136,128]{2,1,0:T(8,128)} %get-tuple-element.20), channel_id=1, source_target_pairs={{0,2},{2,0},{4,6},{6,4},{8,10},{10,8},{12,14},{14,12},{16,18},{18,... | collective-permute-start | bytes 3342344 | tf_op jit(solution)/shard_map/ppermute | solution.py:389
  75.0 1.0 %copy-done.2 = s32[16,9,4,128]{3,2,1,0:T(4,128)S(1)} copy-done((s32[16,9,4,128]{3,2,1,0:T(4,128)S(1)}, s32[16,9,4,128]{3,2,1,0:T(4,128)}, u32[]{:S(2)}) %copy-start.2) | copy-done | bytes 294936
  75.9 1.0 %copy-done.13 = bf16[8,136,128]{2,1,0:T(8,128)(2,1)S(1)} copy-done((bf16[8,136,128]{2,1,0:T(8,128)(2,1)S(1)}, bf16[8,136,128]{2,1,0:T(8,128)(2,1)}, u32[]{:S(2)}) %copy-start.13) | copy-done | bytes 278552
  76.9 1.0 %copy-done.15 = bf16[8,136,128]{2,1,0:T(8,128)(2,1)S(1)} copy-done((bf16[8,136,128]{2,1,0:T(8,128)(2,1)S(1)}, bf16[8,136,128]{2,1,0:T(8,128)(2,1)}, u32[]{:S(2)}) %copy-start.15) | copy-done | bytes 278552
  77.8 0.8 %copy-done.17 = f32[16,8,128]{2,1,0:T(8,128)S(1)} copy-done((f32[16,8,128]{2,1,0:T(8,128)S(1)}, f32[16,8,128]{2,1,0:T(8,128)}, u32[]{:S(2)}) %copy-start.17) | copy-done | bytes 65560
  78.7 1.5 %shard_map.100.state_ref = f32[32,136,128]{2,1,0:T(8,128)S(1)} custom-call(s32[1040]{0:T(1024)S(1)} %get-tuple-element.13.list_ref, s32[8]{0:T(128)S(1)} %get-tuple-element.14.count_ref, s32[144,4,128]{2,1,0:T(4,128)S(1)} %bitcast.10, f32[16,8,128]{2,1,0:T(8,128)S(1)} %constant_dynamic-update-slice_fusion.own_sc, ...), custom_call_target="tpu_custom_call", output_to_operand_aliasing={{}: (8, {})} | custom-call | flops 8000000000 | tf_op jit(solution)/shard_map/pallas_call | solution.py:259
  80.2 1.4 %shard_map.101 = bf16[128,2048]{1,0:T(8,128)(2,1)} custom-call(f32[32,136,128]{2,1,0:T(8,128)S(1)} %shard_map.100.state_ref, f32[16,136,128]{2,1,0:T(8,128)S(1)} %collective-permute-done.17.other_ref, bf16[128,2048]{1,0:T(8,128)(2,1)S(1)} %copy-done, f32[128,1]{1,0:T(8,128)S(1)} %copy.22.bias_ref), custom_call_target="tpu_custom_call" | custom-call | flops 1000000 | tf_op jit(solution)/shard_map/pallas_call | solution.py:259
  (64 shorter events, 5.8 us)
Async XLA Ops:
  0.0 15.3 %copy-start.3 = (bf16[128,256]{1,0:T(8,128)(2,1)S(1)}, bf16[128,256]{1,0:T(8,128)(2,1)}, u32[]{:S(2)}) copy-start(bf16[128,256]{1,0:T(8,128)(2,1)} %w_ref.3) | copy-start | bytes 196612
  1.1 14.2 %collective-permute-start.1 = (bf16[128,1024]{1,0:T(8,128)(2,1)S(1)}, bf16[128,1024]{1,0:T(8,128)(2,1)S(1)}, u32[]{:S(2)}, u32[]{:S(2)}) collective-permute-start(bf16[128,1024]{1,0:T(8,128)(2,1)S(1)} %get-tuple-element.21.refs_0_), channel_id=1, source_target_pairs={{0,1},{1,0},{2,3},{3,2},{4,5},{5,4},{6,7},{7,6},{8,9},{9,8},{10,11... | collective-permute-start | bytes 786440 | tf_op jit(solution)/shard_map/ppermute | solution.py:309
  2.4 14.9 %collective-permute-start = (bf16[128,1024]{1,0:T(8,128)(2,1)S(1)}, bf16[128,1024]{1,0:T(8,128)(2,1)S(1)}, u32[]{:S(2)}, u32[]{:S(2)}) collective-permute-start(bf16[128,1024]{1,0:T(8,128)(2,1)S(1)} %get-tuple-element.22.refs_0_), channel_id=1, source_target_pairs={{0,1},{1,0},{2,3},{3,2},{4,5},{5,4},{6,7},{7,6},{8,9},{9,8},{10,11... | collective-permute-start | bytes 786440 | tf_op jit(solution)/shard_map/ppermute | solution.py:309
  7.4 28.1 %all-to-all-start = ((s32[16,9,4,128]{3,2,1,0:T(4,128)}), s32[16,9,4,128]{3,2,1,0:T(4,128)S(1)}, u32[]{:S(2)}, u32[]{:S(2)}) async-start(s32[16,9,4,128]{3,2,1,0:T(4,128)} %shard_map.91), calls=%async_computation | async-start | bytes 589824 | tf_op jit(solution)/shard_map/all_to_all | solution.py:322
  15.8 19.7 %copy-start.8 = (bf16[8,136,128]{2,1,0:T(8,128)(2,1)}, bf16[8,136,128]{2,1,0:T(8,128)(2,1)S(1)}, u32[]{:S(2)}) copy-start(bf16[8,136,128]{2,1,0:T(8,128)(2,1)S(1)} %get-tuple-element.18.refs_1_) | copy-start | bytes 835588
  15.8 13.1 %collective-permute-start.11 = (bf16[8,136,128]{2,1,0:T(8,128)(2,1)S(1)}, bf16[8,136,128]{2,1,0:T(8,128)(2,1)}, u32[]{:S(2)}, u32[]{:S(2)}) collective-permute-start(bf16[8,136,128]{2,1,0:T(8,128)(2,1)S(1)} %get-tuple-element.18.refs_1_), channel_id=1, source_target_pairs={{0,8},{2,10},{4,0},{6,2},{8,16},{10,18},{12,4},{14,6},{16,24},{18,... | collective-permute-start | bytes 835592 | tf_op jit(solution)/shard_map/ppermute | solution.py:344
  16.1 12.8 %collective-permute-start.7 = (bf16[8,136,128]{2,1,0:T(8,128)(2,1)S(1)}, bf16[8,136,128]{2,1,0:T(8,128)(2,1)}, u32[]{:S(2)}, u32[]{:S(2)}) collective-permute-start(bf16[8,136,128]{2,1,0:T(8,128)(2,1)S(1)} %get-tuple-element.18.refs_1_), channel_id=1, source_target_pairs={{0,4},{2,6},{4,12},{6,14},{8,0},{10,2},{12,20},{14,22},{16,8},{18,... | collective-permute-start | bytes 835592 | tf_op jit(solution)/shard_map/ppermute | solution.py:344
  17.8 15.4 %collective-permute-start.14 = (bf16[8,136,128]{2,1,0:T(8,128)(2,1)S(1)}, bf16[8,136,128]{2,1,0:T(8,128)(2,1)S(1)}, u32[]{:S(2)}, u32[]{:S(2)}) collective-permute-start(bf16[8,136,128]{2,1,0:T(8,128)(2,1)S(1)} %get-tuple-element.17.refs_0_), channel_id=1, source_target_pairs={{0,4},{2,6},{4,12},{6,14},{8,0},{10,2},{12,20},{14,22},{16,8},{18,... | collective-permute-start | bytes 835592 | tf_op jit(solution)/shard_map/ppermute | solution.py:344
  19.0 16.4 %collective-permute-start.3 = (bf16[8,136,128]{2,1,0:T(8,128)(2,1)S(1)}, bf16[8,136,128]{2,1,0:T(8,128)(2,1)}, u32[]{:S(2)}, u32[]{:S(2)}) collective-permute-start(bf16[8,136,128]{2,1,0:T(8,128)(2,1)S(1)} %get-tuple-element.17.refs_0_), channel_id=1, source_target_pairs={{0,8},{2,10},{4,0},{6,2},{8,16},{10,18},{12,4},{14,6},{16,24},{18,... | collective-permute-start | bytes 835592 | tf_op jit(solution)/shard_map/ppermute | solution.py:344
  20.0 17.2 %collective-permute-start.2 = (f32[16,8,128]{2,1,0:T(8,128)S(1)}, f32[16,8,128]{2,1,0:T(8,128)S(1)}, u32[]{:S(2)}, u32[]{:S(2)}) collective-permute-start(f32[16,8,128]{2,1,0:T(8,128)S(1)} %constant_dynamic-update-slice_fusion.own_sc), channel_id=1, source_target_pairs={{0,2},{2,0},{4,6},{6,4},{8,10},{10,8},{12,14},{14,12},{16,18},{18,... | collective-permute-start | bytes 196616 | tf_op jit(solution)/shard_map/ppermute | solution.py:336
  28.9 18.7 %collective-permute-start.12 = (bf16[8,136,128]{2,1,0:T(8,128)(2,1)}, bf16[8,136,128]{2,1,0:T(8,128)(2,1)S(1)}, u32[]{:S(2)}, u32[]{:S(2)}) collective-permute-start(bf16[8,136,128]{2,1,0:T(8,128)(2,1)} %collective-permute-done.11.refs_1_), channel_id=1, source_target_pairs={{0,8},{2,10},{4,0},{6,2},{8,16},{10,18},{12,4},{14,6},{16,24},{18,... | collective-permute-start | bytes 835592 | tf_op jit(solution)/shard_map/ppermute | solution.py:344
  28.9 16.3 %collective-permute-start.8 = (bf16[8,136,128]{2,1,0:T(8,128)(2,1)}, bf16[8,136,128]{2,1,0:T(8,128)(2,1)}, u32[]{:S(2)}, u32[]{:S(2)}) collective-permute-start(bf16[8,136,128]{2,1,0:T(8,128)(2,1)} %collective-permute-done.7.refs_3_), channel_id=1, source_target_pairs={{0,4},{2,6},{4,12},{6,14},{8,0},{10,2},{12,20},{14,22},{16,8},{18,... | collective-permute-start | bytes 835592 | tf_op jit(solution)/shard_map/ppermute | solution.py:344
  33.2 14.5 %collective-permute-start.15 = (bf16[8,136,128]{2,1,0:T(8,128)(2,1)S(1)}, bf16[8,136,128]{2,1,0:T(8,128)(2,1)}, u32[]{:S(2)}, u32[]{:S(2)}) collective-permute-start(bf16[8,136,128]{2,1,0:T(8,128)(2,1)S(1)} %collective-permute-done.14.refs_2_), channel_id=1, source_target_pairs={{0,4},{2,6},{4,12},{6,14},{8,0},{10,2},{12,20},{14,22},{16,8},{18,... | collective-permute-start | bytes 835592 | tf_op jit(solution)/shard_map/ppermute | solution.py:344
  35.5 12.2 %collective-permute-start.4 = (bf16[8,136,128]{2,1,0:T(8,128)(2,1)}, bf16[8,136,128]{2,1,0:T(8,128)(2,1)}, u32[]{:S(2)}, u32[]{:S(2)}) collective-permute-start(bf16[8,136,128]{2,1,0:T(8,128)(2,1)} %collective-permute-done.3.refs_0_), channel_id=1, source_target_pairs={{0,8},{2,10},{4,0},{6,2},{8,16},{10,18},{12,4},{14,6},{16,24},{18,... | collective-permute-start | bytes 835592 | tf_op jit(solution)/shard_map/ppermute | solution.py:344
  35.5 30.0 %copy-start.1 = (s32[16,9,4,128]{3,2,1,0:T(4,128)}, s32[16,9,4,128]{3,2,1,0:T(4,128)S(1)}, u32[]{:S(2)}) copy-start(s32[16,9,4,128]{3,2,1,0:T(4,128)S(1)} %all-to-all-done) | copy-start | bytes 884740
  37.2 28.2 %copy-start.16 = (f32[16,8,128]{2,1,0:T(8,128)}, f32[16,8,128]{2,1,0:T(8,128)S(1)}, u32[]{:S(2)}) copy-start(f32[16,8,128]{2,1,0:T(8,128)S(1)} %collective-permute-done.2.other_sc) | copy-start | bytes 196612
  37.2 1.0 %copy-start.9 = (bf16[8,136,128]{2,1,0:T(8,128)(2,1)S(1)}, bf16[8,136,128]{2,1,0:T(8,128)(2,1)}, u32[]{:S(2)}) copy-start(bf16[8,136,128]{2,1,0:T(8,128)(2,1)} %copy-done.8) | copy-start | bytes 835588
  38.2 1.0 %copy-start.11 = (bf16[8,136,128]{2,1,0:T(8,128)(2,1)S(1)}, bf16[8,136,128]{2,1,0:T(8,128)(2,1)}, u32[]{:S(2)}) copy-start(bf16[8,136,128]{2,1,0:T(8,128)(2,1)} %copy-done.10) | copy-start | bytes 835588
  45.3 7.5 %collective-permute-start.9 = (bf16[8,136,128]{2,1,0:T(8,128)(2,1)}, bf16[8,136,128]{2,1,0:T(8,128)(2,1)S(1)}, u32[]{:S(2)}, u32[]{:S(2)}) collective-permute-start(bf16[8,136,128]{2,1,0:T(8,128)(2,1)} %collective-permute-done.8.refs_3_), channel_id=1, source_target_pairs={{0,4},{2,6},{4,12},{6,14},{8,0},{10,2},{12,20},{14,22},{16,8},{18,... | collective-permute-start | bytes 835592 | tf_op jit(solution)/shard_map/ppermute | solution.py:344
  47.6 7.5 %collective-permute-start.5 = (bf16[8,136,128]{2,1,0:T(8,128)(2,1)}, bf16[8,136,128]{2,1,0:T(8,128)(2,1)S(1)}, u32[]{:S(2)}, u32[]{:S(2)}) collective-permute-start(bf16[8,136,128]{2,1,0:T(8,128)(2,1)} %collective-permute-done.4.refs_0_), channel_id=1, source_target_pairs={{0,8},{2,10},{4,0},{6,2},{8,16},{10,18},{12,4},{14,6},{16,24},{18,... | collective-permute-start | bytes 835592 | tf_op jit(solution)/shard_map/ppermute | solution.py:344
  47.6 12.7 %collective-permute-start.13 = (bf16[8,136,128]{2,1,0:T(8,128)(2,1)S(1)}, bf16[8,136,128]{2,1,0:T(8,128)(2,1)S(1)}, u32[]{:S(2)}, u32[]{:S(2)}) collective-permute-start(bf16[8,136,128]{2,1,0:T(8,128)(2,1)S(1)} %collective-permute-done.12.refs_1_), channel_id=1, source_target_pairs={{0,8},{2,10},{4,0},{6,2},{8,16},{10,18},{12,4},{14,6},{16,24},{18,... | collective-permute-start | bytes 835592 | tf_op jit(solution)/shard_map/ppermute | solution.py:344
  47.7 12.6 %collective-permute-start.16 = (bf16[8,136,128]{2,1,0:T(8,128)(2,1)}, bf16[8,136,128]{2,1,0:T(8,128)(2,1)S(1)}, u32[]{:S(2)}, u32[]{:S(2)}) collective-permute-start(bf16[8,136,128]{2,1,0:T(8,128)(2,1)} %collective-permute-done.15.refs_2_), channel_id=1, source_target_pairs={{0,4},{2,6},{4,12},{6,14},{8,0},{10,2},{12,20},{14,22},{16,8},{18,... | collective-permute-start | bytes 835592 | tf_op jit(solution)/shard_map/ppermute | solution.py:344
  52.8 11.5 %collective-permute-start.10 = (bf16[8,136,128]{2,1,0:T(8,128)(2,1)S(1)}, bf16[8,136,128]{2,1,0:T(8,128)(2,1)S(1)}, u32[]{:S(2)}, u32[]{:S(2)}) collective-permute-start(bf16[8,136,128]{2,1,0:T(8,128)(2,1)S(1)} %collective-permute-done.9.refs_3_), channel_id=1, source_target_pairs={{0,4},{2,6},{4,12},{6,14},{8,0},{10,2},{12,20},{14,22},{16,8},{18,... | collective-permute-start | bytes 835592 | tf_op jit(solution)/shard_map/ppermute | solution.py:344
  55.1 10.4 %collective-permute-start.6 = (bf16[8,136,128]{2,1,0:T(8,128)(2,1)S(1)}, bf16[8,136,128]{2,1,0:T(8,128)(2,1)S(1)}, u32[]{:S(2)}, u32[]{:S(2)}) collective-permute-start(bf16[8,136,128]{2,1,0:T(8,128)(2,1)S(1)} %collective-permute-done.5.refs_0_), channel_id=1, source_target_pairs={{0,8},{2,10},{4,0},{6,2},{8,16},{10,18},{12,4},{14,6},{16,24},{18,... | collective-permute-start | bytes 835592 | tf_op jit(solution)/shard_map/ppermute | solution.py:344
  64.2 10.6 %copy-start.18 = (f32[128]{0:T(128)S(1)}, f32[128]{0:T(128)}, u32[]{:S(2)}) copy-start(f32[128]{0:T(128)} %param.13) | copy-start | bytes 1540
  64.4 3.7 %copy-start.12 = (bf16[8,136,128]{2,1,0:T(8,128)(2,1)}, bf16[8,136,128]{2,1,0:T(8,128)(2,1)S(1)}, u32[]{:S(2)}) copy-start(bf16[8,136,128]{2,1,0:T(8,128)(2,1)S(1)} %collective-permute-done.10.refs_1_) | copy-start | bytes 835588
  65.5 2.6 %copy-start.14 = (bf16[8,136,128]{2,1,0:T(8,128)(2,1)}, bf16[8,136,128]{2,1,0:T(8,128)(2,1)S(1)}, u32[]{:S(2)}) copy-start(bf16[8,136,128]{2,1,0:T(8,128)(2,1)S(1)} %collective-permute-done.6.refs_0_) | copy-start | bytes 835588
  68.0 12.1 %collective-permute-start.17 = (f32[16,136,128]{2,1,0:T(8,128)}, f32[16,136,128]{2,1,0:T(8,128)S(1)}, u32[]{:S(2)}, u32[]{:S(2)}) collective-permute-start(f32[16,136,128]{2,1,0:T(8,128)} %get-tuple-element.20), channel_id=1, source_target_pairs={{0,2},{2,0},{4,6},{6,4},{8,10},{10,8},{12,14},{14,12},{16,18},{18,... | collective-permute-start | bytes 3342344 | tf_op jit(solution)/shard_map/ppermute | solution.py:389
  75.0 1.0 %copy-start.2 = (s32[16,9,4,128]{3,2,1,0:T(4,128)S(1)}, s32[16,9,4,128]{3,2,1,0:T(4,128)}, u32[]{:S(2)}) copy-start(s32[16,9,4,128]{3,2,1,0:T(4,128)} %copy-done.1) | copy-start | bytes 884740
  75.9 1.0 %copy-start.13 = (bf16[8,136,128]{2,1,0:T(8,128)(2,1)S(1)}, bf16[8,136,128]{2,1,0:T(8,128)(2,1)}, u32[]{:S(2)}) copy-start(bf16[8,136,128]{2,1,0:T(8,128)(2,1)} %copy-done.12) | copy-start | bytes 835588
  76.9 1.0 %copy-start.15 = (bf16[8,136,128]{2,1,0:T(8,128)(2,1)S(1)}, bf16[8,136,128]{2,1,0:T(8,128)(2,1)}, u32[]{:S(2)}) copy-start(bf16[8,136,128]{2,1,0:T(8,128)(2,1)} %copy-done.14) | copy-start | bytes 835588
  78.7 1.5 %copy-start = (bf16[128,2048]{1,0:T(8,128)(2,1)S(1)}, bf16[128,2048]{1,0:T(8,128)(2,1)}, u32[]{:S(2)}) copy-start(bf16[128,2048]{1,0:T(8,128)(2,1)} %x_ref.1) | copy-start | bytes 1572868
  (6 other events, 4.4 us)
where the time goes:
time: 82.2 us; the launch traced here: 81.5 us
  starting transfers between devices  29.9 us (36%)
  Pallas kernels  23.5 us (29%)
  waiting for transfers between devices  16.6 us (20%)
  local copies, waits for them, and re-layouts  10.6 us (13%)
    pallas_call x11, Pallas kernels, call(): pl.pallas_call(kernel, out_shape=outs, in_specs=in_specs or [VMEM] * len(...  23.5 us
    ppermute x14, waiting for transfers between devices, local(): going[way] = lax.ppermute(going[way], 'dp', pairs)  16.5 us
    ppermute x14, starting transfers between devices, local(): going[way] = lax.ppermute(going[way], 'dp', pairs)  13 us
    unnamed x39, local copies, waits for them, and re-layouts  9.19 us
    all_to_all x1, starting transfers between devices, local(): got = lax.all_to_all(packed, 'dp', split_axis=0, concat_axis=0, tiled=True)  7.08 us
    ppermute x1, starting transfers between devices, local(): back = lax.ppermute(other, 'dp', swap)  6.8 us
  transfers between devices with their start and end apart: 19, of which 5 were waited for; matrix products, arithmetic and copies ran while one was open for 1% of the time, Pallas kernels for 24%

commit v1 on v0

v1 whole, which is shorter than its diff:
```python
import functools

import jax
import jax.numpy as jnp
from jax import lax
from jax.experimental import pallas as pl
from jax.experimental.pallas import tpu as pltpu
from jax.sharding import PartitionSpec as P


HD = 32
LOG2E = 1.4426950408889634
FAR = -1e30
F32 = jnp.float32
BF16 = jnp.bfloat16


WIDE = 1
LIMIT = 16 * 1024 * 1024

VMEM = pl.BlockSpec(memory_space=pltpu.VMEM)
SMEM = pl.BlockSpec(memory_space=pltpu.SMEM)


def split(value, size):
    if size & (size - 1) == 0:
        return value >> (size.bit_length() - 1), value & (size - 1)
    return lax.div(value, jnp.int32(size)), lax.rem(value, jnp.int32(size))


def pad8(count):
    return -(-count // 8) * 8


def leaky(scores):
    return jnp.maximum(scores, 0.2 * scores)


def head_sums(rows):
    return jnp.sum(rows.reshape(rows.shape[0] // HD, HD, rows.shape[1]), axis=1)


def stack_rows(pieces, total):
    have = sum(p.shape[0] for p in pieces)
    if have < total:
        pieces = pieces + [jnp.zeros((total - have, pieces[0].shape[1]), F32)]
    return jnp.concatenate(pieces, axis=0)


def ring_order(chips):
    columns = max(1, chips // 4)
    rows = chips // columns
    if columns == 1:
        return list(range(chips))
    order = [row * columns for row in range(rows)]
    for row in reversed(range(rows)):
        inner = list(range(1, columns))
        order += [row * columns + col for col in (inner if (rows - 1 - row) % 2 == 0 else inner[::-1])]
    return order


def column(row_ref):
    return jnp.transpose(jnp.broadcast_to(row_ref[...], (8, row_ref.shape[1])))[:, 0:1]


def project_kernel(parts, base, mp_ref, w_ref, src_ref, dst_ref, *refs):
    x_refs, (pay_ref, sc_ref) = refs[:parts], refs[-2:]
    me = mp_ref[0]
    depth = w_ref.shape[1] // parts
    total = None
    for k in range(parts):
        at = pl.multiple_of((me ^ k) * depth, depth) if parts > 1 else 0
        term = jnp.dot(w_ref[:, pl.ds(at, depth)], x_refs[k][...], preferred_element_type=F32)
        total = term if total is None else total + term
    rounded = total.astype(BF16)
    a_src, a_dst = column(src_ref) * LOG2E, column(dst_ref) * LOG2E
    source = head_sums(total * a_src)
    target = head_sums(total * a_dst)
    rest = source - head_sums(rounded.astype(F32) * a_src)
    rest_hi = rest.astype(BF16).astype(F32)
    extra = stack_rows([rest_hi, rest - rest_hi], pay_ref.shape[1] - rounded.shape[0]).astype(BF16)
    scores = stack_rows([target, leaky(source + target)], sc_ref.shape[1])
    dims, tile = rounded.shape[0], pay_ref.shape[2]
    for b in range(pay_ref.shape[0]):
        at = slice(b * tile, (b + 1) * tile)
        pay_ref[b, :dims, :] = rounded[:, at]
        pay_ref[b, dims:, :] = extra[:, at]
        sc_ref[base + b] = scores[:, at]


def open_kernel(halves, *refs):
    count = (len(refs) - halves) // 2
    sources, outs, sems = refs[:count], refs[count:-1], refs[-1]
    size = outs[0].shape[1]
    sources = [sources[0].at[:, k * size : (k + 1) * size] for k in range(halves)] + list(sources[1:])
    copies = [pltpu.make_async_copy(v, w, sems.at[k]) for k, (v, w) in enumerate(zip(sources, outs))]
    for copy in copies:
        copy.start()
    for copy in copies:
        copy.wait()


def pack_kernel(blocks, place, groups, rows_in, cols_in, masks_in, out_ref, rows_ref, cols_ref, masks_ref, count, place_ref, sems):
    ins, tos = (rows_in, cols_in, masks_in), (rows_ref, cols_ref, masks_ref)
    copies = [pltpu.make_async_copy(v, w, sems.at[k]) for k, (v, w) in enumerate(zip(ins, tos))]
    for copy in copies:
        copy.start()
    devices, slots = out_ref.shape[0], out_ref.shape[1] - 1
    words = out_ref.shape[2:]
    half = blocks // 2
    chips = len(place)
    lane = lax.broadcasted_iota(jnp.int32, words, 1)
    for c in range(chips):
        place_ref[c] = place[c]
    for d in range(devices):
        count[d] = 0
        out_ref[d, slots] = jnp.zeros(words, jnp.int32)
    for copy in copies:
        copy.wait()

    def body(t, carry):
        row, col = rows_ref[t], cols_ref[t]
        owner, row_at = split(row, blocks)
        holder, col_at = split(col, blocks)
        at = count[owner]
        count[owner] = at + 1
        out_ref[owner, at] = masks_ref[t]
        back = place_ref[owner >> 1] - place_ref[holder >> 1]
        back = jnp.where(back < 0, back + chips, back)
        step = jnp.minimum(back, chips - back)
        part, j = split(col_at, half)
        last = 2 * back == chips
        spot = col_at + jnp.where(back > step, blocks, 0) + jnp.where(step == 1, blocks, 0)
        before = step == chips // 2 - 1
        spot = jnp.where(before, j + jnp.where(back > step, half, 0), jnp.where(last, j, spot))
        group = jnp.where(step > 0, step - 1, 0) + jnp.where(before | last, part, 0) + jnp.where(last, 1, 0)
        code = ((row_at * (4 * blocks) + spot) * 2 + (holder & 1)) * groups + group
        here = out_ref[owner, slots]
        here = jnp.where(lane == at, code, jnp.where(lane == slots, at + 1, here))
        out_ref[owner, slots] = here
        return carry

    lax.fori_loop(0, rows_ref.shape[0], body, 0)


def list_kernel(devices, slots, groups, blocks, final, core_ref, own_ids, other_ids, own_masks, other_masks, list_ref, count_ref, masks_ref):
    total = list_ref.shape[0] // groups
    width = devices * (slots + 1)
    core = core_ref[0]
    for g in range(groups):
        count_ref[g] = 0
    for side, (ids, masks) in enumerate(((own_ids, own_masks), (other_ids, other_masks))):
        masks_ref[side * width : (side + 1) * width] = masks[...]
        for d in range(devices):
            base = d * (slots + 1)

            def body(n, carry, side=side, ids=ids, base=base):
                code, group = split(ids[base + n], groups)

                @pl.when((code & 1) == core)
                def _():
                    code_here = (code >> 1) + side * (4 * blocks * blocks)
                    to = group if side else group + jnp.where(group == final, 1, 0)
                    at = count_ref[to]
                    list_ref[to * total + at] = (code_here * (2 * width) + side * width + base + n) * 2 + 1
                    count_ref[to] = at + 1

                return carry

            lax.fori_loop(0, ids[base + slots], body, 0)
    for g in range(groups):
        at = count_ref[g]
        for k in range(3 * WIDE):
            list_ref[g * total + at + k] = 0
        count_ref[g] = lax.div(at + 2 * WIDE - 1, 2 * WIDE)


def prepare(entry, fields, heads, dims, masks_ref, att, buf, edges, tops):
    _, spot, slot = fields
    tile = masks_ref.shape[2]
    up = 31 - lax.broadcasted_iota(jnp.int32, (32, tile), 0)
    packed = masks_ref[slot] & -(entry & 1)
    block = [
        jnp.where((jnp.broadcast_to(packed[w : w + 1], (32, tile)) << up) < 0, 0.0, FAR)
        for w in range(packed.shape[0])
    ]
    block = jnp.concatenate(block, axis=0)
    feats = buf[spot, :dims, :]
    extra = buf[spot, dims:, :].astype(F32)
    source = head_sums(feats.astype(F32) * att) + extra[:heads] + extra[heads : 2 * heads]
    columns = jnp.transpose(stack_rows([source], pad8(heads)))
    for h in range(heads):
        edge = jnp.broadcast_to(columns[:, h : h + 1], (tile, tile)) + block
        edges[h] = edge
        tops[h : h + 1, :] = jnp.max(edge, axis=0, keepdims=True)


def absorb(fields, heads, dims, tscore, buf, edges, tops, state):
    row, spot, _ = fields
    tile = state.shape[2]
    ones = jnp.ones((16, tile), BF16)
    target = tscore[row, :heads, :]
    old = state[row, dims : dims + heads, :]
    new = jnp.maximum(old, leaky(target + tops[:heads, :]))
    state[row, dims : dims + heads, :] = new
    alpha, up1, up2 = jnp.exp2(old - new), target - new, 0.2 * target - new
    values = []
    for h in range(heads):
        edge = edges[h]
        raw = jnp.maximum(edge + up1[h : h + 1], 0.2 * edge + up2[h : h + 1])
        weight = jnp.exp2(raw).astype(BF16)
        left = jnp.concatenate([buf[spot, h * HD : (h + 1) * HD, :], ones], axis=0)
        values.append(jnp.dot(left, weight, preferred_element_type=F32))
    at = slice(dims + heads, dims + 2 * heads)
    mass = jnp.concatenate([v[HD : HD + 1] for v in values], axis=0)
    state[row, at, :] = state[row, at, :] * alpha + mass
    for h in range(heads):
        at = slice(h * HD, (h + 1) * HD)
        state[row, at, :] = state[row, at, :] * alpha[h : h + 1] + values[h][:HD]


def stage_kernel(group, groups, first, count, list_ref, count_ref, masks_ref, own_sc, other_sc, src_ref, *refs):
    pays, (tscore, buf, edges0, edges1, tops0, tops1) = refs[:count], refs[-6:]
    outs = refs[count if first else count + 1 : -6]
    state = outs[0]
    total = list_ref.shape[0] // groups
    blocks, dims = own_sc.shape[0], src_ref.shape[1]
    heads = dims // HD
    base = 0
    for pay in pays:
        buf[base : base + pay.shape[0]] = pay[...]
        base += pay.shape[0]
    tscore[:blocks] = own_sc[...]
    tscore[blocks:] = other_sc[...]
    if first:
        tile = state.shape[2]
        rest = state.shape[1] - dims - 2 * heads
        for b in range(blocks):
            state[b, :dims] = buf[b, :dims].astype(F32)
            state[b, dims : dims + heads] = own_sc[b, heads : 2 * heads]
            state[b, dims + heads : dims + 2 * heads] = jnp.ones((heads, tile), F32)
            state[blocks + b, :dims] = jnp.zeros((dims, tile), F32)
            state[blocks + b, dims : dims + heads] = jnp.full((heads, tile), 0.1 * FAR, F32)
            state[blocks + b, dims + heads :] = jnp.zeros((heads + rest, tile), F32)
            if rest:
                state[b, dims + 2 * heads :] = jnp.zeros((rest, tile), F32)
    att = column(src_ref) * LOG2E
    spaces = ((edges0, tops0), (edges1, tops1))

    def fields(entry):
        code, slot = split(entry >> 1, masks_ref.shape[0])
        row, spot = split(code, 4 * blocks)
        return row, spot, slot

    def ready(n, side):
        for k in range(WIDE):
            entry = list_ref[group * total + n * WIDE + k]
            space = [v.at[k] for v in spaces[side]]
            prepare(entry, fields(entry), heads, dims, masks_ref, att, buf, *space)

    def take(n, side):
        for k in range(WIDE):
            entry = list_ref[group * total + n * WIDE + k]
            space = [v.at[k] for v in spaces[side]]
            absorb(fields(entry), heads, dims, tscore, buf, *space, state)

    def body(i, carry):
        ready(2 * i + 1, 1)
        take(2 * i, 0)
        ready(2 * i + 2, 0)
        take(2 * i + 1, 1)
        return carry

    ready(0, 0)
    lax.fori_loop(0, count_ref[group], body, 0)
    if len(outs) > 1:
        outs[1][...] = state[blocks:]


def merge_kernel(state_ref, other_ref, x_ref, bias_ref, out_ref):
    blocks, dims, tile = other_ref.shape[0], x_ref.shape[0], other_ref.shape[2]
    heads = dims // HD
    bias = column(bias_ref)
    for b in range(blocks):
        m1, m2 = state_ref[b, dims : dims + heads], other_ref[b, dims : dims + heads]
        l1 = state_ref[b, dims + heads : dims + 2 * heads]
        l2 = other_ref[b, dims + heads : dims + 2 * heads]
        best = jnp.maximum(m1, m2)
        c1, c2 = jnp.exp2(m1 - best), jnp.exp2(m2 - best)
        scale = 1.0 / (l1 * c1 + l2 * c2)
        c1, c2 = (c1 * scale)[:, None, :], (c2 * scale)[:, None, :]
        mixed = state_ref[b, :dims].reshape(heads, HD, tile) * c1
        mixed = mixed + other_ref[b, :dims].reshape(heads, HD, tile) * c2
        at = slice(b * tile, (b + 1) * tile)
        v = mixed.reshape(dims, tile) + x_ref[:, at].astype(F32) + bias
        out_ref[:, at] = jnp.where(v > 0, v, jnp.exp(jnp.minimum(v, 0.0)) - 1.0).astype(BF16)


def call(kernel, outs, args, in_specs=None, out_specs=VMEM, scratch=(), aliases=None, flops=1000000):
    return pl.pallas_call(
        kernel,
        out_shape=outs,
        in_specs=in_specs or [VMEM] * len(args),
        out_specs=out_specs,
        scratch_shapes=list(scratch),
        input_output_aliases=aliases or {},
        compiler_params=pltpu.CompilerParams(vmem_limit_bytes=LIMIT),
        cost_estimate=pl.CostEstimate(flops=flops, bytes_accessed=0, transcendentals=0),
    )(*args)


def near(x):
    return pltpu.with_memory_space_constraint(x, pltpu.VMEM)


def far(x):
    return pltpu.with_memory_space_constraint(x, pltpu.HBM)


def local(node_feats, proj_weight, att_src, att_dst, out_bias, tile_rows, tile_cols, tile_masks):
    nodes = node_feats.shape[1]
    dims = proj_weight.shape[0]
    heads = dims // HD
    words, tile = tile_masks.shape[1:]
    blocks = nodes // tile
    tiles = tile_rows.shape[0]
    n_dp, n_mp = lax.axis_size("dp"), lax.axis_size("mp")
    chips = n_dp // 2
    slots = max(2, 2 * tiles // n_dp)
    half = blocks // 2
    extra = pad8(2 * heads)
    order = ring_order(chips)
    place = [order.index(c) for c in range(chips)]
    me_mp = lax.axis_index("mp")
    steps = chips // 2
    groups = 8
    while groups < steps + 3:
        groups *= 2

    def hop(step):
        pairs = []
        for p, c in enumerate(order):
            to = order[(p + step) % chips]
            pairs += [(2 * c, 2 * to), (2 * c + 1, 2 * to + 1)]
        return sorted(pairs)

    right, left = hop(1), hop(-1)
    swap = [(i, i ^ 1) for i in range(n_dp)]

    mine = jnp.full((1,), me_mp, jnp.int32)
    core = jnp.full((1,), lax.axis_index("dp") & 1, jnp.int32)
    parts = 2 if n_mp == 2 else 1
    moved = [node_feats, proj_weight, att_src.reshape(1, dims), att_dst.reshape(1, dims)]
    shapes = [(node_feats.shape[0], nodes // parts)] * parts + [v.shape for v in moved[1:]]
    kinds = [BF16] * (parts + 1) + [F32] * 2
    anywhere = pl.BlockSpec(memory_space=pl.ANY)
    *cuts, weight, a_src, a_dst = call(
        functools.partial(open_kernel, parts),
        [pltpu.VMEM(v, k) for v, k in zip(shapes, kinds)],
        [far(v) for v in moved],
        in_specs=[anywhere] * len(moved),
        out_specs=[VMEM] * len(shapes),
        scratch=[pltpu.SemaphoreType.DMA((len(shapes),))],
    )
    if n_mp == 2:
        flip = [(0, 1), (1, 0)]
        inputs = [[x, lax.ppermute(x, "mp", flip)] for x in cuts]
    else:
        whole = lax.all_gather(node_feats, "mp", axis=0, tiled=True)
        inputs = [[whole[:, k * (nodes // 2) : (k + 1) * (nodes // 2)]] for k in range(2)]
    att = (a_src, a_dst)

    packed = call(
        functools.partial(pack_kernel, blocks, place, groups),
        pltpu.HBM((n_dp, slots + 1, words, tile), jnp.int32),
        [far(v) for v in (tile_rows, tile_cols, tile_masks)],
        in_specs=[anywhere] * 3,
        scratch=[
            pltpu.SMEM(tile_rows.shape, jnp.int32),
            pltpu.SMEM(tile_cols.shape, jnp.int32),
            pltpu.VMEM(tile_masks.shape, jnp.int32),
            pltpu.SMEM((n_dp,), jnp.int32),
            pltpu.SMEM((chips,), jnp.int32),
            pltpu.SemaphoreType.DMA((3,)),
        ],
    )
    got = lax.all_to_all(packed, "dp", split_axis=0, concat_axis=0, tiled=True)
    got = got.reshape(n_dp * (slots + 1), words, tile)
    got_other = lax.ppermute(got, "dp", swap)

    pays, own_sc = [], None
    for k, xs in enumerate(inputs):
        args = [mine] + [near(v) for v in (weight, *att, *xs)]
        if own_sc is not None:
            args.append(near(own_sc))
        pay, own_sc = call(
            functools.partial(project_kernel, len(xs), k * half),
            (
                pltpu.VMEM((half, dims + extra, tile), BF16),
                pltpu.VMEM((blocks, extra, tile), F32),
            ),
            args,
            in_specs=[SMEM] + [VMEM] * (len(args) - 1),
            out_specs=(VMEM, VMEM),
            aliases={len(args) - 1: 1} if k else None,
        )
        pays.append(pay)
    other_sc = lax.ppermute(own_sc, "dp", swap)

    arrivals = []
    going = {w + p: pays["AB".index(p)] for w in "rl" for p in "AB"}
    for k in range(1, steps):
        for way in ("rA", "lA", "rB", "lB"):
            going[way] = lax.ppermute(going[way], "dp", right if way[0] == "r" else left)
        if k < steps - 1:
            arrivals.append([going[w] for w in ("rA", "rB", "lA", "lB")])
        else:
            arrivals += [[going[w] for w in ways] for ways in (("rA", "lA"), ("rB", "lB"))]
    arrivals[0] = pays + arrivals[0]
    for p in "AB":
        both = []
        for w, pairs, cut in (("r", right, slice(0, half // 2)), ("l", left, slice(half // 2, half))):
            both.append(lax.ppermute(going[w + p][cut], "dp", pairs))
        arrivals.append(both)

    width = n_dp * (slots + 1)
    total = 2 * n_dp * slots + 4 * WIDE
    ids = [v.reshape(n_dp, slots + 1, words, tile)[:, slots, 0, : slots + 1] for v in (got, got_other)]
    lists, counts, masks = call(
        functools.partial(list_kernel, n_dp, slots, groups, blocks, steps + 1),
        (
            jax.ShapeDtypeStruct((groups * total,), jnp.int32),
            jax.ShapeDtypeStruct((groups,), jnp.int32),
            pltpu.VMEM((2 * width, words, tile), jnp.int32),
        ),
        (core, *[v.reshape(width) for v in ids], near(got), near(got_other)),
        in_specs=[SMEM] * 3 + [VMEM] * 2,
        out_specs=(SMEM, SMEM, VMEM),
    )

    shared = [masks, own_sc, other_sc, att[0]]
    state_shape = pltpu.VMEM((2 * blocks, dims + extra, tile), F32)
    half_shape = pltpu.VMEM((blocks, dims + extra, tile), F32)

    def stage(g, bufs, state, hand=False):
        args = [lists, counts] + [near(v) for v in shared + bufs]
        outs, aliases = [state_shape], {}
        if state is not None:
            args.append(near(state))
            aliases[len(args) - 1] = 0
        if hand:
            outs.append(half_shape)
            for k, v in enumerate(shared + bufs):
                aliases[2 + k] = len(outs)
                outs.append(pltpu.VMEM(v.shape, v.dtype))
        return call(
            functools.partial(stage_kernel, g, groups, state is None, len(bufs)),
            outs,
            args,
            in_specs=[SMEM, SMEM] + [VMEM] * (len(args) - 2),
            out_specs=[VMEM] * len(outs),
            scratch=[
                pltpu.VMEM((2 * blocks, extra, tile), F32),
                pltpu.VMEM((sum(v.shape[0] for v in bufs), dims + extra, tile), BF16),
                *[pltpu.VMEM((WIDE, heads, tile, tile), F32)] * 2,
                *[pltpu.VMEM((WIDE, pad8(heads), tile), F32)] * 2,
            ],
            aliases=aliases,
            flops=8000000000,
        )

    state = None
    for g, bufs in enumerate(arrivals[:-1]):
        (state,) = stage(g, bufs, state)
    state, other, *rest = stage(steps + 1, arrivals[-1], state, True)
    back = lax.ppermute(other, "dp", swap)
    shared = rest[: len(shared)]
    (state,) = stage(steps + 2, rest[len(shared) :], state)
    return call(
        merge_kernel,
        jax.ShapeDtypeStruct((dims, nodes), BF16),
        (near(state), near(back), node_feats, out_bias.reshape(1, dims)),
    )


def solution(mesh):
    return jax.shard_map(
        local,
        mesh=mesh,
        in_specs=(
            P("mp", "dp"),
            P("mp", None),
            P("mp"),
            P("mp"),
            P("mp"),
            P("dp"),
            P("dp"),
            P("dp", None, None),
        ),
        out_specs=P("mp", "dp"),
        check_vma=False,
    )
```

time: 82.2 us -> 83.5 us (1.016)
  local copies, waits for them, and re-layouts: 10.6 us -> 0.25 us
  waiting for transfers between devices: 16.6 us -> 26.8 us
  starting transfers between devices: 29.9 us -> 31.9 us
    unnamed x39 -> x4, local copies, waits for them, and re-layouts: 9.19 us -> 0.01 us
    ppermute x16 -> x19, waiting for transfers between devices: 16.6 us -> 25.5 us  [the longest x12 13.3 us: local(): lax.ppermute(going[way], 'dp', right if way[0] == 'r' else left)]
    ppermute x1, starting transfers between devices: 6.8 us -> 9.04 us  [local(): back = lax.ppermute(other, 'dp', swap)]
    ppermute x16 -> x19, starting transfers between devices: 14.5 us -> 15.9 us  [the longest x12 8.9 us: local(): lax.ppermute(going[way], 'dp', right if way[0] == 'r' else left)]
    ppermute x1, waiting for transfers between devices: 0.01 us -> 1.34 us  [local(): back = lax.ppermute(other, 'dp', swap)]
    ppermute x1, starting transfers between devices: 1.58 us -> 0.37 us  [local(): other_sc = lax.ppermute(own_sc, 'dp', swap)]
    slice x2 -> x6, local copies, waits for them, and re-layouts: 1.12 us -> 0.07 us  [the longest x4 0.04 us: local(): both.append(lax.ppermute(going[w + p][cut], 'dp', pairs))]
    pallas_call x11 -> x13, Pallas kernels: 23.5 us -> 23.7 us  [call(): pl.pallas_call(kernel, out_shape=outs, in_specs=in_specs or [VMEM] * len(...]
  transfers between devices with their start and end apart: 19 -> 22, of which waited for: 5 -> 8; matrix products, arithmetic and copies ran while one was open for 1% -> 0% of each run, Pallas kernels for 24% -> 23%
where the time goes in v1:
time: 83.5 us; the launch traced here: 82.8 us
  starting transfers between devices  31.9 us (38%)
  waiting for transfers between devices  26.8 us (32%)
  Pallas kernels  23.7 us (28%)
    pallas_call x13, Pallas kernels, call(): pl.pallas_call(kernel, out_shape=outs, in_specs=in_specs or [VMEM] * len(...  23.7 us
    ppermute x12, waiting for transfers between devices, local(): lax.ppermute(going[way], 'dp', right if way[0] == 'r' else left)  13.3 us
    ppermute x2, waiting for transfers between devices, local(): inputs = [[x, lax.ppermute(x, 'mp', flip)] for x in cuts]  11.1 us
    ppermute x1, starting transfers between devices, local(): back = lax.ppermute(other, 'dp', swap)  9.04 us
    ppermute x12, starting transfers between devices, local(): lax.ppermute(going[way], 'dp', right if way[0] == 'r' else left)  8.9 us
    all_to_all x1, starting transfers between devices, local(): got = lax.all_to_all(packed, 'dp', split_axis=0, concat_axis=0, tiled=True)  6.53 us
    ppermute x4, starting transfers between devices, local(): both.append(lax.ppermute(going[w + p][cut], 'dp', pairs))  3.14 us
    ppermute x1, starting transfers between devices, local(): got_other = lax.ppermute(got, 'dp', swap)  2.37 us
  transfers between devices with their start and end apart: 22, of which 8 were waited for; matrix products, arithmetic and copies ran while one was open for 0% of the time, Pallas kernels for 23%

profile of v1, /device:TPU:11, one launch (start us, length us, event | category | flops | bytes accessed | tf_op | source)
XLA Modules:
  0.0 82.8 jit_solution(10379699584304787211)
XLA Ops:
  0.0 2.2 %shard_map.82 = s32[16,5,4,128]{3,2,1,0:T(4,128)} custom-call(s32[32]{0:T(128)} %rows_in.1, s32[32]{0:T(128)} %cols_in.1, s32[32,4,128]{2,1,0:T(4,128)} %masks_in.1), custom_call_target="tpu_custom_call" | custom-call | flops 1000000 | tf_op jit(solution)/shard_map/pallas_call | solution.py:300
  2.2 6.5 %all-to-all-start = ((s32[16,5,4,128]{3,2,1,0:T(4,128)}), s32[16,5,4,128]{3,2,1,0:T(4,128)S(1)}, u32[]{:S(2)}, u32[]{:S(2)}) async-start(s32[16,5,4,128]{3,2,1,0:T(4,128)} %shard_map.82), calls=%async_computation | async-start | bytes 327680 | tf_op jit(solution)/shard_map/all_to_all | solution.py:387
  8.8 1.1 %shard_map.84 = (bf16[128,1024]{1,0:T(8,128)(2,1)S(1)}, bf16[128,1024]{1,0:T(8,128)(2,1)S(1)}, bf16[128,256]{1,0:T(8,128)(2,1)S(1)}, f32[1,128]{1,0:T(1,128)S(1)}, f32[1,128]{1,0:T(1,128)S(1)}) custom-call(bf16[128,2048]{1,0:T(8,128)(2,1)} %x_ref.1, bf16[128,256]{1,0:T(8,128)(2,1)} %refs_1_.1, f32[1,128]{1,0:T(1,128)} %bitcast.17, f32[1,128]{1,0:T(1,128)} %bitcast.18), custom_call_target="tpu_custom_call" | custom-call | flops 1000000 | tf_op jit(solution)/shard_map/pallas_call | solution.py:300
  9.9 1.3 %collective-permute-start.2 = (bf16[128,1024]{1,0:T(8,128)(2,1)S(1)}, bf16[128,1024]{1,0:T(8,128)(2,1)S(1)}, u32[]{:S(2)}, u32[]{:S(2)}) collective-permute-start(bf16[128,1024]{1,0:T(8,128)(2,1)S(1)} %get-tuple-element.32.refs_0_), channel_id=1, source_target_pairs={{0,1},{1,0},{2,3},{3,2},{4,5},{5,4},{6,7},{7,6},{8,9},{9,8},{10,11... | collective-permute-start | bytes 786440 | tf_op jit(solution)/shard_map/ppermute | solution.py:367
  11.4 6.0 %collective-permute-done.2.refs_1_ = bf16[128,1024]{1,0:T(8,128)(2,1)S(1)} collective-permute-done((bf16[128,1024]{1,0:T(8,128)(2,1)S(1)}, bf16[128,1024]{1,0:T(8,128)(2,1)S(1)}, u32[]{:S(2)}, u32[]{:S(2)}) %collective-permute-start.2) | collective-permute-done | bytes 262176 | tf_op jit(solution)/shard_map/ppermute | solution.py:367
  17.4 0.5 shard_map.85
  17.9 5.1 %collective-permute-done.1.refs_1_ = bf16[128,1024]{1,0:T(8,128)(2,1)S(1)} collective-permute-done((bf16[128,1024]{1,0:T(8,128)(2,1)S(1)}, bf16[128,1024]{1,0:T(8,128)(2,1)S(1)}, u32[]{:S(2)}, u32[]{:S(2)}) %collective-permute-start.1) | collective-permute-done | bytes 262176 | tf_op jit(solution)/shard_map/ppermute | solution.py:367
  23.0 0.5 shard_map.86
  23.9 1.2 %collective-permute-start.8 = (bf16[8,136,128]{2,1,0:T(8,128)(2,1)S(1)}, bf16[8,136,128]{2,1,0:T(8,128)(2,1)S(1)}, u32[]{:S(2)}, u32[]{:S(2)}) collective-permute-start(bf16[8,136,128]{2,1,0:T(8,128)(2,1)S(1)} %get-tuple-element.35.refs_1_), channel_id=1, source_target_pairs={{0,4},{2,6},{4,12},{6,14},{8,0},{10,2},{12,20},{14,22},{16,8},{18,... | collective-permute-start | bytes 835592 | tf_op jit(solution)/shard_map/ppermute | solution.py:414
  25.3 1.2 %collective-permute-start.16 = (bf16[8,136,128]{2,1,0:T(8,128)(2,1)S(1)}, bf16[8,136,128]{2,1,0:T(8,128)(2,1)S(1)}, u32[]{:S(2)}, u32[]{:S(2)}) collective-permute-start(bf16[8,136,128]{2,1,0:T(8,128)(2,1)S(1)} %get-tuple-element.36.refs_0_), channel_id=1, source_target_pairs={{0,4},{2,6},{4,12},{6,14},{8,0},{10,2},{12,20},{14,22},{16,8},{18,... | collective-permute-start | bytes 835592 | tf_op jit(solution)/shard_map/ppermute | solution.py:414
  26.5 2.4 %collective-permute-start = (s32[80,4,128]{2,1,0:T(4,128)S(1)}, s32[80,4,128]{2,1,0:T(4,128)S(1)}, u32[]{:S(2)}, u32[]{:S(2)}) collective-permute-start(s32[80,4,128]{2,1,0:T(4,128)S(1)} %bitcast.12), channel_id=1, source_target_pairs={{0,2},{2,0},{4,6},{6,4},{8,10},{10,8},{12,14},{14,12},{16,18},{18,... | collective-permute-start | bytes 491528 | tf_op jit(solution)/shard_map/ppermute | solution.py:389
  28.9 1.0 %collective-permute-done.other_masks = s32[80,4,128]{2,1,0:T(4,128)S(1)} collective-permute-done((s32[80,4,128]{2,1,0:T(4,128)S(1)}, s32[80,4,128]{2,1,0:T(4,128)S(1)}, u32[]{:S(2)}, u32[]{:S(2)}) %collective-permute-start) | collective-permute-done | bytes 163872 | tf_op jit(solution)/shard_map/ppermute | solution.py:389
  30.5 2.3 %shard_map.83 = (s32[1056]{0:T(1024)S(1)}, s32[8]{0:T(128)S(1)}, s32[160,4,128]{2,1,0:T(4,128)S(1)}) custom-call(s32[1]{0:T(128)} %bitcast.core_ref, s32[80]{0:T(128)S(1)} %reshape_squeeze.6.own_ids, s32[80]{0:T(128)S(1)} %reshape_squeeze.7.other_ids, s32[80,4,128]{2,1,0:T(4,128)S(1)} %bitcast.13, s32[80,4,128]{2,1,0:T(4,128)S(1)} %collective-permute-done.other_masks), custom_call_target="tpu_custom_call" | custom-call | flops 1000000 | tf_op jit(solution)/shard_map/pallas_call | solution.py:300
  33.1 1.3 %collective-permute-start.9 = (bf16[8,136,128]{2,1,0:T(8,128)(2,1)S(1)}, bf16[8,136,128]{2,1,0:T(8,128)(2,1)S(1)}, u32[]{:S(2)}, u32[]{:S(2)}) collective-permute-start(bf16[8,136,128]{2,1,0:T(8,128)(2,1)S(1)} %collective-permute-done.8.refs_5_), channel_id=1, source_target_pairs={{0,4},{2,6},{4,12},{6,14},{8,0},{10,2},{12,20},{14,22},{16,8},{18,... | collective-permute-start | bytes 835592 | tf_op jit(solution)/shard_map/ppermute | solution.py:414
  34.3 2.2 %collective-permute-done.12.refs_2_ = bf16[8,136,128]{2,1,0:T(8,128)(2,1)S(1)} collective-permute-done((bf16[8,136,128]{2,1,0:T(8,128)(2,1)S(1)}, bf16[8,136,128]{2,1,0:T(8,128)(2,1)S(1)}, u32[]{:S(2)}, u32[]{:S(2)}) %collective-permute-start.12) | collective-permute-done | bytes 278560 | tf_op jit(solution)/shard_map/ppermute | solution.py:414
  36.8 1.2 %collective-permute-start.17 = (bf16[8,136,128]{2,1,0:T(8,128)(2,1)S(1)}, bf16[8,136,128]{2,1,0:T(8,128)(2,1)S(1)}, u32[]{:S(2)}, u32[]{:S(2)}) collective-permute-start(bf16[8,136,128]{2,1,0:T(8,128)(2,1)S(1)} %collective-permute-done.16.refs_4_), channel_id=1, source_target_pairs={{0,4},{2,6},{4,12},{6,14},{8,0},{10,2},{12,20},{14,22},{16,8},{18,... | collective-permute-start | bytes 835592 | tf_op jit(solution)/shard_map/ppermute | solution.py:414
  38.0 4.1 %shard_map.87.refs_4_ = f32[32,136,128]{2,1,0:T(8,128)S(1)} custom-call(s32[1056]{0:T(1024)S(1)} %get-tuple-element.25.list_ref, s32[8]{0:T(128)S(1)} %get-tuple-element.26.count_ref, s32[160,4,128]{2,1,0:T(4,128)S(1)} %get-tuple-element.27.masks_ref, f32[16,8,128]{2,1,0:T(8,128)S(1)} %get-tuple-element.34.own_sc, ...), custom_call_target="tpu_custom_call" | custom-call | flops 8000000000 | tf_op jit(solution)/shard_map/pallas_call | solution.py:300
  42.1 6.4 %collective-permute-done.13.refs_0_ = bf16[8,136,128]{2,1,0:T(8,128)(2,1)S(1)} collective-permute-done((bf16[8,136,128]{2,1,0:T(8,128)(2,1)S(1)}, bf16[8,136,128]{2,1,0:T(8,128)(2,1)S(1)}, u32[]{:S(2)}, u32[]{:S(2)}) %collective-permute-start.13) | collective-permute-done | bytes 278560 | tf_op jit(solution)/shard_map/ppermute | solution.py:414
  48.7 1.2 %collective-permute-start.18 = (bf16[8,136,128]{2,1,0:T(8,128)(2,1)S(1)}, bf16[8,136,128]{2,1,0:T(8,128)(2,1)S(1)}, u32[]{:S(2)}, u32[]{:S(2)}) collective-permute-start(bf16[8,136,128]{2,1,0:T(8,128)(2,1)S(1)} %collective-permute-done.17.refs_2_), channel_id=1, source_target_pairs={{0,4},{2,6},{4,12},{6,14},{8,0},{10,2},{12,20},{14,22},{16,8},{18,... | collective-permute-start | bytes 835592 | tf_op jit(solution)/shard_map/ppermute | solution.py:414
  49.9 1.2 %collective-permute-start.10 = (bf16[8,136,128]{2,1,0:T(8,128)(2,1)S(1)}, bf16[8,136,128]{2,1,0:T(8,128)(2,1)S(1)}, u32[]{:S(2)}, u32[]{:S(2)}) collective-permute-start(bf16[8,136,128]{2,1,0:T(8,128)(2,1)S(1)} %collective-permute-done.9.refs_3_), channel_id=1, source_target_pairs={{0,4},{2,6},{4,12},{6,14},{8,0},{10,2},{12,20},{14,22},{16,8},{18,... | collective-permute-start | bytes 835592 | tf_op jit(solution)/shard_map/ppermute | solution.py:414
  51.4 2.8 %shard_map.88.refs_2_ = f32[32,136,128]{2,1,0:T(8,128)S(1)} custom-call(s32[1056]{0:T(1024)S(1)} %get-tuple-element.25.list_ref, s32[8]{0:T(128)S(1)} %get-tuple-element.26.count_ref, s32[160,4,128]{2,1,0:T(4,128)S(1)} %get-tuple-element.27.masks_ref, f32[16,8,128]{2,1,0:T(8,128)S(1)} %get-tuple-element.34.own_sc, ...), custom_call_target="tpu_custom_call", output_to_operand_aliasing={{}: (10, {})} | custom-call | flops 8000000000 | tf_op jit(solution)/shard_map/pallas_call | solution.py:300
  54.9 1.2 %collective-permute-start.19 = (bf16[4,136,128]{2,1,0:T(8,128)(2,1)S(1)}, bf16[4,136,128]{2,1,0:T(8,128)(2,1)S(1)}, u32[]{:S(2)}, u32[]{:S(2)}) collective-permute-start(bf16[4,136,128]{2,1,0:T(8,128)(2,1)S(1)} %slice.29), channel_id=1, source_target_pairs={{0,4},{2,6},{4,12},{6,14},{8,0},{10,2},{12,20},{14,22},{16,8},{18,... | collective-permute-start | bytes 417800 | tf_op jit(solution)/shard_map/ppermute | solution.py:423
  56.2 4.4 %collective-permute-done.10.refs_1_ = bf16[8,136,128]{2,1,0:T(8,128)(2,1)S(1)} collective-permute-done((bf16[8,136,128]{2,1,0:T(8,128)(2,1)S(1)}, bf16[8,136,128]{2,1,0:T(8,128)(2,1)S(1)}, u32[]{:S(2)}, u32[]{:S(2)}) %collective-permute-start.10) | collective-permute-done | bytes 278560 | tf_op jit(solution)/shard_map/ppermute | solution.py:414
  60.6 1.2 %collective-permute-start.11 = (bf16[4,136,128]{2,1,0:T(8,128)(2,1)S(1)}, bf16[4,136,128]{2,1,0:T(8,128)(2,1)S(1)}, u32[]{:S(2)}, u32[]{:S(2)}) collective-permute-start(bf16[4,136,128]{2,1,0:T(8,128)(2,1)S(1)} %slice.27), channel_id=1, source_target_pairs={{0,4},{2,6},{4,12},{6,14},{8,0},{10,2},{12,20},{14,22},{16,8},{18,... | collective-permute-start | bytes 417800 | tf_op jit(solution)/shard_map/ppermute | solution.py:423
  62.1 2.8 %shard_map.89.refs_2_ = f32[32,136,128]{2,1,0:T(8,128)S(1)} custom-call(s32[1056]{0:T(1024)S(1)} %get-tuple-element.25.list_ref, s32[8]{0:T(128)S(1)} %get-tuple-element.26.count_ref, s32[160,4,128]{2,1,0:T(4,128)S(1)} %get-tuple-element.27.masks_ref, f32[16,8,128]{2,1,0:T(8,128)S(1)} %get-tuple-element.34.own_sc, ...), custom_call_target="tpu_custom_call", output_to_operand_aliasing={{}: (8, {})} | custom-call | flops 8000000000 | tf_op jit(solution)/shard_map/pallas_call | solution.py:300
  64.9 1.6 %shard_map.90.refs_2_ = f32[32,136,128]{2,1,0:T(8,128)S(1)} custom-call(s32[1056]{0:T(1024)S(1)} %get-tuple-element.25.list_ref, s32[8]{0:T(128)S(1)} %get-tuple-element.26.count_ref, s32[160,4,128]{2,1,0:T(4,128)S(1)} %get-tuple-element.27.masks_ref, f32[16,8,128]{2,1,0:T(8,128)S(1)} %get-tuple-element.34.own_sc, ...), custom_call_target="tpu_custom_call", output_to_operand_aliasing={{}: (8, {})} | custom-call | flops 8000000000 | tf_op jit(solution)/shard_map/pallas_call | solution.py:300
  66.6 2.2 %shard_map.91.refs_2_ = f32[32,136,128]{2,1,0:T(8,128)S(1)} custom-call(s32[1056]{0:T(1024)S(1)} %get-tuple-element.25.list_ref, s32[8]{0:T(128)S(1)} %get-tuple-element.26.count_ref, s32[160,4,128]{2,1,0:T(4,128)S(1)} %get-tuple-element.27.masks_ref, f32[16,8,128]{2,1,0:T(8,128)S(1)} %get-tuple-element.34.own_sc, ...), custom_call_target="tpu_custom_call", output_to_operand_aliasing={{}: (8, {})} | custom-call | flops 8000000000 | tf_op jit(solution)/shard_map/pallas_call | solution.py:300
  68.8 1.1 %shard_map.92 = (f32[32,136,128]{2,1,0:T(8,128)S(1)}, f32[16,136,128]{2,1,0:T(8,128)S(1)}, s32[160,4,128]{2,1,0:T(4,128)S(1)}, f32[16,8,128]{2,1,0:T(8,128)S(1)}...) custom-call(s32[1056]{0:T(1024)S(1)} %get-tuple-element.25.list_ref,, ...), custom_call_target="tpu_custom_call", output_to_operand_aliasing={{0}: (8, {}), {2}: (2, {}), {3}: (3, {}), {4}: (4, {}), {5}... | custom-call | flops 8000000000 | tf_op jit(solution)/shard_map/pallas_call | solution.py:300
  69.9 9.0 %collective-permute-start.20 = (f32[16,136,128]{2,1,0:T(8,128)S(1)}, f32[16,136,128]{2,1,0:T(8,128)S(1)}, u32[]{:S(2)}, u32[]{:S(2)}) collective-permute-start(f32[16,136,128]{2,1,0:T(8,128)S(1)} %get-tuple-element.44), channel_id=1, source_target_pairs={{0,2},{2,0},{4,6},{6,4},{8,10},{10,8},{12,14},{14,12},{16,18},{18,... | collective-permute-start | bytes 3342344 | tf_op jit(solution)/shard_map/ppermute | solution.py:476
  79.0 1.0 %shard_map.93.state_ref = f32[32,136,128]{2,1,0:T(8,128)S(1)} custom-call(s32[1056]{0:T(1024)S(1)} %get-tuple-element.25.list_ref, s32[8]{0:T(128)S(1)} %get-tuple-element.26.count_ref, s32[160,4,128]{2,1,0:T(4,128)S(1)} %get-tuple-element.37.masks_ref, f32[16,8,128]{2,1,0:T(8,128)S(1)} %get-tuple-element.38.own_sc, ...), custom_call_target="tpu_custom_call", output_to_operand_aliasing={{}: (8, {})} | custom-call | flops 8000000000 | tf_op jit(solution)/shard_map/pallas_call | solution.py:300
  80.0 1.3 %collective-permute-done.20.other_ref = f32[16,136,128]{2,1,0:T(8,128)S(1)} collective-permute-done((f32[16,136,128]{2,1,0:T(8,128)S(1)}, f32[16,136,128]{2,1,0:T(8,128)S(1)}, u32[]{:S(2)}, u32[]{:S(2)}) %collective-permute-start.20) | collective-permute-done | bytes 1114144 | tf_op jit(solution)/shard_map/ppermute | solution.py:476
  81.4 1.4 %shard_map.94 = bf16[128,2048]{1,0:T(8,128)(2,1)} custom-call(f32[32,136,128]{2,1,0:T(8,128)S(1)} %shard_map.93.state_ref, f32[16,136,128]{2,1,0:T(8,128)S(1)} %collective-permute-done.20.other_ref, bf16[128,2048]{1,0:T(8,128)(2,1)S(1)} %copy-done, f32[1,128]{1,0:T(1,128)S(1)} %bitcast.15), custom_call_target="tpu_custom_call" | custom-call | flops 1000000 | tf_op jit(solution)/shard_map/pallas_call | solution.py:300
  (37 shorter events, 3.6 us)
Async XLA Ops:
  2.2 24.3 %all-to-all-start = ((s32[16,5,4,128]{3,2,1,0:T(4,128)}), s32[16,5,4,128]{3,2,1,0:T(4,128)S(1)}, u32[]{:S(2)}, u32[]{:S(2)}) async-start(s32[16,5,4,128]{3,2,1,0:T(4,128)} %shard_map.82), calls=%async_computation | async-start | bytes 327680 | tf_op jit(solution)/shard_map/all_to_all | solution.py:387
  9.9 7.5 %collective-permute-start.2 = (bf16[128,1024]{1,0:T(8,128)(2,1)S(1)}, bf16[128,1024]{1,0:T(8,128)(2,1)S(1)}, u32[]{:S(2)}, u32[]{:S(2)}) collective-permute-start(bf16[128,1024]{1,0:T(8,128)(2,1)S(1)} %get-tuple-element.32.refs_0_), channel_id=1, source_target_pairs={{0,1},{1,0},{2,3},{3,2},{4,5},{5,4},{6,7},{7,6},{8,9},{9,8},{10,11... | collective-permute-start | bytes 786440 | tf_op jit(solution)/shard_map/ppermute | solution.py:367
  11.2 11.8 %collective-permute-start.1 = (bf16[128,1024]{1,0:T(8,128)(2,1)S(1)}, bf16[128,1024]{1,0:T(8,128)(2,1)S(1)}, u32[]{:S(2)}, u32[]{:S(2)}) collective-permute-start(bf16[128,1024]{1,0:T(8,128)(2,1)S(1)} %get-tuple-element.31.refs_0_), channel_id=1, source_target_pairs={{0,1},{1,0},{2,3},{3,2},{4,5},{5,4},{6,7},{7,6},{8,9},{9,8},{10,11... | collective-permute-start | bytes 786440 | tf_op jit(solution)/shard_map/ppermute | solution.py:367
  23.5 9.3 %collective-permute-start.4 = (bf16[8,136,128]{2,1,0:T(8,128)(2,1)S(1)}, bf16[8,136,128]{2,1,0:T(8,128)(2,1)S(1)}, u32[]{:S(2)}, u32[]{:S(2)}) collective-permute-start(bf16[8,136,128]{2,1,0:T(8,128)(2,1)S(1)} %get-tuple-element.35.refs_1_), channel_id=1, source_target_pairs={{0,8},{2,10},{4,0},{6,2},{8,16},{10,18},{12,4},{14,6},{16,24},{18,... | collective-permute-start | bytes 835592 | tf_op jit(solution)/shard_map/ppermute | solution.py:414
  23.9 9.2 %collective-permute-start.8 = (bf16[8,136,128]{2,1,0:T(8,128)(2,1)S(1)}, bf16[8,136,128]{2,1,0:T(8,128)(2,1)S(1)}, u32[]{:S(2)}, u32[]{:S(2)}) collective-permute-start(bf16[8,136,128]{2,1,0:T(8,128)(2,1)S(1)} %get-tuple-element.35.refs_1_), channel_id=1, source_target_pairs={{0,4},{2,6},{4,12},{6,14},{8,0},{10,2},{12,20},{14,22},{16,8},{18,... | collective-permute-start | bytes 835592 | tf_op jit(solution)/shard_map/ppermute | solution.py:414
  25.1 11.5 %collective-permute-start.12 = (bf16[8,136,128]{2,1,0:T(8,128)(2,1)S(1)}, bf16[8,136,128]{2,1,0:T(8,128)(2,1)S(1)}, u32[]{:S(2)}, u32[]{:S(2)}) collective-permute-start(bf16[8,136,128]{2,1,0:T(8,128)(2,1)S(1)} %get-tuple-element.36.refs_0_), channel_id=1, source_target_pairs={{0,8},{2,10},{4,0},{6,2},{8,16},{10,18},{12,4},{14,6},{16,24},{18,... | collective-permute-start | bytes 835592 | tf_op jit(solution)/shard_map/ppermute | solution.py:414
  25.3 11.5 %collective-permute-start.16 = (bf16[8,136,128]{2,1,0:T(8,128)(2,1)S(1)}, bf16[8,136,128]{2,1,0:T(8,128)(2,1)S(1)}, u32[]{:S(2)}, u32[]{:S(2)}) collective-permute-start(bf16[8,136,128]{2,1,0:T(8,128)(2,1)S(1)} %get-tuple-element.36.refs_0_), channel_id=1, source_target_pairs={{0,4},{2,6},{4,12},{6,14},{8,0},{10,2},{12,20},{14,22},{16,8},{18,... | collective-permute-start | bytes 835592 | tf_op jit(solution)/shard_map/ppermute | solution.py:414
  26.5 3.4 %collective-permute-start = (s32[80,4,128]{2,1,0:T(4,128)S(1)}, s32[80,4,128]{2,1,0:T(4,128)S(1)}, u32[]{:S(2)}, u32[]{:S(2)}) collective-permute-start(s32[80,4,128]{2,1,0:T(4,128)S(1)} %bitcast.12), channel_id=1, source_target_pairs={{0,2},{2,0},{4,6},{6,4},{8,10},{10,8},{12,14},{14,12},{16,18},{18,... | collective-permute-start | bytes 491528 | tf_op jit(solution)/shard_map/ppermute | solution.py:389
  29.9 8.1 %collective-permute-start.3 = (f32[16,8,128]{2,1,0:T(8,128)S(1)}, f32[16,8,128]{2,1,0:T(8,128)S(1)}, u32[]{:S(2)}, u32[]{:S(2)}) collective-permute-start(f32[16,8,128]{2,1,0:T(8,128)S(1)} %get-tuple-element.34.own_sc), channel_id=1, source_target_pairs={{0,2},{2,0},{4,6},{6,4},{8,10},{10,8},{12,14},{14,12},{16,18},{18,... | collective-permute-start | bytes 196616 | tf_op jit(solution)/shard_map/ppermute | solution.py:408
  32.8 18.3 %collective-permute-start.5 = (bf16[8,136,128]{2,1,0:T(8,128)(2,1)S(1)}, bf16[8,136,128]{2,1,0:T(8,128)(2,1)S(1)}, u32[]{:S(2)}, u32[]{:S(2)}) collective-permute-start(bf16[8,136,128]{2,1,0:T(8,128)(2,1)S(1)} %collective-permute-done.4.refs_3_), channel_id=1, source_target_pairs={{0,8},{2,10},{4,0},{6,2},{8,16},{10,18},{12,4},{14,6},{16,24},{18,... | collective-permute-start | bytes 835592 | tf_op jit(solution)/shard_map/ppermute | solution.py:414
  33.1 16.9 %collective-permute-start.9 = (bf16[8,136,128]{2,1,0:T(8,128)(2,1)S(1)}, bf16[8,136,128]{2,1,0:T(8,128)(2,1)S(1)}, u32[]{:S(2)}, u32[]{:S(2)}) collective-permute-start(bf16[8,136,128]{2,1,0:T(8,128)(2,1)S(1)} %collective-permute-done.8.refs_5_), channel_id=1, source_target_pairs={{0,4},{2,6},{4,12},{6,14},{8,0},{10,2},{12,20},{14,22},{16,8},{18,... | collective-permute-start | bytes 835592 | tf_op jit(solution)/shard_map/ppermute | solution.py:414
  36.5 11.9 %collective-permute-start.13 = (bf16[8,136,128]{2,1,0:T(8,128)(2,1)S(1)}, bf16[8,136,128]{2,1,0:T(8,128)(2,1)S(1)}, u32[]{:S(2)}, u32[]{:S(2)}) collective-permute-start(bf16[8,136,128]{2,1,0:T(8,128)(2,1)S(1)} %collective-permute-done.12.refs_2_), channel_id=1, source_target_pairs={{0,8},{2,10},{4,0},{6,2},{8,16},{10,18},{12,4},{14,6},{16,24},{18,... | collective-permute-start | bytes 835592 | tf_op jit(solution)/shard_map/ppermute | solution.py:414
  36.8 11.9 %collective-permute-start.17 = (bf16[8,136,128]{2,1,0:T(8,128)(2,1)S(1)}, bf16[8,136,128]{2,1,0:T(8,128)(2,1)S(1)}, u32[]{:S(2)}, u32[]{:S(2)}) collective-permute-start(bf16[8,136,128]{2,1,0:T(8,128)(2,1)S(1)} %collective-permute-done.16.refs_4_), channel_id=1, source_target_pairs={{0,4},{2,6},{4,12},{6,14},{8,0},{10,2},{12,20},{14,22},{16,8},{18,... | collective-permute-start | bytes 835592 | tf_op jit(solution)/shard_map/ppermute | solution.py:414
  48.5 6.1 %collective-permute-start.14 = (bf16[8,136,128]{2,1,0:T(8,128)(2,1)S(1)}, bf16[8,136,128]{2,1,0:T(8,128)(2,1)S(1)}, u32[]{:S(2)}, u32[]{:S(2)}) collective-permute-start(bf16[8,136,128]{2,1,0:T(8,128)(2,1)S(1)} %collective-permute-done.13.refs_0_), channel_id=1, source_target_pairs={{0,8},{2,10},{4,0},{6,2},{8,16},{10,18},{12,4},{14,6},{16,24},{18,... | collective-permute-start | bytes 835592 | tf_op jit(solution)/shard_map/ppermute | solution.py:414
  48.7 6.2 %collective-permute-start.18 = (bf16[8,136,128]{2,1,0:T(8,128)(2,1)S(1)}, bf16[8,136,128]{2,1,0:T(8,128)(2,1)S(1)}, u32[]{:S(2)}, u32[]{:S(2)}) collective-permute-start(bf16[8,136,128]{2,1,0:T(8,128)(2,1)S(1)} %collective-permute-done.17.refs_2_), channel_id=1, source_target_pairs={{0,4},{2,6},{4,12},{6,14},{8,0},{10,2},{12,20},{14,22},{16,8},{18,... | collective-permute-start | bytes 835592 | tf_op jit(solution)/shard_map/ppermute | solution.py:414
  49.9 10.6 %collective-permute-start.10 = (bf16[8,136,128]{2,1,0:T(8,128)(2,1)S(1)}, bf16[8,136,128]{2,1,0:T(8,128)(2,1)S(1)}, u32[]{:S(2)}, u32[]{:S(2)}) collective-permute-start(bf16[8,136,128]{2,1,0:T(8,128)(2,1)S(1)} %collective-permute-done.9.refs_3_), channel_id=1, source_target_pairs={{0,4},{2,6},{4,12},{6,14},{8,0},{10,2},{12,20},{14,22},{16,8},{18,... | collective-permute-start | bytes 835592 | tf_op jit(solution)/shard_map/ppermute | solution.py:414
  51.1 10.7 %collective-permute-start.6 = (bf16[8,136,128]{2,1,0:T(8,128)(2,1)S(1)}, bf16[8,136,128]{2,1,0:T(8,128)(2,1)S(1)}, u32[]{:S(2)}, u32[]{:S(2)}) collective-permute-start(bf16[8,136,128]{2,1,0:T(8,128)(2,1)S(1)} %collective-permute-done.5.refs_1_), channel_id=1, source_target_pairs={{0,8},{2,10},{4,0},{6,2},{8,16},{10,18},{12,4},{14,6},{16,24},{18,... | collective-permute-start | bytes 835592 | tf_op jit(solution)/shard_map/ppermute | solution.py:414
  54.6 12.0 %collective-permute-start.15 = (bf16[4,136,128]{2,1,0:T(8,128)(2,1)S(1)}, bf16[4,136,128]{2,1,0:T(8,128)(2,1)S(1)}, u32[]{:S(2)}, u32[]{:S(2)}) collective-permute-start(bf16[4,136,128]{2,1,0:T(8,128)(2,1)S(1)} %slice.28), channel_id=1, source_target_pairs={{0,8},{2,10},{4,0},{6,2},{8,16},{10,18},{12,4},{14,6},{16,24},{18,... | collective-permute-start | bytes 417800 | tf_op jit(solution)/shard_map/ppermute | solution.py:423
  54.9 11.6 %collective-permute-start.19 = (bf16[4,136,128]{2,1,0:T(8,128)(2,1)S(1)}, bf16[4,136,128]{2,1,0:T(8,128)(2,1)S(1)}, u32[]{:S(2)}, u32[]{:S(2)}) collective-permute-start(bf16[4,136,128]{2,1,0:T(8,128)(2,1)S(1)} %slice.29), channel_id=1, source_target_pairs={{0,4},{2,6},{4,12},{6,14},{8,0},{10,2},{12,20},{14,22},{16,8},{18,... | collective-permute-start | bytes 417800 | tf_op jit(solution)/shard_map/ppermute | solution.py:423
  60.6 8.2 %collective-permute-start.11 = (bf16[4,136,128]{2,1,0:T(8,128)(2,1)S(1)}, bf16[4,136,128]{2,1,0:T(8,128)(2,1)S(1)}, u32[]{:S(2)}, u32[]{:S(2)}) collective-permute-start(bf16[4,136,128]{2,1,0:T(8,128)(2,1)S(1)} %slice.27), channel_id=1, source_target_pairs={{0,4},{2,6},{4,12},{6,14},{8,0},{10,2},{12,20},{14,22},{16,8},{18,... | collective-permute-start | bytes 417800 | tf_op jit(solution)/shard_map/ppermute | solution.py:423
  61.8 7.0 %collective-permute-start.7 = (bf16[4,136,128]{2,1,0:T(8,128)(2,1)S(1)}, bf16[4,136,128]{2,1,0:T(8,128)(2,1)S(1)}, u32[]{:S(2)}, u32[]{:S(2)}) collective-permute-start(bf16[4,136,128]{2,1,0:T(8,128)(2,1)S(1)} %slice.26), channel_id=1, source_target_pairs={{0,8},{2,10},{4,0},{6,2},{8,16},{10,18},{12,4},{14,6},{16,24},{18,... | collective-permute-start | bytes 417800 | tf_op jit(solution)/shard_map/ppermute | solution.py:423
  69.9 11.4 %collective-permute-start.20 = (f32[16,136,128]{2,1,0:T(8,128)S(1)}, f32[16,136,128]{2,1,0:T(8,128)S(1)}, u32[]{:S(2)}, u32[]{:S(2)}) collective-permute-start(f32[16,136,128]{2,1,0:T(8,128)S(1)} %get-tuple-element.44), channel_id=1, source_target_pairs={{0,2},{2,0},{4,6},{6,4},{8,10},{10,8},{12,14},{14,12},{16,18},{18,... | collective-permute-start | bytes 3342344 | tf_op jit(solution)/shard_map/ppermute | solution.py:476
  79.0 2.4 %copy-start = (bf16[128,2048]{1,0:T(8,128)(2,1)S(1)}, bf16[128,2048]{1,0:T(8,128)(2,1)}, u32[]{:S(2)}) copy-start(bf16[128,2048]{1,0:T(8,128)(2,1)} %x_ref.1) | copy-start | bytes 1572868
  79.0 2.4 %copy-start.1 = (f32[128]{0:T(128)S(1)}, f32[128]{0:T(128)}, u32[]{:S(2)}) copy-start(f32[128]{0:T(128)} %param.12) | copy-start | bytes 1540

commit v2 on v1

--- a/solution.py
+++ b/solution.py
@@ -1,4 +1,5 @@
 import functools
+import math
 
 import jax
 import jax.numpy as jnp
@@ -15,7 +16,7 @@
 BF16 = jnp.bfloat16
 
 
-WIDE = 1
+WIDE = 2
 LIMIT = 16 * 1024 * 1024
 
 VMEM = pl.BlockSpec(memory_space=pltpu.VMEM)
@@ -100,47 +101,50 @@
         copy.wait()
 
 
-def pack_kernel(blocks, place, groups, rows_in, cols_in, masks_in, out_ref, rows_ref, cols_ref, masks_ref, count, place_ref, sems):
-    ins, tos = (rows_in, cols_in, masks_in), (rows_ref, cols_ref, masks_ref)
-    copies = [pltpu.make_async_copy(v, w, sems.at[k]) for k, (v, w) in enumerate(zip(ins, tos))]
-    for copy in copies:
-        copy.start()
+def pack_kernel(blocks, place, groups, rows_ref, cols_ref, masks_ref, out_ref, count, place_ref, codes):
     devices, slots = out_ref.shape[0], out_ref.shape[1] - 1
     words = out_ref.shape[2:]
     half = blocks // 2
     chips = len(place)
-    lane = lax.broadcasted_iota(jnp.int32, words, 1)
+    width = slots + 2
     for c in range(chips):
         place_ref[c] = place[c]
     for d in range(devices):
-        count[d] = 0
-        out_ref[d, slots] = jnp.zeros(words, jnp.int32)
-    for copy in copies:
-        copy.wait()
+        count[2 * d] = 0
+        count[2 * d + 1] = 0
+        for n in range(slots):
+            codes[d * width + n] = 0
 
     def body(t, carry):
         row, col = rows_ref[t], cols_ref[t]
         owner, row_at = split(row, blocks)
         holder, col_at = split(col, blocks)
-        at = count[owner]
-        count[owner] = at + 1
+        odd = holder & 1
+        have = count[2 * owner + odd]
+        count[2 * owner + odd] = have + 1
+        at = jnp.where(odd == 1, slots - 1 - have, have)
         out_ref[owner, at] = masks_ref[t]
         back = place_ref[owner >> 1] - place_ref[holder >> 1]
         back = jnp.where(back < 0, back + chips, back)
         step = jnp.minimum(back, chips - back)
         part, j = split(col_at, half)
         last = 2 * back == chips
+        before = step == chips // 2 - 1
         spot = col_at + jnp.where(back > step, blocks, 0) + jnp.where(step == 1, blocks, 0)
-        before = step == chips // 2 - 1
         spot = jnp.where(before, j + jnp.where(back > step, half, 0), jnp.where(last, j, spot))
         group = jnp.where(step > 0, step - 1, 0) + jnp.where(before | last, part, 0) + jnp.where(last, 1, 0)
-        code = ((row_at * (4 * blocks) + spot) * 2 + (holder & 1)) * groups + group
-        here = out_ref[owner, slots]
-        here = jnp.where(lane == at, code, jnp.where(lane == slots, at + 1, here))
-        out_ref[owner, slots] = here
+        codes[owner * width + at] = (row_at * (4 * blocks) + spot) * groups + group
         return carry
 
     lax.fori_loop(0, rows_ref.shape[0], body, 0)
+    lane = lax.broadcasted_iota(jnp.int32, words, 1)
+    for d in range(devices):
+        here = jnp.zeros(words, jnp.int32)
+        for n in range(slots):
+            here = jnp.where(lane == n, codes[d * width + n], here)
+        for n in range(2):
+            here = jnp.where(lane == slots + n, count[2 * d + n], here)
+        out_ref[d, slots] = here
 
 
 def list_kernel(devices, slots, groups, blocks, final, core_ref, own_ids, other_ids, own_masks, other_masks, list_ref, count_ref, masks_ref):
@@ -151,28 +155,30 @@
         count_ref[g] = 0
     for side, (ids, masks) in enumerate(((own_ids, own_masks), (other_ids, other_masks))):
         masks_ref[side * width : (side + 1) * width] = masks[...]
-        for d in range(devices):
-            base = d * (slots + 1)
-
-            def body(n, carry, side=side, ids=ids, base=base):
-                code, group = split(ids[base + n], groups)
-
-                @pl.when((code & 1) == core)
-                def _():
-                    code_here = (code >> 1) + side * (4 * blocks * blocks)
-                    to = group if side else group + jnp.where(group == final, 1, 0)
-                    at = count_ref[to]
-                    list_ref[to * total + at] = (code_here * (2 * width) + side * width + base + n) * 2 + 1
-                    count_ref[to] = at + 1
-
+        turn = 0 if side else 1
+
+        def holder(d, carry, side=side, ids=ids, turn=turn):
+            at_ids, at_slots = d * (slots + 2), d * (slots + 1) + side * width
+            number = ids[at_ids + slots + core]
+            base = jnp.where(core == 1, slots - number, 0)
+
+            def body(n, carry):
+                code, group = split(ids[at_ids + n], groups)
+                to = group + jnp.where(group == final, turn, 0)
+                at = count_ref[to]
+                code = code + side * (4 * blocks * blocks)
+                list_ref[to * total + at] = (code * (2 * width) + at_slots + n) * 2 + 1
+                count_ref[to] = at + 1
                 return carry
 
-            lax.fori_loop(0, ids[base + slots], body, 0)
+            return lax.fori_loop(base, base + number, body, carry)
+
+        lax.fori_loop(0, devices, holder, 0)
     for g in range(groups):
         at = count_ref[g]
         for k in range(3 * WIDE):
             list_ref[g * total + at + k] = 0
-        count_ref[g] = lax.div(at + 2 * WIDE - 1, 2 * WIDE)
+        count_ref[g] = lax.div(at + WIDE - 1, WIDE)
 
 
 def prepare(entry, fields, heads, dims, masks_ref, att, buf, edges, tops):
@@ -219,7 +225,7 @@
         state[row, at, :] = state[row, at, :] * alpha[h : h + 1] + values[h][:HD]
 
 
-def stage_kernel(group, groups, first, count, list_ref, count_ref, masks_ref, own_sc, other_sc, src_ref, *refs):
+def stage_kernel(group, groups, first, short, count, list_ref, count_ref, masks_ref, own_sc, other_sc, src_ref, *refs):
     pays, (tscore, buf, edges0, edges1, tops0, tops1) = refs[:count], refs[-6:]
     outs = refs[count if first else count + 1 : -6]
     state = outs[0]
@@ -264,23 +270,42 @@
             space = [v.at[k] for v in spaces[side]]
             absorb(fields(entry), heads, dims, tscore, buf, *space, state)
 
+    number = count_ref[group]
+
     def body(i, carry):
         ready(2 * i + 1, 1)
         take(2 * i, 0)
-        ready(2 * i + 2, 0)
-        take(2 * i + 1, 1)
+
+        @pl.when(2 * i + 1 < number)
+        def _():
+            ready(2 * i + 2, 0)
+            take(2 * i + 1, 1)
+
         return carry
 
-    ready(0, 0)
-    lax.fori_loop(0, count_ref[group], body, 0)
+    def plain(i, carry):
+        ready(i, 0)
+        take(i, 0)
+        return carry
+
+    if short:
+        lax.fori_loop(0, number, plain, 0)
+    else:
+
+        @pl.when(number > 0)
+        def _():
+            ready(0, 0)
+            lax.fori_loop(0, (number + 1) >> 1, body, 0)
+
     if len(outs) > 1:
         outs[1][...] = state[blocks:]
 
 
-def merge_kernel(state_ref, other_ref, x_ref, bias_ref, out_ref):
+def merge_kernel(state_ref, other_ref, x_ref, bias_ref, whole_ref, out_ref, sems):
     blocks, dims, tile = other_ref.shape[0], x_ref.shape[0], other_ref.shape[2]
     heads = dims // HD
     bias = column(bias_ref)
+    share, copies = blocks // sems.shape[0], []
     for b in range(blocks):
         m1, m2 = state_ref[b, dims : dims + heads], other_ref[b, dims : dims + heads]
         l1 = state_ref[b, dims + heads : dims + 2 * heads]
@@ -294,6 +319,12 @@
         at = slice(b * tile, (b + 1) * tile)
         v = mixed.reshape(dims, tile) + x_ref[:, at].astype(F32) + bias
         out_ref[:, at] = jnp.where(v > 0, v, jnp.exp(jnp.minimum(v, 0.0)) - 1.0).astype(BF16)
+        if (b + 1) % share == 0:
+            at = slice((b + 1 - share) * tile, (b + 1) * tile)
+            copies.append(pltpu.make_async_copy(out_ref.at[:, at], whole_ref.at[:, at], sems.at[b // share]))
+            copies[-1].start()
+    for copy in copies:
+        copy.wait()
 
 
 def call(kernel, outs, args, in_specs=None, out_specs=VMEM, scratch=(), aliases=None, flops=1000000):
@@ -311,6 +342,10 @@
 
 def near(x):
     return pltpu.with_memory_space_constraint(x, pltpu.VMEM)
+
+
+def held(x):
+    return pltpu.with_memory_space_constraint(x, pltpu.SMEM)
 
 
 def far(x):
@@ -351,15 +386,16 @@
     core = jnp.full((1,), lax.axis_index("dp") & 1, jnp.int32)
     parts = 2 if n_mp == 2 else 1
     moved = [node_feats, proj_weight, att_src.reshape(1, dims), att_dst.reshape(1, dims)]
-    shapes = [(node_feats.shape[0], nodes // parts)] * parts + [v.shape for v in moved[1:]]
-    kinds = [BF16] * (parts + 1) + [F32] * 2
+    moved += [tile_masks, tile_rows, tile_cols]
+    shapes = [((node_feats.shape[0], nodes // parts), BF16)] * parts + [(v.shape, v.dtype) for v in moved[1:]]
+    spaces = [pltpu.VMEM] * (len(shapes) - 2) + [pltpu.SMEM] * 2
     anywhere = pl.BlockSpec(memory_space=pl.ANY)
-    *cuts, weight, a_src, a_dst = call(
+    *cuts, weight, a_src, a_dst, near_masks, near_rows, near_cols = call(
         functools.partial(open_kernel, parts),
-        [pltpu.VMEM(v, k) for v, k in zip(shapes, kinds)],
+        [space(*v) for space, v in zip(spaces, shapes)],
         [far(v) for v in moved],
         in_specs=[anywhere] * len(moved),
-        out_specs=[VMEM] * len(shapes),
+        out_specs=[pl.BlockSpec(memory_space=v) for v in spaces],
         scratch=[pltpu.SemaphoreType.DMA((len(shapes),))],
     )
     if n_mp == 2:
@@ -373,15 +409,12 @@
     packed = call(
         functools.partial(pack_kernel, blocks, place, groups),
         pltpu.HBM((n_dp, slots + 1, words, tile), jnp.int32),
-        [far(v) for v in (tile_rows, tile_cols, tile_masks)],
-        in_specs=[anywhere] * 3,
+        [held(near_rows), held(near_cols), near(near_masks)],
+        in_specs=[SMEM, SMEM, VMEM],
         scratch=[
-            pltpu.SMEM(tile_rows.shape, jnp.int32),
-            pltpu.SMEM(tile_cols.shape, jnp.int32),
-            pltpu.VMEM(tile_masks.shape, jnp.int32),
-            pltpu.SMEM((n_dp,), jnp.int32),
+            pltpu.SMEM((2 * n_dp,), jnp.int32),
             pltpu.SMEM((chips,), jnp.int32),
-            pltpu.SemaphoreType.DMA((3,)),
+            pltpu.SMEM((n_dp * (slots + 2),), jnp.int32),
         ],
     )
     got = lax.all_to_all(packed, "dp", split_axis=0, concat_axis=0, tiled=True)
@@ -425,15 +458,15 @@
 
     width = n_dp * (slots + 1)
     total = 2 * n_dp * slots + 4 * WIDE
-    ids = [v.reshape(n_dp, slots + 1, words, tile)[:, slots, 0, : slots + 1] for v in (got, got_other)]
+    ids = [v.reshape(n_dp, slots + 1, words, tile)[:, slots, 0, : slots + 2] for v in (got, got_other)]
     lists, counts, masks = call(
         functools.partial(list_kernel, n_dp, slots, groups, blocks, steps + 1),
         (
-            jax.ShapeDtypeStruct((groups * total,), jnp.int32),
-            jax.ShapeDtypeStruct((groups,), jnp.int32),
+            pltpu.SMEM((groups * total,), jnp.int32),
+            pltpu.SMEM((groups,), jnp.int32),
             pltpu.VMEM((2 * width, words, tile), jnp.int32),
         ),
-        (core, *[v.reshape(width) for v in ids], near(got), near(got_other)),
+        (core, *[v.reshape(n_dp * (slots + 2)) for v in ids], near(got), near(got_other)),
         in_specs=[SMEM] * 3 + [VMEM] * 2,
         out_specs=(SMEM, SMEM, VMEM),
     )
@@ -443,7 +476,7 @@
     half_shape = pltpu.VMEM((blocks, dims + extra, tile), F32)
 
     def stage(g, bufs, state, hand=False):
-        args = [lists, counts] + [near(v) for v in shared + bufs]
+        args = [held(lists), held(counts)] + [near(v) for v in shared + bufs]
         outs, aliases = [state_shape], {}
         if state is not None:
             args.append(near(state))
@@ -454,7 +487,7 @@
                 aliases[2 + k] = len(outs)
                 outs.append(pltpu.VMEM(v.shape, v.dtype))
         return call(
-            functools.partial(stage_kernel, g, groups, state is None, len(bufs)),
+            functools.partial(stage_kernel, g, groups, state is None, g >= steps, len(bufs)),
             outs,
             args,
             in_specs=[SMEM, SMEM] + [VMEM] * (len(args) - 2),
@@ -480,6 +513,8 @@
         merge_kernel,
         jax.ShapeDtypeStruct((dims, nodes), BF16),
         (near(state), near(back), node_feats, out_bias.reshape(1, dims)),
+        out_specs=anywhere,
+        scratch=[pltpu.VMEM((dims, nodes), BF16), pltpu.SemaphoreType.DMA((math.gcd(blocks, 4),))],
     )
 
 

time: 83.5 us -> 80.1 us (0.959)
  Pallas kernels: 23.7 us -> 16.7 us
  waiting for transfers between devices: 26.8 us -> 30.8 us
    pallas_call x13, Pallas kernels: 23.7 us -> 16.7 us  [call(): pl.pallas_call(kernel, out_shape=outs, in_specs=in_specs or [VMEM] * len(...]
    ppermute x12, waiting for transfers between devices: 13.3 us -> 15.9 us  [local(): lax.ppermute(going[way], 'dp', right if way[0] == 'r' else left)]
    ppermute x1, waiting for transfers between devices: 1.34 us -> 2.28 us  [local(): back = lax.ppermute(other, 'dp', swap)]
  transfers between devices with their start and end apart: 22 -> 22, of which waited for: 8 -> 9; matrix products, arithmetic and copies ran while one was open for 0% -> 0% of each run, Pallas kernels for 23% -> 16%
where the time goes in v2:
time: 80.1 us; the launch traced here: 79.8 us
  starting transfers between devices  31.8 us (40%)
  waiting for transfers between devices  30.8 us (38%)
  Pallas kernels  16.7 us (21%)
    pallas_call x13, Pallas kernels, call(): pl.pallas_call(kernel, out_shape=outs, in_specs=in_specs or [VMEM] * len(...  16.7 us
    ppermute x12, waiting for transfers between devices, local(): lax.ppermute(going[way], 'dp', right if way[0] == 'r' else left)  15.9 us
    ppermute x2, waiting for transfers between devices, local(): inputs = [[x, lax.ppermute(x, 'mp', flip)] for x in cuts]  11.1 us
    ppermute x1, starting transfers between devices, local(): back = lax.ppermute(other, 'dp', swap)  9.04 us
    ppermute x12, starting transfers between devices, local(): lax.ppermute(going[way], 'dp', right if way[0] == 'r' else left)  8.9 us
    all_to_all x1, starting transfers between devices, local(): got = lax.all_to_all(packed, 'dp', split_axis=0, concat_axis=0, tiled=True)  6.52 us
    ppermute x4, starting transfers between devices, local(): both.append(lax.ppermute(going[w + p][cut], 'dp', pairs))  3.14 us
    ppermute x1, starting transfers between devices, local(): got_other = lax.ppermute(got, 'dp', swap)  2.37 us
  transfers between devices with their start and end apart: 22, of which 9 were waited for; matrix products, arithmetic and copies ran while one was open for 0% of the time, Pallas kernels for 16%

profile of v2, /device:TPU:11, one launch (start us, length us, event | category | flops | bytes accessed | tf_op | source)
XLA Modules:
  0.0 79.8 jit_solution(16208667772421395422)
XLA Ops:
  0.0 1.1 %shard_map.82 = (bf16[128,1024]{1,0:T(8,128)(2,1)S(1)}, bf16[128,1024]{1,0:T(8,128)(2,1)S(1)}, bf16[128,256]{1,0:T(8,128)(2,1)S(1)}, f32[1,128]{1,0:T(1,128)S(1)...) custom-call(bf16[128,2048]{1,0:T(8,128)(2,1)} %x_ref.1, ...), custom_call_target="tpu_custom_call" | custom-call | flops 1000000 | tf_op jit(solution)/shard_map/pallas_call | solution.py:331
  1.1 1.5 %shard_map.83 = s32[16,5,4,128]{3,2,1,0:T(4,128)} custom-call(s32[32]{0:T(128)S(4)} %get-tuple-element.28.rows_ref, s32[32]{0:T(128)S(4)} %get-tuple-element.29.cols_ref, s32[32,4,128]{2,1,0:T(4,128)S(1)} %get-tuple-element.30.masks_ref), custom_call_target="tpu_custom_call" | custom-call | flops 1000000 | tf_op jit(solution)/shard_map/pallas_call | solution.py:331
  2.7 6.5 %all-to-all-start = ((s32[16,5,4,128]{3,2,1,0:T(4,128)}), s32[16,5,4,128]{3,2,1,0:T(4,128)S(1)}, u32[]{:S(2)}, u32[]{:S(2)}) async-start(s32[16,5,4,128]{3,2,1,0:T(4,128)} %shard_map.83), calls=%async_computation | async-start | bytes 327680 | tf_op jit(solution)/shard_map/all_to_all | solution.py:420
  9.2 1.2 %collective-permute-start.2 = (bf16[128,1024]{1,0:T(8,128)(2,1)S(1)}, bf16[128,1024]{1,0:T(8,128)(2,1)S(1)}, u32[]{:S(2)}, u32[]{:S(2)}) collective-permute-start(bf16[128,1024]{1,0:T(8,128)(2,1)S(1)} %get-tuple-element.38.refs_0_), channel_id=1, source_target_pairs={{0,1},{1,0},{2,3},{3,2},{4,5},{5,4},{6,7},{7,6},{8,9},{9,8},{10,11... | collective-permute-start | bytes 786440 | tf_op jit(solution)/shard_map/ppermute | solution.py:403
  10.7 6.0 %collective-permute-done.2.refs_1_ = bf16[128,1024]{1,0:T(8,128)(2,1)S(1)} collective-permute-done((bf16[128,1024]{1,0:T(8,128)(2,1)S(1)}, bf16[128,1024]{1,0:T(8,128)(2,1)S(1)}, u32[]{:S(2)}, u32[]{:S(2)}) %collective-permute-start.2) | collective-permute-done | bytes 262176 | tf_op jit(solution)/shard_map/ppermute | solution.py:403
  16.7 0.5 shard_map.85
  17.2 5.1 %collective-permute-done.1.refs_1_ = bf16[128,1024]{1,0:T(8,128)(2,1)S(1)} collective-permute-done((bf16[128,1024]{1,0:T(8,128)(2,1)S(1)}, bf16[128,1024]{1,0:T(8,128)(2,1)S(1)}, u32[]{:S(2)}, u32[]{:S(2)}) %collective-permute-start.1) | collective-permute-done | bytes 262176 | tf_op jit(solution)/shard_map/ppermute | solution.py:403
  22.3 0.5 shard_map.86
  23.2 1.2 %collective-permute-start.8 = (bf16[8,136,128]{2,1,0:T(8,128)(2,1)S(1)}, bf16[8,136,128]{2,1,0:T(8,128)(2,1)S(1)}, u32[]{:S(2)}, u32[]{:S(2)}) collective-permute-start(bf16[8,136,128]{2,1,0:T(8,128)(2,1)S(1)} %get-tuple-element.41.refs_1_), channel_id=1, source_target_pairs={{0,4},{2,6},{4,12},{6,14},{8,0},{10,2},{12,20},{14,22},{16,8},{18,... | collective-permute-start | bytes 835592 | tf_op jit(solution)/shard_map/ppermute | solution.py:447
  24.6 1.2 %collective-permute-start.16 = (bf16[8,136,128]{2,1,0:T(8,128)(2,1)S(1)}, bf16[8,136,128]{2,1,0:T(8,128)(2,1)S(1)}, u32[]{:S(2)}, u32[]{:S(2)}) collective-permute-start(bf16[8,136,128]{2,1,0:T(8,128)(2,1)S(1)} %get-tuple-element.42.refs_0_), channel_id=1, source_target_pairs={{0,4},{2,6},{4,12},{6,14},{8,0},{10,2},{12,20},{14,22},{16,8},{18,... | collective-permute-start | bytes 835592 | tf_op jit(solution)/shard_map/ppermute | solution.py:447
  25.8 2.4 %collective-permute-start = (s32[80,4,128]{2,1,0:T(4,128)S(1)}, s32[80,4,128]{2,1,0:T(4,128)S(1)}, u32[]{:S(2)}, u32[]{:S(2)}) collective-permute-start(s32[80,4,128]{2,1,0:T(4,128)S(1)} %bitcast.12), channel_id=1, source_target_pairs={{0,2},{2,0},{4,6},{6,4},{8,10},{10,8},{12,14},{14,12},{16,18},{18,... | collective-permute-start | bytes 491528 | tf_op jit(solution)/shard_map/ppermute | solution.py:422
  28.2 1.0 %collective-permute-done.other_masks = s32[80,4,128]{2,1,0:T(4,128)S(1)} collective-permute-done((s32[80,4,128]{2,1,0:T(4,128)S(1)}, s32[80,4,128]{2,1,0:T(4,128)S(1)}, u32[]{:S(2)}, u32[]{:S(2)}) %collective-permute-start) | collective-permute-done | bytes 163872 | tf_op jit(solution)/shard_map/ppermute | solution.py:422
  29.8 1.5 %shard_map.84 = (s32[1088]{0:T(1024)S(4)}, s32[8]{0:T(128)S(4)}, s32[160,4,128]{2,1,0:T(4,128)S(1)}) custom-call(s32[1]{0:T(128)} %bitcast.core_ref, s32[96]{0:T(128)S(1)} %reshape_squeeze.6.own_ids, s32[96]{0:T(128)S(1)} %reshape_squeeze.7.other_ids, s32[80,4,128]{2,1,0:T(4,128)S(1)} %bitcast.13, s32[80,4,128]{2,1,0:T(4,128)S(1)} %collective-permute-done.other_masks), custom_call_target="tpu_custom_call" | custom-call | flops 1000000 | tf_op jit(solution)/shard_map/pallas_call | solution.py:331
  31.6 1.2 %collective-permute-start.9 = (bf16[8,136,128]{2,1,0:T(8,128)(2,1)S(1)}, bf16[8,136,128]{2,1,0:T(8,128)(2,1)S(1)}, u32[]{:S(2)}, u32[]{:S(2)}) collective-permute-start(bf16[8,136,128]{2,1,0:T(8,128)(2,1)S(1)} %collective-permute-done.8.refs_5_), channel_id=1, source_target_pairs={{0,4},{2,6},{4,12},{6,14},{8,0},{10,2},{12,20},{14,22},{16,8},{18,... | collective-permute-start | bytes 835592 | tf_op jit(solution)/shard_map/ppermute | solution.py:447
  32.8 3.0 %collective-permute-done.12.refs_2_ = bf16[8,136,128]{2,1,0:T(8,128)(2,1)S(1)} collective-permute-done((bf16[8,136,128]{2,1,0:T(8,128)(2,1)S(1)}, bf16[8,136,128]{2,1,0:T(8,128)(2,1)S(1)}, u32[]{:S(2)}, u32[]{:S(2)}) %collective-permute-start.12) | collective-permute-done | bytes 278560 | tf_op jit(solution)/shard_map/ppermute | solution.py:447
  36.1 1.2 %collective-permute-start.17 = (bf16[8,136,128]{2,1,0:T(8,128)(2,1)S(1)}, bf16[8,136,128]{2,1,0:T(8,128)(2,1)S(1)}, u32[]{:S(2)}, u32[]{:S(2)}) collective-permute-start(bf16[8,136,128]{2,1,0:T(8,128)(2,1)S(1)} %collective-permute-done.16.refs_4_), channel_id=1, source_target_pairs={{0,4},{2,6},{4,12},{6,14},{8,0},{10,2},{12,20},{14,22},{16,8},{18,... | collective-permute-start | bytes 835592 | tf_op jit(solution)/shard_map/ppermute | solution.py:447
  37.3 3.1 %shard_map.87.refs_4_ = f32[32,136,128]{2,1,0:T(8,128)S(1)} custom-call(s32[1088]{0:T(1024)S(4)} %get-tuple-element.31.list_ref, s32[8]{0:T(128)S(4)} %get-tuple-element.32.count_ref, s32[160,4,128]{2,1,0:T(4,128)S(1)} %get-tuple-element.33.masks_ref, f32[16,8,128]{2,1,0:T(8,128)S(1)} %get-tuple-element.40.own_sc, ...), custom_call_target="tpu_custom_call" | custom-call | flops 8000000000 | tf_op jit(solution)/shard_map/pallas_call | solution.py:331
  40.4 7.3 %collective-permute-done.13.refs_0_ = bf16[8,136,128]{2,1,0:T(8,128)(2,1)S(1)} collective-permute-done((bf16[8,136,128]{2,1,0:T(8,128)(2,1)S(1)}, bf16[8,136,128]{2,1,0:T(8,128)(2,1)S(1)}, u32[]{:S(2)}, u32[]{:S(2)}) %collective-permute-start.13) | collective-permute-done | bytes 278560 | tf_op jit(solution)/shard_map/ppermute | solution.py:447
  48.0 1.2 %collective-permute-start.18 = (bf16[8,136,128]{2,1,0:T(8,128)(2,1)S(1)}, bf16[8,136,128]{2,1,0:T(8,128)(2,1)S(1)}, u32[]{:S(2)}, u32[]{:S(2)}) collective-permute-start(bf16[8,136,128]{2,1,0:T(8,128)(2,1)S(1)} %collective-permute-done.17.refs_2_), channel_id=1, source_target_pairs={{0,4},{2,6},{4,12},{6,14},{8,0},{10,2},{12,20},{14,22},{16,8},{18,... | collective-permute-start | bytes 835592 | tf_op jit(solution)/shard_map/ppermute | solution.py:447
  49.2 1.2 %collective-permute-start.10 = (bf16[8,136,128]{2,1,0:T(8,128)(2,1)S(1)}, bf16[8,136,128]{2,1,0:T(8,128)(2,1)S(1)}, u32[]{:S(2)}, u32[]{:S(2)}) collective-permute-start(bf16[8,136,128]{2,1,0:T(8,128)(2,1)S(1)} %collective-permute-done.9.refs_3_), channel_id=1, source_target_pairs={{0,4},{2,6},{4,12},{6,14},{8,0},{10,2},{12,20},{14,22},{16,8},{18,... | collective-permute-start | bytes 835592 | tf_op jit(solution)/shard_map/ppermute | solution.py:447
  50.7 2.0 %shard_map.88.refs_2_ = f32[32,136,128]{2,1,0:T(8,128)S(1)} custom-call(s32[1088]{0:T(1024)S(4)} %get-tuple-element.31.list_ref, s32[8]{0:T(128)S(4)} %get-tuple-element.32.count_ref, s32[160,4,128]{2,1,0:T(4,128)S(1)} %get-tuple-element.33.masks_ref, f32[16,8,128]{2,1,0:T(8,128)S(1)} %get-tuple-element.40.own_sc, ...), custom_call_target="tpu_custom_call", output_to_operand_aliasing={{}: (10, {})} | custom-call | flops 8000000000 | tf_op jit(solution)/shard_map/pallas_call | solution.py:331
  52.7 1.1 %collective-permute-done.14.refs_0_ = bf16[8,136,128]{2,1,0:T(8,128)(2,1)S(1)} collective-permute-done((bf16[8,136,128]{2,1,0:T(8,128)(2,1)S(1)}, bf16[8,136,128]{2,1,0:T(8,128)(2,1)S(1)}, u32[]{:S(2)}, u32[]{:S(2)}) %collective-permute-start.14) | collective-permute-done | bytes 278560 | tf_op jit(solution)/shard_map/ppermute | solution.py:447
  54.2 1.2 %collective-permute-start.19 = (bf16[4,136,128]{2,1,0:T(8,128)(2,1)S(1)}, bf16[4,136,128]{2,1,0:T(8,128)(2,1)S(1)}, u32[]{:S(2)}, u32[]{:S(2)}) collective-permute-start(bf16[4,136,128]{2,1,0:T(8,128)(2,1)S(1)} %slice.29), channel_id=1, source_target_pairs={{0,4},{2,6},{4,12},{6,14},{8,0},{10,2},{12,20},{14,22},{16,8},{18,... | collective-permute-start | bytes 417800 | tf_op jit(solution)/shard_map/ppermute | solution.py:456
  55.5 4.4 %collective-permute-done.10.refs_1_ = bf16[8,136,128]{2,1,0:T(8,128)(2,1)S(1)} collective-permute-done((bf16[8,136,128]{2,1,0:T(8,128)(2,1)S(1)}, bf16[8,136,128]{2,1,0:T(8,128)(2,1)S(1)}, u32[]{:S(2)}, u32[]{:S(2)}) %collective-permute-start.10) | collective-permute-done | bytes 278560 | tf_op jit(solution)/shard_map/ppermute | solution.py:447
  59.8 1.2 %collective-permute-start.11 = (bf16[4,136,128]{2,1,0:T(8,128)(2,1)S(1)}, bf16[4,136,128]{2,1,0:T(8,128)(2,1)S(1)}, u32[]{:S(2)}, u32[]{:S(2)}) collective-permute-start(bf16[4,136,128]{2,1,0:T(8,128)(2,1)S(1)} %slice.27), channel_id=1, source_target_pairs={{0,4},{2,6},{4,12},{6,14},{8,0},{10,2},{12,20},{14,22},{16,8},{18,... | collective-permute-start | bytes 417800 | tf_op jit(solution)/shard_map/ppermute | solution.py:456
  61.4 2.0 %shard_map.89.refs_2_ = f32[32,136,128]{2,1,0:T(8,128)S(1)} custom-call(s32[1088]{0:T(1024)S(4)} %get-tuple-element.31.list_ref, s32[8]{0:T(128)S(4)} %get-tuple-element.32.count_ref, s32[160,4,128]{2,1,0:T(4,128)S(1)} %get-tuple-element.33.masks_ref, f32[16,8,128]{2,1,0:T(8,128)S(1)} %get-tuple-element.40.own_sc, ...), custom_call_target="tpu_custom_call", output_to_operand_aliasing={{}: (8, {})} | custom-call | flops 8000000000 | tf_op jit(solution)/shard_map/pallas_call | solution.py:331
  63.4 1.1 %shard_map.90.refs_2_ = f32[32,136,128]{2,1,0:T(8,128)S(1)} custom-call(s32[1088]{0:T(1024)S(4)} %get-tuple-element.31.list_ref, s32[8]{0:T(128)S(4)} %get-tuple-element.32.count_ref, s32[160,4,128]{2,1,0:T(4,128)S(1)} %get-tuple-element.33.masks_ref, f32[16,8,128]{2,1,0:T(8,128)S(1)} %get-tuple-element.40.own_sc, ...), custom_call_target="tpu_custom_call", output_to_operand_aliasing={{}: (8, {})} | custom-call | flops 8000000000 | tf_op jit(solution)/shard_map/pallas_call | solution.py:331
  64.6 1.7 %shard_map.91.refs_2_ = f32[32,136,128]{2,1,0:T(8,128)S(1)} custom-call(s32[1088]{0:T(1024)S(4)} %get-tuple-element.31.list_ref, s32[8]{0:T(128)S(4)} %get-tuple-element.32.count_ref, s32[160,4,128]{2,1,0:T(4,128)S(1)} %get-tuple-element.33.masks_ref, f32[16,8,128]{2,1,0:T(8,128)S(1)} %get-tuple-element.40.own_sc, ...), custom_call_target="tpu_custom_call", output_to_operand_aliasing={{}: (8, {})} | custom-call | flops 8000000000 | tf_op jit(solution)/shard_map/pallas_call | solution.py:331
  66.3 0.6 collective-permute-done.7.refs_0_
  67.0 9.0 %collective-permute-start.20 = (f32[16,136,128]{2,1,0:T(8,128)S(1)}, f32[16,136,128]{2,1,0:T(8,128)S(1)}, u32[]{:S(2)}, u32[]{:S(2)}) collective-permute-start(f32[16,136,128]{2,1,0:T(8,128)S(1)} %get-tuple-element.50), channel_id=1, source_target_pairs={{0,2},{2,0},{4,6},{6,4},{8,10},{10,8},{12,14},{14,12},{16,18},{18,... | collective-permute-start | bytes 3342344 | tf_op jit(solution)/shard_map/ppermute | solution.py:509
  76.2 2.3 %collective-permute-done.20.other_ref = f32[16,136,128]{2,1,0:T(8,128)S(1)} collective-permute-done((f32[16,136,128]{2,1,0:T(8,128)S(1)}, f32[16,136,128]{2,1,0:T(8,128)S(1)}, u32[]{:S(2)}, u32[]{:S(2)}) %collective-permute-start.20) | collective-permute-done | bytes 1114144 | tf_op jit(solution)/shard_map/ppermute | solution.py:509
  78.4 1.3 %shard_map.94 = bf16[128,2048]{1,0:T(8,128)(2,1)} custom-call(f32[32,136,128]{2,1,0:T(8,128)S(1)} %shard_map.93.state_ref, f32[16,136,128]{2,1,0:T(8,128)S(1)} %collective-permute-done.20.other_ref, bf16[128,2048]{1,0:T(8,128)(2,1)S(1)} %copy-done, f32[1,128]{1,0:T(1,128)S(1)} %bitcast.15), custom_call_target="tpu_custom_call" | custom-call | flops 1000000 | tf_op jit(solution)/shard_map/pallas_call | solution.py:331
  (37 shorter events, 3.6 us)
Async XLA Ops:
  2.7 23.1 %all-to-all-start = ((s32[16,5,4,128]{3,2,1,0:T(4,128)}), s32[16,5,4,128]{3,2,1,0:T(4,128)S(1)}, u32[]{:S(2)}, u32[]{:S(2)}) async-start(s32[16,5,4,128]{3,2,1,0:T(4,128)} %shard_map.83), calls=%async_computation | async-start | bytes 327680 | tf_op jit(solution)/shard_map/all_to_all | solution.py:420
  9.2 7.5 %collective-permute-start.2 = (bf16[128,1024]{1,0:T(8,128)(2,1)S(1)}, bf16[128,1024]{1,0:T(8,128)(2,1)S(1)}, u32[]{:S(2)}, u32[]{:S(2)}) collective-permute-start(bf16[128,1024]{1,0:T(8,128)(2,1)S(1)} %get-tuple-element.38.refs_0_), channel_id=1, source_target_pairs={{0,1},{1,0},{2,3},{3,2},{4,5},{5,4},{6,7},{7,6},{8,9},{9,8},{10,11... | collective-permute-start | bytes 786440 | tf_op jit(solution)/shard_map/ppermute | solution.py:403
  10.4 11.8 %collective-permute-start.1 = (bf16[128,1024]{1,0:T(8,128)(2,1)S(1)}, bf16[128,1024]{1,0:T(8,128)(2,1)S(1)}, u32[]{:S(2)}, u32[]{:S(2)}) collective-permute-start(bf16[128,1024]{1,0:T(8,128)(2,1)S(1)} %get-tuple-element.37.refs_0_), channel_id=1, source_target_pairs={{0,1},{1,0},{2,3},{3,2},{4,5},{5,4},{6,7},{7,6},{8,9},{9,8},{10,11... | collective-permute-start | bytes 786440 | tf_op jit(solution)/shard_map/ppermute | solution.py:403
  22.8 8.5 %collective-permute-start.4 = (bf16[8,136,128]{2,1,0:T(8,128)(2,1)S(1)}, bf16[8,136,128]{2,1,0:T(8,128)(2,1)S(1)}, u32[]{:S(2)}, u32[]{:S(2)}) collective-permute-start(bf16[8,136,128]{2,1,0:T(8,128)(2,1)S(1)} %get-tuple-element.41.refs_1_), channel_id=1, source_target_pairs={{0,8},{2,10},{4,0},{6,2},{8,16},{10,18},{12,4},{14,6},{16,24},{18,... | collective-permute-start | bytes 835592 | tf_op jit(solution)/shard_map/ppermute | solution.py:447
  23.2 8.4 %collective-permute-start.8 = (bf16[8,136,128]{2,1,0:T(8,128)(2,1)S(1)}, bf16[8,136,128]{2,1,0:T(8,128)(2,1)S(1)}, u32[]{:S(2)}, u32[]{:S(2)}) collective-permute-start(bf16[8,136,128]{2,1,0:T(8,128)(2,1)S(1)} %get-tuple-element.41.refs_1_), channel_id=1, source_target_pairs={{0,4},{2,6},{4,12},{6,14},{8,0},{10,2},{12,20},{14,22},{16,8},{18,... | collective-permute-start | bytes 835592 | tf_op jit(solution)/shard_map/ppermute | solution.py:447
  24.3 11.5 %collective-permute-start.12 = (bf16[8,136,128]{2,1,0:T(8,128)(2,1)S(1)}, bf16[8,136,128]{2,1,0:T(8,128)(2,1)S(1)}, u32[]{:S(2)}, u32[]{:S(2)}) collective-permute-start(bf16[8,136,128]{2,1,0:T(8,128)(2,1)S(1)} %get-tuple-element.42.refs_0_), channel_id=1, source_target_pairs={{0,8},{2,10},{4,0},{6,2},{8,16},{10,18},{12,4},{14,6},{16,24},{18,... | collective-permute-start | bytes 835592 | tf_op jit(solution)/shard_map/ppermute | solution.py:447
  24.6 11.5 %collective-permute-start.16 = (bf16[8,136,128]{2,1,0:T(8,128)(2,1)S(1)}, bf16[8,136,128]{2,1,0:T(8,128)(2,1)S(1)}, u32[]{:S(2)}, u32[]{:S(2)}) collective-permute-start(bf16[8,136,128]{2,1,0:T(8,128)(2,1)S(1)} %get-tuple-element.42.refs_0_), channel_id=1, source_target_pairs={{0,4},{2,6},{4,12},{6,14},{8,0},{10,2},{12,20},{14,22},{16,8},{18,... | collective-permute-start | bytes 835592 | tf_op jit(solution)/shard_map/ppermute | solution.py:447
  25.8 3.4 %collective-permute-start = (s32[80,4,128]{2,1,0:T(4,128)S(1)}, s32[80,4,128]{2,1,0:T(4,128)S(1)}, u32[]{:S(2)}, u32[]{:S(2)}) collective-permute-start(s32[80,4,128]{2,1,0:T(4,128)S(1)} %bitcast.12), channel_id=1, source_target_pairs={{0,2},{2,0},{4,6},{6,4},{8,10},{10,8},{12,14},{14,12},{16,18},{18,... | collective-permute-start | bytes 491528 | tf_op jit(solution)/shard_map/ppermute | solution.py:422
  29.2 8.1 %collective-permute-start.3 = (f32[16,8,128]{2,1,0:T(8,128)S(1)}, f32[16,8,128]{2,1,0:T(8,128)S(1)}, u32[]{:S(2)}, u32[]{:S(2)}) collective-permute-start(f32[16,8,128]{2,1,0:T(8,128)S(1)} %get-tuple-element.40.own_sc), channel_id=1, source_target_pairs={{0,2},{2,0},{4,6},{6,4},{8,10},{10,8},{12,14},{14,12},{16,18},{18,... | collective-permute-start | bytes 196616 | tf_op jit(solution)/shard_map/ppermute | solution.py:441
  31.3 19.1 %collective-permute-start.5 = (bf16[8,136,128]{2,1,0:T(8,128)(2,1)S(1)}, bf16[8,136,128]{2,1,0:T(8,128)(2,1)S(1)}, u32[]{:S(2)}, u32[]{:S(2)}) collective-permute-start(bf16[8,136,128]{2,1,0:T(8,128)(2,1)S(1)} %collective-permute-done.4.refs_3_), channel_id=1, source_target_pairs={{0,8},{2,10},{4,0},{6,2},{8,16},{10,18},{12,4},{14,6},{16,24},{18,... | collective-permute-start | bytes 835592 | tf_op jit(solution)/shard_map/ppermute | solution.py:447
  31.6 17.6 %collective-permute-start.9 = (bf16[8,136,128]{2,1,0:T(8,128)(2,1)S(1)}, bf16[8,136,128]{2,1,0:T(8,128)(2,1)S(1)}, u32[]{:S(2)}, u32[]{:S(2)}) collective-permute-start(bf16[8,136,128]{2,1,0:T(8,128)(2,1)S(1)} %collective-permute-done.8.refs_5_), channel_id=1, source_target_pairs={{0,4},{2,6},{4,12},{6,14},{8,0},{10,2},{12,20},{14,22},{16,8},{18,... | collective-permute-start | bytes 835592 | tf_op jit(solution)/shard_map/ppermute | solution.py:447
  35.8 11.9 %collective-permute-start.13 = (bf16[8,136,128]{2,1,0:T(8,128)(2,1)S(1)}, bf16[8,136,128]{2,1,0:T(8,128)(2,1)S(1)}, u32[]{:S(2)}, u32[]{:S(2)}) collective-permute-start(bf16[8,136,128]{2,1,0:T(8,128)(2,1)S(1)} %collective-permute-done.12.refs_2_), channel_id=1, source_target_pairs={{0,8},{2,10},{4,0},{6,2},{8,16},{10,18},{12,4},{14,6},{16,24},{18,... | collective-permute-start | bytes 835592 | tf_op jit(solution)/shard_map/ppermute | solution.py:447
  36.1 11.9 %collective-permute-start.17 = (bf16[8,136,128]{2,1,0:T(8,128)(2,1)S(1)}, bf16[8,136,128]{2,1,0:T(8,128)(2,1)S(1)}, u32[]{:S(2)}, u32[]{:S(2)}) collective-permute-start(bf16[8,136,128]{2,1,0:T(8,128)(2,1)S(1)} %collective-permute-done.16.refs_4_), channel_id=1, source_target_pairs={{0,4},{2,6},{4,12},{6,14},{8,0},{10,2},{12,20},{14,22},{16,8},{18,... | collective-permute-start | bytes 835592 | tf_op jit(solution)/shard_map/ppermute | solution.py:447
  47.7 6.1 %collective-permute-start.14 = (bf16[8,136,128]{2,1,0:T(8,128)(2,1)S(1)}, bf16[8,136,128]{2,1,0:T(8,128)(2,1)S(1)}, u32[]{:S(2)}, u32[]{:S(2)}) collective-permute-start(bf16[8,136,128]{2,1,0:T(8,128)(2,1)S(1)} %collective-permute-done.13.refs_0_), channel_id=1, source_target_pairs={{0,8},{2,10},{4,0},{6,2},{8,16},{10,18},{12,4},{14,6},{16,24},{18,... | collective-permute-start | bytes 835592 | tf_op jit(solution)/shard_map/ppermute | solution.py:447
  48.0 6.2 %collective-permute-start.18 = (bf16[8,136,128]{2,1,0:T(8,128)(2,1)S(1)}, bf16[8,136,128]{2,1,0:T(8,128)(2,1)S(1)}, u32[]{:S(2)}, u32[]{:S(2)}) collective-permute-start(bf16[8,136,128]{2,1,0:T(8,128)(2,1)S(1)} %collective-permute-done.17.refs_2_), channel_id=1, source_target_pairs={{0,4},{2,6},{4,12},{6,14},{8,0},{10,2},{12,20},{14,22},{16,8},{18,... | collective-permute-start | bytes 835592 | tf_op jit(solution)/shard_map/ppermute | solution.py:447
  49.2 10.6 %collective-permute-start.10 = (bf16[8,136,128]{2,1,0:T(8,128)(2,1)S(1)}, bf16[8,136,128]{2,1,0:T(8,128)(2,1)S(1)}, u32[]{:S(2)}, u32[]{:S(2)}) collective-permute-start(bf16[8,136,128]{2,1,0:T(8,128)(2,1)S(1)} %collective-permute-done.9.refs_3_), channel_id=1, source_target_pairs={{0,4},{2,6},{4,12},{6,14},{8,0},{10,2},{12,20},{14,22},{16,8},{18,... | collective-permute-start | bytes 835592 | tf_op jit(solution)/shard_map/ppermute | solution.py:447
  50.4 10.7 %collective-permute-start.6 = (bf16[8,136,128]{2,1,0:T(8,128)(2,1)S(1)}, bf16[8,136,128]{2,1,0:T(8,128)(2,1)S(1)}, u32[]{:S(2)}, u32[]{:S(2)}) collective-permute-start(bf16[8,136,128]{2,1,0:T(8,128)(2,1)S(1)} %collective-permute-done.5.refs_1_), channel_id=1, source_target_pairs={{0,8},{2,10},{4,0},{6,2},{8,16},{10,18},{12,4},{14,6},{16,24},{18,... | collective-permute-start | bytes 835592 | tf_op jit(solution)/shard_map/ppermute | solution.py:447
  53.9 10.7 %collective-permute-start.15 = (bf16[4,136,128]{2,1,0:T(8,128)(2,1)S(1)}, bf16[4,136,128]{2,1,0:T(8,128)(2,1)S(1)}, u32[]{:S(2)}, u32[]{:S(2)}) collective-permute-start(bf16[4,136,128]{2,1,0:T(8,128)(2,1)S(1)} %slice.28), channel_id=1, source_target_pairs={{0,8},{2,10},{4,0},{6,2},{8,16},{10,18},{12,4},{14,6},{16,24},{18,... | collective-permute-start | bytes 417800 | tf_op jit(solution)/shard_map/ppermute | solution.py:456
  54.2 10.3 %collective-permute-start.19 = (bf16[4,136,128]{2,1,0:T(8,128)(2,1)S(1)}, bf16[4,136,128]{2,1,0:T(8,128)(2,1)S(1)}, u32[]{:S(2)}, u32[]{:S(2)}) collective-permute-start(bf16[4,136,128]{2,1,0:T(8,128)(2,1)S(1)} %slice.29), channel_id=1, source_target_pairs={{0,4},{2,6},{4,12},{6,14},{8,0},{10,2},{12,20},{14,22},{16,8},{18,... | collective-permute-start | bytes 417800 | tf_op jit(solution)/shard_map/ppermute | solution.py:456
  59.8 6.4 %collective-permute-start.11 = (bf16[4,136,128]{2,1,0:T(8,128)(2,1)S(1)}, bf16[4,136,128]{2,1,0:T(8,128)(2,1)S(1)}, u32[]{:S(2)}, u32[]{:S(2)}) collective-permute-start(bf16[4,136,128]{2,1,0:T(8,128)(2,1)S(1)} %slice.27), channel_id=1, source_target_pairs={{0,4},{2,6},{4,12},{6,14},{8,0},{10,2},{12,20},{14,22},{16,8},{18,... | collective-permute-start | bytes 417800 | tf_op jit(solution)/shard_map/ppermute | solution.py:456
  61.1 5.7 %collective-permute-start.7 = (bf16[4,136,128]{2,1,0:T(8,128)(2,1)S(1)}, bf16[4,136,128]{2,1,0:T(8,128)(2,1)S(1)}, u32[]{:S(2)}, u32[]{:S(2)}) collective-permute-start(bf16[4,136,128]{2,1,0:T(8,128)(2,1)S(1)} %slice.26), channel_id=1, source_target_pairs={{0,8},{2,10},{4,0},{6,2},{8,16},{10,18},{12,4},{14,6},{16,24},{18,... | collective-permute-start | bytes 417800 | tf_op jit(solution)/shard_map/ppermute | solution.py:456
  67.0 11.4 %collective-permute-start.20 = (f32[16,136,128]{2,1,0:T(8,128)S(1)}, f32[16,136,128]{2,1,0:T(8,128)S(1)}, u32[]{:S(2)}, u32[]{:S(2)}) collective-permute-start(f32[16,136,128]{2,1,0:T(8,128)S(1)} %get-tuple-element.50), channel_id=1, source_target_pairs={{0,2},{2,0},{4,6},{6,4},{8,10},{10,8},{12,14},{14,12},{16,18},{18,... | collective-permute-start | bytes 3342344 | tf_op jit(solution)/shard_map/ppermute | solution.py:509
  76.1 2.4 %copy-start = (bf16[128,2048]{1,0:T(8,128)(2,1)S(1)}, bf16[128,2048]{1,0:T(8,128)(2,1)}, u32[]{:S(2)}) copy-start(bf16[128,2048]{1,0:T(8,128)(2,1)} %x_ref.1) | copy-start | bytes 1572868
  76.1 2.4 %copy-start.1 = (f32[128]{0:T(128)S(1)}, f32[128]{0:T(128)}, u32[]{:S(2)}) copy-start(f32[128]{0:T(128)} %param.12) | copy-start | bytes 1540

commit v3 on v2

--- a/solution.py
+++ b/solution.py
@@ -101,9 +101,11 @@
         copy.wait()
 
 
-def pack_kernel(blocks, place, groups, rows_ref, cols_ref, masks_ref, out_ref, count, place_ref, codes):
+def pack_kernel(blocks, place, groups, mp_ref, rows_ref, cols_ref, masks_ref, out_ref, count, place_ref, codes):
     devices, slots = out_ref.shape[0], out_ref.shape[1] - 1
     words = out_ref.shape[2:]
+    whole = masks_ref.shape[1]
+    low = mp_ref[0] == 0
     half = blocks // 2
     chips = len(place)
     width = slots + 2
@@ -123,7 +125,8 @@
         have = count[2 * owner + odd]
         count[2 * owner + odd] = have + 1
         at = jnp.where(odd == 1, slots - 1 - have, have)
-        out_ref[owner, at] = masks_ref[t]
+        mask = masks_ref[t]
+        out_ref[owner, at] = mask if words[0] == whole else jnp.where(low, mask[: words[0]], mask[words[0] :])
         back = place_ref[owner >> 1] - place_ref[holder >> 1]
         back = jnp.where(back < 0, back + chips, back)
         step = jnp.minimum(back, chips - back)
@@ -147,14 +150,27 @@
         out_ref[d, slots] = here
 
 
-def list_kernel(devices, slots, groups, blocks, final, core_ref, own_ids, other_ids, own_masks, other_masks, list_ref, count_ref, masks_ref):
+def mix_kernel(mp_ref, *refs):
+    *parts, masks_ref = refs
+    width = masks_ref.shape[0] // 2
+    low = mp_ref[0] == 0
+    for side in range(2):
+        at = slice(side * width, (side + 1) * width)
+        if len(parts) == 2:
+            masks_ref[at] = parts[side][...]
+        else:
+            here, peer = parts[2 * side][...], parts[2 * side + 1][...]
+            masks_ref[at, : here.shape[1]] = jnp.where(low, here, peer)
+            masks_ref[at, here.shape[1] :] = jnp.where(low, peer, here)
+
+
+def list_kernel(devices, slots, groups, blocks, final, core_ref, own_ids, other_ids, list_ref, count_ref):
     total = list_ref.shape[0] // groups
     width = devices * (slots + 1)
     core = core_ref[0]
     for g in range(groups):
         count_ref[g] = 0
-    for side, (ids, masks) in enumerate(((own_ids, own_masks), (other_ids, other_masks))):
-        masks_ref[side * width : (side + 1) * width] = masks[...]
+    for side, ids in enumerate((own_ids, other_ids)):
         turn = 0 if side else 1
 
         def holder(d, carry, side=side, ids=ids, turn=turn):
@@ -408,9 +424,9 @@
 
     packed = call(
         functools.partial(pack_kernel, blocks, place, groups),
-        pltpu.HBM((n_dp, slots + 1, words, tile), jnp.int32),
-        [held(near_rows), held(near_cols), near(near_masks)],
-        in_specs=[SMEM, SMEM, VMEM],
+        pltpu.HBM((n_dp, slots + 1, words // parts, tile), jnp.int32),
+        [mine, held(near_rows), held(near_cols), near(near_masks)],
+        in_specs=[SMEM, SMEM, SMEM, VMEM],
         scratch=[
             pltpu.SMEM((2 * n_dp,), jnp.int32),
             pltpu.SMEM((chips,), jnp.int32),
@@ -418,8 +434,10 @@
         ],
     )
     got = lax.all_to_all(packed, "dp", split_axis=0, concat_axis=0, tiled=True)
-    got = got.reshape(n_dp * (slots + 1), words, tile)
-    got_other = lax.ppermute(got, "dp", swap)
+    got = [got.reshape(n_dp * (slots + 1), words // parts, tile)]
+    if parts == 2:
+        got.append(lax.ppermute(got[0], "mp", flip))
+    got_other = [lax.ppermute(v, "dp", swap) for v in got]
 
     pays, own_sc = [], None
     for k, xs in enumerate(inputs):
@@ -458,17 +476,22 @@
 
     width = n_dp * (slots + 1)
     total = 2 * n_dp * slots + 4 * WIDE
-    ids = [v.reshape(n_dp, slots + 1, words, tile)[:, slots, 0, : slots + 2] for v in (got, got_other)]
-    lists, counts, masks = call(
+    ids = [v.reshape(n_dp, slots + 1, words // parts, tile)[:, slots, 0, : slots + 2] for v in (got[0], got_other[0])]
+    lists, counts = call(
         functools.partial(list_kernel, n_dp, slots, groups, blocks, steps + 1),
         (
             pltpu.SMEM((groups * total,), jnp.int32),
             pltpu.SMEM((groups,), jnp.int32),
-            pltpu.VMEM((2 * width, words, tile), jnp.int32),
         ),
-        (core, *[v.reshape(n_dp * (slots + 2)) for v in ids], near(got), near(got_other)),
-        in_specs=[SMEM] * 3 + [VMEM] * 2,
-        out_specs=(SMEM, SMEM, VMEM),
+        (core, *[v.reshape(n_dp * (slots + 2)) for v in ids]),
+        in_specs=[SMEM] * 3,
+        out_specs=(SMEM, SMEM),
+    )
+    masks = call(
+        mix_kernel,
+        pltpu.VMEM((2 * width, words, tile), jnp.int32),
+        (mine, *[near(v) for v in got + got_other]),
+        in_specs=[SMEM] + [VMEM] * (2 * parts),
     )
 
     shared = [masks, own_sc, other_sc, att[0]]

time: 80.1 us -> 76.6 us (0.956)
  blocking collectives: 0 us -> 11.5 us
  waiting for transfers between devices: 30.8 us -> 21.2 us
  starting transfers between devices: 31.8 us -> 26.2 us
    all_to_all x0 -> x1, blocking collectives: none -> 11.5 us  [local(): got = lax.all_to_all(packed, 'dp', split_axis=0, concat_axis=0, tiled=True)]
    ppermute x2, waiting for transfers between devices: 11.1 us -> 0.01 us  [local(): inputs = [[x, lax.ppermute(x, 'mp', flip)] for x in cuts]]
    all_to_all x1 -> x0, starting transfers between devices: 6.52 us -> none  [local(): got = lax.all_to_all(packed, 'dp', split_axis=0, concat_axis=0, tiled=True)]
    ppermute x12, waiting for transfers between devices: 15.9 us -> 17 us  [local(): lax.ppermute(going[way], 'dp', right if way[0] == 'r' else left)]
    ppermute x1 -> x3, starting transfers between devices: 2.37 us -> 3.35 us  [the longest x2 2.11 us: local(): got_other = [lax.ppermute(v, 'dp', swap) for v in got]]
    ppermute x1 -> x3, waiting for transfers between devices: 1.03 us -> 1.85 us  [the longest x2 1.85 us: local(): got_other = [lax.ppermute(v, 'dp', swap) for v in got]]
    pallas_call x13 -> x14, Pallas kernels: 16.7 us -> 16.7 us  [call(): pl.pallas_call(kernel, out_shape=outs, in_specs=in_specs or [VMEM] * len(...]
  transfers between devices with their start and end apart: 22 -> 23, of which waited for: 9 -> 7; matrix products, arithmetic and copies ran while one was open for 0% -> 0% of each run, Pallas kernels for 16% -> 19%
where the time goes in v3:
time: 76.6 us; the launch traced here: 76 us
  starting transfers between devices  26.2 us (34%)
  waiting for transfers between devices  21.2 us (28%)
  Pallas kernels  16.7 us (22%)
  blocking collectives  11.5 us (15%)
    ppermute x12, waiting for transfers between devices, local(): lax.ppermute(going[way], 'dp', right if way[0] == 'r' else left)  17 us
    pallas_call x14, Pallas kernels, call(): pl.pallas_call(kernel, out_shape=outs, in_specs=in_specs or [VMEM] * len(...  16.7 us
    all_to_all x1, blocking collectives, local(): got = lax.all_to_all(packed, 'dp', split_axis=0, concat_axis=0, tiled=True)  11.5 us
    ppermute x1, starting transfers between devices, local(): back = lax.ppermute(other, 'dp', swap)  8.93 us
    ppermute x12, starting transfers between devices, local(): lax.ppermute(going[way], 'dp', right if way[0] == 'r' else left)  8.9 us
    ppermute x4, starting transfers between devices, local(): both.append(lax.ppermute(going[w + p][cut], 'dp', pairs))  3.14 us
    ppermute x1, waiting for transfers between devices, local(): back = lax.ppermute(other, 'dp', swap)  2.27 us
    ppermute x2, starting transfers between devices, local(): got_other = [lax.ppermute(v, 'dp', swap) for v in got]  2.11 us
  transfers between devices with their start and end apart: 23, of which 7 were waited for; matrix products, arithmetic and copies ran while one was open for 0% of the time, Pallas kernels for 19%

profile of v3, /device:TPU:11, one launch (start us, length us, event | category | flops | bytes accessed | tf_op | source)
XLA Modules:
  0.0 76.0 jit_solution(7328778092919632582)
XLA Ops:
  0.0 1.1 %shard_map.82 = (bf16[128,1024]{1,0:T(8,128)(2,1)S(1)}, bf16[128,1024]{1,0:T(8,128)(2,1)S(1)}, bf16[128,256]{1,0:T(8,128)(2,1)S(1)}, f32[1,128]{1,0:T(1,128)S(1)...) custom-call(bf16[128,2048]{1,0:T(8,128)(2,1)} %x_ref.1, ...), custom_call_target="tpu_custom_call" | custom-call | flops 1000000 | tf_op jit(solution)/shard_map/pallas_call | solution.py:347
  1.1 1.3 %collective-permute-start.4 = (bf16[128,1024]{1,0:T(8,128)(2,1)S(1)}, bf16[128,1024]{1,0:T(8,128)(2,1)S(1)}, u32[]{:S(2)}, u32[]{:S(2)}) collective-permute-start(bf16[128,1024]{1,0:T(8,128)(2,1)S(1)} %get-tuple-element.36.refs_0_), channel_id=1, source_target_pairs={{0,1},{1,0},{2,3},{3,2},{4,5},{5,4},{6,7},{7,6},{8,9},{9,8},{10,11... | collective-permute-start | bytes 786440 | tf_op jit(solution)/shard_map/ppermute | solution.py:419
  2.7 1.4 %shard_map.83 = s32[16,5,2,128]{3,2,1,0:T(2,128)} custom-call(s32[1]{0:T(128)} %bitcast.1.mp_ref, s32[32]{0:T(128)S(4)} %get-tuple-element.27.rows_ref, s32[32]{0:T(128)S(4)} %get-tuple-element.28.cols_ref, s32[32,4,128]{2,1,0:T(4,128)S(1)} %get-tuple-element.29.masks_ref), custom_call_target="tpu_custom_call" | custom-call | flops 1000000 | tf_op jit(solution)/shard_map/pallas_call | solution.py:347
  4.1 11.5 %all_to_all.5 = s32[16,5,2,128]{3,2,1,0:T(2,128)S(1)} all-to-all(s32[16,5,2,128]{3,2,1,0:T(2,128)} %shard_map.83), channel_id=1, replica_groups=mesh['dp'=16,'mp'=2] {'dp'}, dimensions={0} | all-to-all | bytes 163840 | tf_op jit(solution)/shard_map/all_to_all | solution.py:436
  15.6 1.2 %collective-permute-start.1 = (s32[80,2,128]{2,1,0:T(2,128)S(1)}, s32[80,2,128]{2,1,0:T(2,128)S(1)}, u32[]{:S(2)}, u32[]{:S(2)}) collective-permute-start(s32[80,2,128]{2,1,0:T(2,128)S(1)} %bitcast.12), channel_id=1, source_target_pairs={{0,1},{1,0},{2,3},{3,2},{4,5},{5,4},{6,7},{7,6},{8,9},{9,8},{10,11... | collective-permute-start | bytes 245768 | tf_op jit(solution)/shard_map/ppermute | solution.py:439
  17.9 0.7 collective-permute-start.10
  18.6 0.8 %collective-permute-start.6 = (bf16[8,136,128]{2,1,0:T(8,128)(2,1)S(1)}, bf16[8,136,128]{2,1,0:T(8,128)(2,1)S(1)}, u32[]{:S(2)}, u32[]{:S(2)}) collective-permute-start(bf16[8,136,128]{2,1,0:T(8,128)(2,1)S(1)} %get-tuple-element.39.refs_1_), channel_id=1, source_target_pairs={{0,8},{2,10},{4,0},{6,2},{8,16},{10,18},{12,4},{14,6},{16,24},{18,... | collective-permute-start | bytes 835592 | tf_op jit(solution)/shard_map/ppermute | solution.py:465
  19.4 1.1 %collective-permute-start.14 = (bf16[8,136,128]{2,1,0:T(8,128)(2,1)S(1)}, bf16[8,136,128]{2,1,0:T(8,128)(2,1)S(1)}, u32[]{:S(2)}, u32[]{:S(2)}) collective-permute-start(bf16[8,136,128]{2,1,0:T(8,128)(2,1)S(1)} %get-tuple-element.40.refs_0_), channel_id=1, source_target_pairs={{0,8},{2,10},{4,0},{6,2},{8,16},{10,18},{12,4},{14,6},{16,24},{18,... | collective-permute-start | bytes 835592 | tf_op jit(solution)/shard_map/ppermute | solution.py:465
  20.9 1.8 %collective-permute-start = (s32[80,2,128]{2,1,0:T(2,128)S(1)}, s32[80,2,128]{2,1,0:T(2,128)S(1)}, u32[]{:S(2)}, u32[]{:S(2)}) collective-permute-start(s32[80,2,128]{2,1,0:T(2,128)S(1)} %bitcast.13), channel_id=1, source_target_pairs={{0,2},{2,0},{4,6},{6,4},{8,10},{10,8},{12,14},{14,12},{16,18},{18,... | collective-permute-start | bytes 245768 | tf_op jit(solution)/shard_map/ppermute | solution.py:440
  22.6 0.9 %collective-permute-done.refs_2_ = s32[80,2,128]{2,1,0:T(2,128)S(1)} collective-permute-done((s32[80,2,128]{2,1,0:T(2,128)S(1)}, s32[80,2,128]{2,1,0:T(2,128)S(1)}, u32[]{:S(2)}, u32[]{:S(2)}) %collective-permute-start) | collective-permute-done | bytes 81952 | tf_op jit(solution)/shard_map/ppermute | solution.py:440
  23.9 0.9 %collective-permute-done.2.refs_3_ = s32[80,2,128]{2,1,0:T(2,128)S(1)} collective-permute-done((s32[80,2,128]{2,1,0:T(2,128)S(1)}, s32[80,2,128]{2,1,0:T(2,128)S(1)}, u32[]{:S(2)}, u32[]{:S(2)}) %collective-permute-start.2) | collective-permute-done | bytes 81952 | tf_op jit(solution)/shard_map/ppermute | solution.py:440
  25.4 1.5 %shard_map.84 = (s32[1088]{0:T(1024)S(4)}, s32[8]{0:T(128)S(4)}) custom-call(s32[1]{0:T(128)} %bitcast.core_ref, s32[96]{0:T(128)S(1)} %reshape_squeeze.6.own_ids, s32[96]{0:T(128)S(1)} %reshape_squeeze.7.other_ids), custom_call_target="tpu_custom_call" | custom-call | flops 1000000 | tf_op jit(solution)/shard_map/pallas_call | solution.py:347
  27.5 1.0 %collective-permute-start.7 = (bf16[8,136,128]{2,1,0:T(8,128)(2,1)S(1)}, bf16[8,136,128]{2,1,0:T(8,128)(2,1)S(1)}, u32[]{:S(2)}, u32[]{:S(2)}) collective-permute-start(bf16[8,136,128]{2,1,0:T(8,128)(2,1)S(1)} %collective-permute-done.6.refs_3_), channel_id=1, source_target_pairs={{0,8},{2,10},{4,0},{6,2},{8,16},{10,18},{12,4},{14,6},{16,24},{18,... | collective-permute-start | bytes 835592 | tf_op jit(solution)/shard_map/ppermute | solution.py:465
  28.6 3.5 %collective-permute-done.14.refs_2_ = bf16[8,136,128]{2,1,0:T(8,128)(2,1)S(1)} collective-permute-done((bf16[8,136,128]{2,1,0:T(8,128)(2,1)S(1)}, bf16[8,136,128]{2,1,0:T(8,128)(2,1)S(1)}, u32[]{:S(2)}, u32[]{:S(2)}) %collective-permute-start.14) | collective-permute-done | bytes 278560 | tf_op jit(solution)/shard_map/ppermute | solution.py:465
  32.1 0.6 collective-permute-start.15
  32.7 0.9 %collective-permute-start.19 = (bf16[8,136,128]{2,1,0:T(8,128)(2,1)S(1)}, bf16[8,136,128]{2,1,0:T(8,128)(2,1)S(1)}, u32[]{:S(2)}, u32[]{:S(2)}) collective-permute-start(bf16[8,136,128]{2,1,0:T(8,128)(2,1)S(1)} %collective-permute-done.18.refs_4_), channel_id=1, source_target_pairs={{0,4},{2,6},{4,12},{6,14},{8,0},{10,2},{12,20},{14,22},{16,8},{18,... | collective-permute-start | bytes 835592 | tf_op jit(solution)/shard_map/ppermute | solution.py:465
  33.6 3.1 %shard_map.88.refs_4_ = f32[32,136,128]{2,1,0:T(8,128)S(1)} custom-call(s32[1088]{0:T(1024)S(4)} %get-tuple-element.30.list_ref, s32[8]{0:T(128)S(4)} %get-tuple-element.31.count_ref, s32[160,4,128]{2,1,0:T(4,128)S(1)} %shard_map.85.masks_ref, f32[16,8,128]{2,1,0:T(8,128)S(1)} %get-tuple-element.38.own_sc, ...), custom_call_target="tpu_custom_call" | custom-call | flops 8000000000 | tf_op jit(solution)/shard_map/pallas_call | solution.py:347
  36.7 7.3 %collective-permute-done.15.refs_0_ = bf16[8,136,128]{2,1,0:T(8,128)(2,1)S(1)} collective-permute-done((bf16[8,136,128]{2,1,0:T(8,128)(2,1)S(1)}, bf16[8,136,128]{2,1,0:T(8,128)(2,1)S(1)}, u32[]{:S(2)}, u32[]{:S(2)}) %collective-permute-start.15) | collective-permute-done | bytes 278560 | tf_op jit(solution)/shard_map/ppermute | solution.py:465
  44.0 0.6 collective-permute-start.16
  44.6 0.9 %collective-permute-start.20 = (bf16[8,136,128]{2,1,0:T(8,128)(2,1)S(1)}, bf16[8,136,128]{2,1,0:T(8,128)(2,1)S(1)}, u32[]{:S(2)}, u32[]{:S(2)}) collective-permute-start(bf16[8,136,128]{2,1,0:T(8,128)(2,1)S(1)} %collective-permute-done.19.refs_2_), channel_id=1, source_target_pairs={{0,4},{2,6},{4,12},{6,14},{8,0},{10,2},{12,20},{14,22},{16,8},{18,... | collective-permute-start | bytes 835592 | tf_op jit(solution)/shard_map/ppermute | solution.py:465
  45.7 1.2 %collective-permute-start.8 = (bf16[8,136,128]{2,1,0:T(8,128)(2,1)S(1)}, bf16[8,136,128]{2,1,0:T(8,128)(2,1)S(1)}, u32[]{:S(2)}, u32[]{:S(2)}) collective-permute-start(bf16[8,136,128]{2,1,0:T(8,128)(2,1)S(1)} %collective-permute-done.7.refs_1_), channel_id=1, source_target_pairs={{0,8},{2,10},{4,0},{6,2},{8,16},{10,18},{12,4},{14,6},{16,24},{18,... | collective-permute-start | bytes 835592 | tf_op jit(solution)/shard_map/ppermute | solution.py:465
  47.0 2.0 %shard_map.89.refs_2_ = f32[32,136,128]{2,1,0:T(8,128)S(1)} custom-call(s32[1088]{0:T(1024)S(4)} %get-tuple-element.30.list_ref, s32[8]{0:T(128)S(4)} %get-tuple-element.31.count_ref, s32[160,4,128]{2,1,0:T(4,128)S(1)} %shard_map.85.masks_ref, f32[16,8,128]{2,1,0:T(8,128)S(1)} %get-tuple-element.38.own_sc, ...), custom_call_target="tpu_custom_call", output_to_operand_aliasing={{}: (10, {})} | custom-call | flops 8000000000 | tf_op jit(solution)/shard_map/pallas_call | solution.py:347
  49.0 1.7 %collective-permute-done.16.refs_0_ = bf16[8,136,128]{2,1,0:T(8,128)(2,1)S(1)} collective-permute-done((bf16[8,136,128]{2,1,0:T(8,128)(2,1)S(1)}, bf16[8,136,128]{2,1,0:T(8,128)(2,1)S(1)}, u32[]{:S(2)}, u32[]{:S(2)}) %collective-permute-start.16) | collective-permute-done | bytes 278560 | tf_op jit(solution)/shard_map/ppermute | solution.py:465
  51.1 1.2 %collective-permute-start.21 = (bf16[4,136,128]{2,1,0:T(8,128)(2,1)S(1)}, bf16[4,136,128]{2,1,0:T(8,128)(2,1)S(1)}, u32[]{:S(2)}, u32[]{:S(2)}) collective-permute-start(bf16[4,136,128]{2,1,0:T(8,128)(2,1)S(1)} %slice.29), channel_id=1, source_target_pairs={{0,4},{2,6},{4,12},{6,14},{8,0},{10,2},{12,20},{14,22},{16,8},{18,... | collective-permute-start | bytes 417800 | tf_op jit(solution)/shard_map/ppermute | solution.py:474
  52.3 4.4 %collective-permute-done.12.refs_1_ = bf16[8,136,128]{2,1,0:T(8,128)(2,1)S(1)} collective-permute-done((bf16[8,136,128]{2,1,0:T(8,128)(2,1)S(1)}, bf16[8,136,128]{2,1,0:T(8,128)(2,1)S(1)}, u32[]{:S(2)}, u32[]{:S(2)}) %collective-permute-start.12) | collective-permute-done | bytes 278560 | tf_op jit(solution)/shard_map/ppermute | solution.py:465
  56.8 1.2 %collective-permute-start.13 = (bf16[4,136,128]{2,1,0:T(8,128)(2,1)S(1)}, bf16[4,136,128]{2,1,0:T(8,128)(2,1)S(1)}, u32[]{:S(2)}, u32[]{:S(2)}) collective-permute-start(bf16[4,136,128]{2,1,0:T(8,128)(2,1)S(1)} %slice.27), channel_id=1, source_target_pairs={{0,4},{2,6},{4,12},{6,14},{8,0},{10,2},{12,20},{14,22},{16,8},{18,... | collective-permute-start | bytes 417800 | tf_op jit(solution)/shard_map/ppermute | solution.py:474
  58.4 2.0 %shard_map.90.refs_2_ = f32[32,136,128]{2,1,0:T(8,128)S(1)} custom-call(s32[1088]{0:T(1024)S(4)} %get-tuple-element.30.list_ref, s32[8]{0:T(128)S(4)} %get-tuple-element.31.count_ref, s32[160,4,128]{2,1,0:T(4,128)S(1)} %shard_map.85.masks_ref, f32[16,8,128]{2,1,0:T(8,128)S(1)} %get-tuple-element.38.own_sc, ...), custom_call_target="tpu_custom_call", output_to_operand_aliasing={{}: (8, {})} | custom-call | flops 8000000000 | tf_op jit(solution)/shard_map/pallas_call | solution.py:347
  60.4 1.1 %shard_map.91.refs_2_ = f32[32,136,128]{2,1,0:T(8,128)S(1)} custom-call(s32[1088]{0:T(1024)S(4)} %get-tuple-element.30.list_ref, s32[8]{0:T(128)S(4)} %get-tuple-element.31.count_ref, s32[160,4,128]{2,1,0:T(4,128)S(1)} %shard_map.85.masks_ref, f32[16,8,128]{2,1,0:T(8,128)S(1)} %get-tuple-element.38.own_sc, ...), custom_call_target="tpu_custom_call", output_to_operand_aliasing={{}: (8, {})} | custom-call | flops 8000000000 | tf_op jit(solution)/shard_map/pallas_call | solution.py:347
  61.5 1.7 %shard_map.92.refs_2_ = f32[32,136,128]{2,1,0:T(8,128)S(1)} custom-call(s32[1088]{0:T(1024)S(4)} %get-tuple-element.30.list_ref, s32[8]{0:T(128)S(4)} %get-tuple-element.31.count_ref, s32[160,4,128]{2,1,0:T(4,128)S(1)} %shard_map.85.masks_ref, f32[16,8,128]{2,1,0:T(8,128)S(1)} %get-tuple-element.38.own_sc, ...), custom_call_target="tpu_custom_call", output_to_operand_aliasing={{}: (8, {})} | custom-call | flops 8000000000 | tf_op jit(solution)/shard_map/pallas_call | solution.py:347
  63.4 8.9 %collective-permute-start.22 = (f32[16,136,128]{2,1,0:T(8,128)S(1)}, f32[16,136,128]{2,1,0:T(8,128)S(1)}, u32[]{:S(2)}, u32[]{:S(2)}) collective-permute-start(f32[16,136,128]{2,1,0:T(8,128)S(1)} %get-tuple-element.48), channel_id=1, source_target_pairs={{0,2},{2,0},{4,6},{6,4},{8,10},{10,8},{12,14},{14,12},{16,18},{18,... | collective-permute-start | bytes 3342344 | tf_op jit(solution)/shard_map/ppermute | solution.py:532
  72.4 2.3 %collective-permute-done.22.other_ref = f32[16,136,128]{2,1,0:T(8,128)S(1)} collective-permute-done((f32[16,136,128]{2,1,0:T(8,128)S(1)}, f32[16,136,128]{2,1,0:T(8,128)S(1)}, u32[]{:S(2)}, u32[]{:S(2)}) %collective-permute-start.22) | collective-permute-done | bytes 1114144 | tf_op jit(solution)/shard_map/ppermute | solution.py:532
  74.7 1.3 %shard_map.95 = bf16[128,2048]{1,0:T(8,128)(2,1)} custom-call(f32[32,136,128]{2,1,0:T(8,128)S(1)} %shard_map.94.state_ref, f32[16,136,128]{2,1,0:T(8,128)S(1)} %collective-permute-done.22.other_ref, bf16[128,2048]{1,0:T(8,128)(2,1)S(1)} %copy-done, f32[1,128]{1,0:T(1,128)S(1)} %bitcast.16), custom_call_target="tpu_custom_call" | custom-call | flops 1000000 | tf_op jit(solution)/shard_map/pallas_call | solution.py:347
  (41 shorter events, 4.6 us)
Async XLA Ops:
  1.1 15.7 %collective-permute-start.4 = (bf16[128,1024]{1,0:T(8,128)(2,1)S(1)}, bf16[128,1024]{1,0:T(8,128)(2,1)S(1)}, u32[]{:S(2)}, u32[]{:S(2)}) collective-permute-start(bf16[128,1024]{1,0:T(8,128)(2,1)S(1)} %get-tuple-element.36.refs_0_), channel_id=1, source_target_pairs={{0,1},{1,0},{2,3},{3,2},{4,5},{5,4},{6,7},{7,6},{8,9},{9,8},{10,11... | collective-permute-start | bytes 786440 | tf_op jit(solution)/shard_map/ppermute | solution.py:419
  2.4 14.9 %collective-permute-start.3 = (bf16[128,1024]{1,0:T(8,128)(2,1)S(1)}, bf16[128,1024]{1,0:T(8,128)(2,1)S(1)}, u32[]{:S(2)}, u32[]{:S(2)}) collective-permute-start(bf16[128,1024]{1,0:T(8,128)(2,1)S(1)} %get-tuple-element.35.refs_0_), channel_id=1, source_target_pairs={{0,1},{1,0},{2,3},{3,2},{4,5},{5,4},{6,7},{7,6},{8,9},{9,8},{10,11... | collective-permute-start | bytes 786440 | tf_op jit(solution)/shard_map/ppermute | solution.py:419
  15.6 5.3 %collective-permute-start.1 = (s32[80,2,128]{2,1,0:T(2,128)S(1)}, s32[80,2,128]{2,1,0:T(2,128)S(1)}, u32[]{:S(2)}, u32[]{:S(2)}) collective-permute-start(s32[80,2,128]{2,1,0:T(2,128)S(1)} %bitcast.12), channel_id=1, source_target_pairs={{0,1},{1,0},{2,3},{3,2},{4,5},{5,4},{6,7},{7,6},{8,9},{9,8},{10,11... | collective-permute-start | bytes 245768 | tf_op jit(solution)/shard_map/ppermute | solution.py:439
  17.9 9.1 %collective-permute-start.10 = (bf16[8,136,128]{2,1,0:T(8,128)(2,1)S(1)}, bf16[8,136,128]{2,1,0:T(8,128)(2,1)S(1)}, u32[]{:S(2)}, u32[]{:S(2)}) collective-permute-start(bf16[8,136,128]{2,1,0:T(8,128)(2,1)S(1)} %get-tuple-element.39.refs_1_), channel_id=1, source_target_pairs={{0,4},{2,6},{4,12},{6,14},{8,0},{10,2},{12,20},{14,22},{16,8},{18,... | collective-permute-start | bytes 835592 | tf_op jit(solution)/shard_map/ppermute | solution.py:465
  18.6 9.0 %collective-permute-start.6 = (bf16[8,136,128]{2,1,0:T(8,128)(2,1)S(1)}, bf16[8,136,128]{2,1,0:T(8,128)(2,1)S(1)}, u32[]{:S(2)}, u32[]{:S(2)}) collective-permute-start(bf16[8,136,128]{2,1,0:T(8,128)(2,1)S(1)} %get-tuple-element.39.refs_1_), channel_id=1, source_target_pairs={{0,8},{2,10},{4,0},{6,2},{8,16},{10,18},{12,4},{14,6},{16,24},{18,... | collective-permute-start | bytes 835592 | tf_op jit(solution)/shard_map/ppermute | solution.py:465
  19.4 12.7 %collective-permute-start.14 = (bf16[8,136,128]{2,1,0:T(8,128)(2,1)S(1)}, bf16[8,136,128]{2,1,0:T(8,128)(2,1)S(1)}, u32[]{:S(2)}, u32[]{:S(2)}) collective-permute-start(bf16[8,136,128]{2,1,0:T(8,128)(2,1)S(1)} %get-tuple-element.40.refs_0_), channel_id=1, source_target_pairs={{0,8},{2,10},{4,0},{6,2},{8,16},{10,18},{12,4},{14,6},{16,24},{18,... | collective-permute-start | bytes 835592 | tf_op jit(solution)/shard_map/ppermute | solution.py:465
  20.5 12.2 %collective-permute-start.18 = (bf16[8,136,128]{2,1,0:T(8,128)(2,1)S(1)}, bf16[8,136,128]{2,1,0:T(8,128)(2,1)S(1)}, u32[]{:S(2)}, u32[]{:S(2)}) collective-permute-start(bf16[8,136,128]{2,1,0:T(8,128)(2,1)S(1)} %get-tuple-element.40.refs_0_), channel_id=1, source_target_pairs={{0,4},{2,6},{4,12},{6,14},{8,0},{10,2},{12,20},{14,22},{16,8},{18,... | collective-permute-start | bytes 835592 | tf_op jit(solution)/shard_map/ppermute | solution.py:465
  20.9 2.7 %collective-permute-start = (s32[80,2,128]{2,1,0:T(2,128)S(1)}, s32[80,2,128]{2,1,0:T(2,128)S(1)}, u32[]{:S(2)}, u32[]{:S(2)}) collective-permute-start(s32[80,2,128]{2,1,0:T(2,128)S(1)} %bitcast.13), channel_id=1, source_target_pairs={{0,2},{2,0},{4,6},{6,4},{8,10},{10,8},{12,14},{14,12},{16,18},{18,... | collective-permute-start | bytes 245768 | tf_op jit(solution)/shard_map/ppermute | solution.py:440
  23.6 1.3 %collective-permute-start.2 = (s32[80,2,128]{2,1,0:T(2,128)S(1)}, s32[80,2,128]{2,1,0:T(2,128)S(1)}, u32[]{:S(2)}, u32[]{:S(2)}) collective-permute-start(s32[80,2,128]{2,1,0:T(2,128)S(1)} %collective-permute-done.1.refs_1_), channel_id=1, source_target_pairs={{0,2},{2,0},{4,6},{6,4},{8,10},{10,8},{12,14},{14,12},{16,18},{18,... | collective-permute-start | bytes 245768 | tf_op jit(solution)/shard_map/ppermute | solution.py:440
  24.9 8.7 %collective-permute-start.5 = (f32[16,8,128]{2,1,0:T(8,128)S(1)}, f32[16,8,128]{2,1,0:T(8,128)S(1)}, u32[]{:S(2)}, u32[]{:S(2)}) collective-permute-start(f32[16,8,128]{2,1,0:T(8,128)S(1)} %get-tuple-element.38.own_sc), channel_id=1, source_target_pairs={{0,2},{2,0},{4,6},{6,4},{8,10},{10,8},{12,14},{14,12},{16,18},{18,... | collective-permute-start | bytes 196616 | tf_op jit(solution)/shard_map/ppermute | solution.py:459
  27.0 18.5 %collective-permute-start.11 = (bf16[8,136,128]{2,1,0:T(8,128)(2,1)S(1)}, bf16[8,136,128]{2,1,0:T(8,128)(2,1)S(1)}, u32[]{:S(2)}, u32[]{:S(2)}) collective-permute-start(bf16[8,136,128]{2,1,0:T(8,128)(2,1)S(1)} %collective-permute-done.10.refs_5_), channel_id=1, source_target_pairs={{0,4},{2,6},{4,12},{6,14},{8,0},{10,2},{12,20},{14,22},{16,8},{18,... | collective-permute-start | bytes 835592 | tf_op jit(solution)/shard_map/ppermute | solution.py:465
  27.5 18.2 %collective-permute-start.7 = (bf16[8,136,128]{2,1,0:T(8,128)(2,1)S(1)}, bf16[8,136,128]{2,1,0:T(8,128)(2,1)S(1)}, u32[]{:S(2)}, u32[]{:S(2)}) collective-permute-start(bf16[8,136,128]{2,1,0:T(8,128)(2,1)S(1)} %collective-permute-done.6.refs_3_), channel_id=1, source_target_pairs={{0,8},{2,10},{4,0},{6,2},{8,16},{10,18},{12,4},{14,6},{16,24},{18,... | collective-permute-start | bytes 835592 | tf_op jit(solution)/shard_map/ppermute | solution.py:465
  32.1 11.9 %collective-permute-start.15 = (bf16[8,136,128]{2,1,0:T(8,128)(2,1)S(1)}, bf16[8,136,128]{2,1,0:T(8,128)(2,1)S(1)}, u32[]{:S(2)}, u32[]{:S(2)}) collective-permute-start(bf16[8,136,128]{2,1,0:T(8,128)(2,1)S(1)} %collective-permute-done.14.refs_2_), channel_id=1, source_target_pairs={{0,8},{2,10},{4,0},{6,2},{8,16},{10,18},{12,4},{14,6},{16,24},{18,... | collective-permute-start | bytes 835592 | tf_op jit(solution)/shard_map/ppermute | solution.py:465
  32.7 11.9 %collective-permute-start.19 = (bf16[8,136,128]{2,1,0:T(8,128)(2,1)S(1)}, bf16[8,136,128]{2,1,0:T(8,128)(2,1)S(1)}, u32[]{:S(2)}, u32[]{:S(2)}) collective-permute-start(bf16[8,136,128]{2,1,0:T(8,128)(2,1)S(1)} %collective-permute-done.18.refs_4_), channel_id=1, source_target_pairs={{0,4},{2,6},{4,12},{6,14},{8,0},{10,2},{12,20},{14,22},{16,8},{18,... | collective-permute-start | bytes 835592 | tf_op jit(solution)/shard_map/ppermute | solution.py:465
  44.0 6.7 %collective-permute-start.16 = (bf16[8,136,128]{2,1,0:T(8,128)(2,1)S(1)}, bf16[8,136,128]{2,1,0:T(8,128)(2,1)S(1)}, u32[]{:S(2)}, u32[]{:S(2)}) collective-permute-start(bf16[8,136,128]{2,1,0:T(8,128)(2,1)S(1)} %collective-permute-done.15.refs_0_), channel_id=1, source_target_pairs={{0,8},{2,10},{4,0},{6,2},{8,16},{10,18},{12,4},{14,6},{16,24},{18,... | collective-permute-start | bytes 835592 | tf_op jit(solution)/shard_map/ppermute | solution.py:465
  44.6 6.5 %collective-permute-start.20 = (bf16[8,136,128]{2,1,0:T(8,128)(2,1)S(1)}, bf16[8,136,128]{2,1,0:T(8,128)(2,1)S(1)}, u32[]{:S(2)}, u32[]{:S(2)}) collective-permute-start(bf16[8,136,128]{2,1,0:T(8,128)(2,1)S(1)} %collective-permute-done.19.refs_2_), channel_id=1, source_target_pairs={{0,4},{2,6},{4,12},{6,14},{8,0},{10,2},{12,20},{14,22},{16,8},{18,... | collective-permute-start | bytes 835592 | tf_op jit(solution)/shard_map/ppermute | solution.py:465
  45.5 11.2 %collective-permute-start.12 = (bf16[8,136,128]{2,1,0:T(8,128)(2,1)S(1)}, bf16[8,136,128]{2,1,0:T(8,128)(2,1)S(1)}, u32[]{:S(2)}, u32[]{:S(2)}) collective-permute-start(bf16[8,136,128]{2,1,0:T(8,128)(2,1)S(1)} %collective-permute-done.11.refs_3_), channel_id=1, source_target_pairs={{0,4},{2,6},{4,12},{6,14},{8,0},{10,2},{12,20},{14,22},{16,8},{18,... | collective-permute-start | bytes 835592 | tf_op jit(solution)/shard_map/ppermute | solution.py:465
  45.7 12.2 %collective-permute-start.8 = (bf16[8,136,128]{2,1,0:T(8,128)(2,1)S(1)}, bf16[8,136,128]{2,1,0:T(8,128)(2,1)S(1)}, u32[]{:S(2)}, u32[]{:S(2)}) collective-permute-start(bf16[8,136,128]{2,1,0:T(8,128)(2,1)S(1)} %collective-permute-done.7.refs_1_), channel_id=1, source_target_pairs={{0,8},{2,10},{4,0},{6,2},{8,16},{10,18},{12,4},{14,6},{16,24},{18,... | collective-permute-start | bytes 835592 | tf_op jit(solution)/shard_map/ppermute | solution.py:465
  50.7 10.7 %collective-permute-start.17 = (bf16[4,136,128]{2,1,0:T(8,128)(2,1)S(1)}, bf16[4,136,128]{2,1,0:T(8,128)(2,1)S(1)}, u32[]{:S(2)}, u32[]{:S(2)}) collective-permute-start(bf16[4,136,128]{2,1,0:T(8,128)(2,1)S(1)} %slice.28), channel_id=1, source_target_pairs={{0,8},{2,10},{4,0},{6,2},{8,16},{10,18},{12,4},{14,6},{16,24},{18,... | collective-permute-start | bytes 417800 | tf_op jit(solution)/shard_map/ppermute | solution.py:474
  51.1 10.3 %collective-permute-start.21 = (bf16[4,136,128]{2,1,0:T(8,128)(2,1)S(1)}, bf16[4,136,128]{2,1,0:T(8,128)(2,1)S(1)}, u32[]{:S(2)}, u32[]{:S(2)}) collective-permute-start(bf16[4,136,128]{2,1,0:T(8,128)(2,1)S(1)} %slice.29), channel_id=1, source_target_pairs={{0,4},{2,6},{4,12},{6,14},{8,0},{10,2},{12,20},{14,22},{16,8},{18,... | collective-permute-start | bytes 417800 | tf_op jit(solution)/shard_map/ppermute | solution.py:474
  56.8 6.4 %collective-permute-start.13 = (bf16[4,136,128]{2,1,0:T(8,128)(2,1)S(1)}, bf16[4,136,128]{2,1,0:T(8,128)(2,1)S(1)}, u32[]{:S(2)}, u32[]{:S(2)}) collective-permute-start(bf16[4,136,128]{2,1,0:T(8,128)(2,1)S(1)} %slice.27), channel_id=1, source_target_pairs={{0,4},{2,6},{4,12},{6,14},{8,0},{10,2},{12,20},{14,22},{16,8},{18,... | collective-permute-start | bytes 417800 | tf_op jit(solution)/shard_map/ppermute | solution.py:474
  58.0 5.3 %collective-permute-start.9 = (bf16[4,136,128]{2,1,0:T(8,128)(2,1)S(1)}, bf16[4,136,128]{2,1,0:T(8,128)(2,1)S(1)}, u32[]{:S(2)}, u32[]{:S(2)}) collective-permute-start(bf16[4,136,128]{2,1,0:T(8,128)(2,1)S(1)} %slice.26), channel_id=1, source_target_pairs={{0,8},{2,10},{4,0},{6,2},{8,16},{10,18},{12,4},{14,6},{16,24},{18,... | collective-permute-start | bytes 417800 | tf_op jit(solution)/shard_map/ppermute | solution.py:474
  63.4 11.3 %collective-permute-start.22 = (f32[16,136,128]{2,1,0:T(8,128)S(1)}, f32[16,136,128]{2,1,0:T(8,128)S(1)}, u32[]{:S(2)}, u32[]{:S(2)}) collective-permute-start(f32[16,136,128]{2,1,0:T(8,128)S(1)} %get-tuple-element.48), channel_id=1, source_target_pairs={{0,2},{2,0},{4,6},{6,4},{8,10},{10,8},{12,14},{14,12},{16,18},{18,... | collective-permute-start | bytes 3342344 | tf_op jit(solution)/shard_map/ppermute | solution.py:532
  72.3 2.4 %copy-start = (bf16[128,2048]{1,0:T(8,128)(2,1)S(1)}, bf16[128,2048]{1,0:T(8,128)(2,1)}, u32[]{:S(2)}) copy-start(bf16[128,2048]{1,0:T(8,128)(2,1)} %x_ref.1) | copy-start | bytes 1572868
  72.3 2.4 %copy-start.1 = (f32[128]{0:T(128)S(1)}, f32[128]{0:T(128)}, u32[]{:S(2)}) copy-start(f32[128]{0:T(128)} %param.12) | copy-start | bytes 1540

commit v4 on v3

--- a/solution.py
+++ b/solution.py
@@ -78,15 +78,16 @@
     source = head_sums(total * a_src)
     target = head_sums(total * a_dst)
     rest = source - head_sums(rounded.astype(F32) * a_src)
-    rest_hi = rest.astype(BF16).astype(F32)
-    extra = stack_rows([rest_hi, rest - rest_hi], pay_ref.shape[1] - rounded.shape[0]).astype(BF16)
     scores = stack_rows([target, leaky(source + target)], sc_ref.shape[1])
     dims, tile = rounded.shape[0], pay_ref.shape[2]
-    for b in range(pay_ref.shape[0]):
+    for b in range(2 * pay_ref.shape[0]):
         at = slice(b * tile, (b + 1) * tile)
-        pay_ref[b, :dims, :] = rounded[:, at]
-        pay_ref[b, dims:, :] = extra[:, at]
+        side = b % 2 * dims
+        pay_ref[b // 2, side : side + dims, :] = rounded[:, at]
         sc_ref[base + b] = scores[:, at]
+    for p in range(pay_ref.shape[0]):
+        rests = [rest[:, k * tile : (k + 1) * tile] for k in (2 * p, 2 * p + 1)]
+        pay_ref[p, 2 * dims :, :] = stack_rows(rests, pay_ref.shape[1] - 2 * dims).astype(BF16)
 
 
 def open_kernel(halves, *refs):
@@ -207,9 +208,11 @@
         for w in range(packed.shape[0])
     ]
     block = jnp.concatenate(block, axis=0)
-    feats = buf[spot, :dims, :]
-    extra = buf[spot, dims:, :].astype(F32)
-    source = head_sums(feats.astype(F32) * att) + extra[:heads] + extra[heads : 2 * heads]
+    side = spot & 1
+    feats = buf[spot >> 1, pl.ds(pl.multiple_of(side * dims, dims), dims), :]
+    rests = buf[spot >> 1, 2 * dims :, :].astype(F32)
+    rest = jnp.where(side == 1, rests[heads : 2 * heads], rests[:heads])
+    source = head_sums(feats.astype(F32) * att) + rest
     columns = jnp.transpose(stack_rows([source], pad8(heads)))
     for h in range(heads):
         edge = jnp.broadcast_to(columns[:, h : h + 1], (tile, tile)) + block
@@ -231,7 +234,8 @@
         edge = edges[h]
         raw = jnp.maximum(edge + up1[h : h + 1], 0.2 * edge + up2[h : h + 1])
         weight = jnp.exp2(raw).astype(BF16)
-        left = jnp.concatenate([buf[spot, h * HD : (h + 1) * HD, :], ones], axis=0)
+        at = pl.multiple_of((spot & 1) * dims + h * HD, HD)
+        left = jnp.concatenate([buf[spot >> 1, pl.ds(at, HD), :], ones], axis=0)
         values.append(jnp.dot(left, weight, preferred_element_type=F32))
     at = slice(dims + heads, dims + 2 * heads)
     mass = jnp.concatenate([v[HD : HD + 1] for v in values], axis=0)
@@ -258,7 +262,7 @@
         tile = state.shape[2]
         rest = state.shape[1] - dims - 2 * heads
         for b in range(blocks):
-            state[b, :dims] = buf[b, :dims].astype(F32)
+            state[b, :dims] = buf[b // 2, b % 2 * dims : (b % 2 + 1) * dims].astype(F32)
             state[b, dims : dims + heads] = own_sc[b, heads : 2 * heads]
             state[b, dims + heads : dims + 2 * heads] = jnp.ones((heads, tile), F32)
             state[blocks + b, :dims] = jnp.zeros((dims, tile), F32)
@@ -314,24 +318,25 @@
             lax.fori_loop(0, (number + 1) >> 1, body, 0)
 
     if len(outs) > 1:
-        outs[1][...] = state[blocks:]
-
-
-def merge_kernel(state_ref, other_ref, x_ref, bias_ref, whole_ref, out_ref, sems):
-    blocks, dims, tile = other_ref.shape[0], x_ref.shape[0], other_ref.shape[2]
+        outs[1][...] = state[blocks:, :dims].astype(BF16)
+        outs[2][...] = state[blocks:, dims:]
+
+
+def merge_kernel(state_ref, sums_ref, levels_ref, x_ref, bias_ref, whole_ref, out_ref, sems):
+    blocks, dims, tile = sums_ref.shape
     heads = dims // HD
     bias = column(bias_ref)
     share, copies = blocks // sems.shape[0], []
     for b in range(blocks):
-        m1, m2 = state_ref[b, dims : dims + heads], other_ref[b, dims : dims + heads]
+        m1, m2 = state_ref[b, dims : dims + heads], levels_ref[b, :heads]
         l1 = state_ref[b, dims + heads : dims + 2 * heads]
-        l2 = other_ref[b, dims + heads : dims + 2 * heads]
+        l2 = levels_ref[b, heads : 2 * heads]
         best = jnp.maximum(m1, m2)
         c1, c2 = jnp.exp2(m1 - best), jnp.exp2(m2 - best)
         scale = 1.0 / (l1 * c1 + l2 * c2)
         c1, c2 = (c1 * scale)[:, None, :], (c2 * scale)[:, None, :]
         mixed = state_ref[b, :dims].reshape(heads, HD, tile) * c1
-        mixed = mixed + other_ref[b, :dims].reshape(heads, HD, tile) * c2
+        mixed = mixed + sums_ref[b].astype(F32).reshape(heads, HD, tile) * c2
         at = slice(b * tile, (b + 1) * tile)
         v = mixed.reshape(dims, tile) + x_ref[:, at].astype(F32) + bias
         out_ref[:, at] = jnp.where(v > 0, v, jnp.exp(jnp.minimum(v, 0.0)) - 1.0).astype(BF16)
@@ -447,7 +452,7 @@
         pay, own_sc = call(
             functools.partial(project_kernel, len(xs), k * half),
             (
-                pltpu.VMEM((half, dims + extra, tile), BF16),
+                pltpu.VMEM((half // 2, 2 * dims + extra, tile), BF16),
                 pltpu.VMEM((blocks, extra, tile), F32),
             ),
             args,
@@ -470,7 +475,7 @@
     arrivals[0] = pays + arrivals[0]
     for p in "AB":
         both = []
-        for w, pairs, cut in (("r", right, slice(0, half // 2)), ("l", left, slice(half // 2, half))):
+        for w, pairs, cut in (("r", right, slice(0, half // 4)), ("l", left, slice(half // 4, half // 2))):
             both.append(lax.ppermute(going[w + p][cut], "dp", pairs))
         arrivals.append(both)
 
@@ -496,7 +501,7 @@
 
     shared = [masks, own_sc, other_sc, att[0]]
     state_shape = pltpu.VMEM((2 * blocks, dims + extra, tile), F32)
-    half_shape = pltpu.VMEM((blocks, dims + extra, tile), F32)
+    half_shapes = [pltpu.VMEM((blocks, dims, tile), BF16), pltpu.VMEM((blocks, extra, tile), F32)]
 
     def stage(g, bufs, state, hand=False):
         args = [held(lists), held(counts)] + [near(v) for v in shared + bufs]
@@ -505,7 +510,7 @@
             args.append(near(state))
             aliases[len(args) - 1] = 0
         if hand:
-            outs.append(half_shape)
+            outs += half_shapes
             for k, v in enumerate(shared + bufs):
                 aliases[2 + k] = len(outs)
                 outs.append(pltpu.VMEM(v.shape, v.dtype))
@@ -517,7 +522,7 @@
             out_specs=[VMEM] * len(outs),
             scratch=[
                 pltpu.VMEM((2 * blocks, extra, tile), F32),
-                pltpu.VMEM((sum(v.shape[0] for v in bufs), dims + extra, tile), BF16),
+                pltpu.VMEM((sum(v.shape[0] for v in bufs), 2 * dims + extra, tile), BF16),
                 *[pltpu.VMEM((WIDE, heads, tile, tile), F32)] * 2,
                 *[pltpu.VMEM((WIDE, pad8(heads), tile), F32)] * 2,
             ],
@@ -528,14 +533,14 @@
     state = None
     for g, bufs in enumerate(arrivals[:-1]):
         (state,) = stage(g, bufs, state)
-    state, other, *rest = stage(steps + 1, arrivals[-1], state, True)
-    back = lax.ppermute(other, "dp", swap)
+    state, sums, levels, *rest = stage(steps + 1, arrivals[-1], state, True)
+    back = lax.ppermute(sums, "dp", swap), lax.ppermute(levels, "dp", swap)
     shared = rest[: len(shared)]
     (state,) = stage(steps + 2, rest[len(shared) :], state)
     return call(
         merge_kernel,
         jax.ShapeDtypeStruct((dims, nodes), BF16),
-        (near(state), near(back), node_feats, out_bias.reshape(1, dims)),
+        (near(state), *[near(v) for v in back], node_feats, out_bias.reshape(1, dims)),
         out_specs=anywhere,
         scratch=[pltpu.VMEM((dims, nodes), BF16), pltpu.SemaphoreType.DMA((math.gcd(blocks, 4),))],
     )

time: 76.6 us -> 76.3 us (level); the launches traced: 76 us -> 74.9 us
  starting transfers between devices: 26.2 us -> 24.3 us
    ppermute x12, waiting for transfers between devices: 17 us -> 19.5 us  [local(): lax.ppermute(going[way], 'dp', right if way[0] == 'r' else left)]
    ppermute x1 -> x2, starting transfers between devices: 8.93 us -> 7.21 us  [local(): back = (lax.ppermute(sums, 'dp', swap), lax.ppermute(levels, 'dp', swap))]
    ppermute x2, waiting for transfers between devices: 1.85 us -> 0.93 us  [local(): got_other = [lax.ppermute(v, 'dp', swap) for v in got]]
    ppermute x1 -> x2, waiting for transfers between devices: 2.27 us -> 1.45 us  [local(): back = (lax.ppermute(sums, 'dp', swap), lax.ppermute(levels, 'dp', swap))]
  transfers between devices with their start and end apart: 23 -> 24, of which waited for: 7 -> 8; matrix products, arithmetic and copies ran while one was open for 0% -> 0% of each run, Pallas kernels for 19% -> 19%
where the time goes in v4:
time: 76.3 us; the launch traced here: 74.9 us
  starting transfers between devices  24.3 us (32%)
  waiting for transfers between devices  21.9 us (29%)
  Pallas kernels  16.7 us (22%)
  blocking collectives  11.5 us (15%)
    ppermute x12, waiting for transfers between devices, local(): lax.ppermute(going[way], 'dp', right if way[0] == 'r' else left)  19.5 us
    pallas_call x14, Pallas kernels, call(): pl.pallas_call(kernel, out_shape=outs, in_specs=in_specs or [VMEM] * len(...  16.7 us
    all_to_all x1, blocking collectives, local(): got = lax.all_to_all(packed, 'dp', split_axis=0, concat_axis=0, tiled=True)  11.5 us
    ppermute x12, starting transfers between devices, local(): lax.ppermute(going[way], 'dp', right if way[0] == 'r' else left)  9.07 us
    ppermute x2, starting transfers between devices, local(): back = (lax.ppermute(sums, 'dp', swap), lax.ppermute(levels, 'dp', swap))  7.21 us
    ppermute x4, starting transfers between devices, local(): both.append(lax.ppermute(going[w + p][cut], 'dp', pairs))  3.11 us
    ppermute x2, starting transfers between devices, local(): got_other = [lax.ppermute(v, 'dp', swap) for v in got]  1.76 us
    ppermute x2, starting transfers between devices, local(): inputs = [[x, lax.ppermute(x, 'mp', flip)] for x in cuts]  1.53 us
  transfers between devices with their start and end apart: 24, of which 8 were waited for; matrix products, arithmetic and copies ran while one was open for 0% of the time, Pallas kernels for 19%

profile of v4, /device:TPU:11, one launch (start us, length us, event | category | flops | bytes accessed | tf_op | source)
XLA Modules:
  0.0 74.9 jit_solution(2809835437033710011)
XLA Ops:
  0.0 1.1 %shard_map.82 = (bf16[128,1024]{1,0:T(8,128)(2,1)S(1)}, bf16[128,1024]{1,0:T(8,128)(2,1)S(1)}, bf16[128,256]{1,0:T(8,128)(2,1)S(1)}, f32[1,128]{1,0:T(1,128)S(1)...) custom-call(bf16[128,2048]{1,0:T(8,128)(2,1)} %x_ref.1, ...), custom_call_target="tpu_custom_call" | custom-call | flops 1000000 | tf_op jit(solution)/shard_map/pallas_call | solution.py:352
  1.1 1.3 %collective-permute-start.4 = (bf16[128,1024]{1,0:T(8,128)(2,1)S(1)}, bf16[128,1024]{1,0:T(8,128)(2,1)S(1)}, u32[]{:S(2)}, u32[]{:S(2)}) collective-permute-start(bf16[128,1024]{1,0:T(8,128)(2,1)S(1)} %get-tuple-element.37.refs_0_), channel_id=1, source_target_pairs={{0,1},{1,0},{2,3},{3,2},{4,5},{5,4},{6,7},{7,6},{8,9},{9,8},{10,11... | collective-permute-start | bytes 786440 | tf_op jit(solution)/shard_map/ppermute | solution.py:424
  2.7 1.4 %shard_map.83 = s32[16,5,2,128]{3,2,1,0:T(2,128)} custom-call(s32[1]{0:T(128)} %bitcast.1.mp_ref, s32[32]{0:T(128)S(4)} %get-tuple-element.28.rows_ref, s32[32]{0:T(128)S(4)} %get-tuple-element.29.cols_ref, s32[32,4,128]{2,1,0:T(4,128)S(1)} %get-tuple-element.30.masks_ref), custom_call_target="tpu_custom_call" | custom-call | flops 1000000 | tf_op jit(solution)/shard_map/pallas_call | solution.py:352
  4.1 11.5 %all_to_all.5 = s32[16,5,2,128]{3,2,1,0:T(2,128)S(1)} all-to-all(s32[16,5,2,128]{3,2,1,0:T(2,128)} %shard_map.83), channel_id=1, replica_groups=mesh['dp'=16,'mp'=2] {'dp'}, dimensions={0} | all-to-all | bytes 163840 | tf_op jit(solution)/shard_map/all_to_all | solution.py:441
  15.6 1.2 %collective-permute-start.1 = (s32[80,2,128]{2,1,0:T(2,128)S(1)}, s32[80,2,128]{2,1,0:T(2,128)S(1)}, u32[]{:S(2)}, u32[]{:S(2)}) collective-permute-start(s32[80,2,128]{2,1,0:T(2,128)S(1)} %bitcast.12), channel_id=1, source_target_pairs={{0,1},{1,0},{2,3},{3,2},{4,5},{5,4},{6,7},{7,6},{8,9},{9,8},{10,11... | collective-permute-start | bytes 245768 | tf_op jit(solution)/shard_map/ppermute | solution.py:444
  16.8 0.6 collective-permute-start
  18.0 0.5 shard_map.87
  19.0 1.1 %collective-permute-start.6 = (bf16[4,264,128]{2,1,0:T(8,128)(2,1)S(1)}, bf16[4,264,128]{2,1,0:T(8,128)(2,1)S(1)}, u32[]{:S(2)}, u32[]{:S(2)}) collective-permute-start(bf16[4,264,128]{2,1,0:T(8,128)(2,1)S(1)} %get-tuple-element.40.refs_1_), channel_id=1, source_target_pairs={{0,8},{2,10},{4,0},{6,2},{8,16},{10,18},{12,4},{14,6},{16,24},{18,... | collective-permute-start | bytes 811016 | tf_op jit(solution)/shard_map/ppermute | solution.py:470
  20.0 1.4 %collective-permute-start.14 = (bf16[4,264,128]{2,1,0:T(8,128)(2,1)S(1)}, bf16[4,264,128]{2,1,0:T(8,128)(2,1)S(1)}, u32[]{:S(2)}, u32[]{:S(2)}) collective-permute-start(bf16[4,264,128]{2,1,0:T(8,128)(2,1)S(1)} %get-tuple-element.41.refs_0_), channel_id=1, source_target_pairs={{0,8},{2,10},{4,0},{6,2},{8,16},{10,18},{12,4},{14,6},{16,24},{18,... | collective-permute-start | bytes 811016 | tf_op jit(solution)/shard_map/ppermute | solution.py:470
  21.5 1.1 %collective-permute-start.2 = (s32[80,2,128]{2,1,0:T(2,128)S(1)}, s32[80,2,128]{2,1,0:T(2,128)S(1)}, u32[]{:S(2)}, u32[]{:S(2)}) collective-permute-start(s32[80,2,128]{2,1,0:T(2,128)S(1)} %collective-permute-done.1.refs_1_), channel_id=1, source_target_pairs={{0,2},{2,0},{4,6},{6,4},{8,10},{10,8},{12,14},{14,12},{16,18},{18,... | collective-permute-start | bytes 245768 | tf_op jit(solution)/shard_map/ppermute | solution.py:445
  22.6 0.9 %collective-permute-done.2.refs_3_ = s32[80,2,128]{2,1,0:T(2,128)S(1)} collective-permute-done((s32[80,2,128]{2,1,0:T(2,128)S(1)}, s32[80,2,128]{2,1,0:T(2,128)S(1)}, u32[]{:S(2)}, u32[]{:S(2)}) %collective-permute-start.2) | collective-permute-done | bytes 81952 | tf_op jit(solution)/shard_map/ppermute | solution.py:445
  24.1 1.5 %shard_map.84 = (s32[1088]{0:T(1024)S(4)}, s32[8]{0:T(128)S(4)}) custom-call(s32[1]{0:T(128)} %bitcast.core_ref, s32[96]{0:T(128)S(1)} %reshape_squeeze.6.own_ids, s32[96]{0:T(128)S(1)} %reshape_squeeze.7.other_ids), custom_call_target="tpu_custom_call" | custom-call | flops 1000000 | tf_op jit(solution)/shard_map/pallas_call | solution.py:352
  25.7 0.9 %collective-permute-done.10.refs_5_ = bf16[4,264,128]{2,1,0:T(8,128)(2,1)S(1)} collective-permute-done((bf16[4,264,128]{2,1,0:T(8,128)(2,1)S(1)}, bf16[4,264,128]{2,1,0:T(8,128)(2,1)S(1)}, u32[]{:S(2)}, u32[]{:S(2)}) %collective-permute-start.10) | collective-permute-done | bytes 270368 | tf_op jit(solution)/shard_map/ppermute | solution.py:470
  26.9 1.3 %collective-permute-start.7 = (bf16[4,264,128]{2,1,0:T(8,128)(2,1)S(1)}, bf16[4,264,128]{2,1,0:T(8,128)(2,1)S(1)}, u32[]{:S(2)}, u32[]{:S(2)}) collective-permute-start(bf16[4,264,128]{2,1,0:T(8,128)(2,1)S(1)} %collective-permute-done.6.refs_3_), channel_id=1, source_target_pairs={{0,8},{2,10},{4,0},{6,2},{8,16},{10,18},{12,4},{14,6},{16,24},{18,... | collective-permute-start | bytes 811016 | tf_op jit(solution)/shard_map/ppermute | solution.py:470
  28.2 4.2 %collective-permute-done.14.refs_2_ = bf16[4,264,128]{2,1,0:T(8,128)(2,1)S(1)} collective-permute-done((bf16[4,264,128]{2,1,0:T(8,128)(2,1)S(1)}, bf16[4,264,128]{2,1,0:T(8,128)(2,1)S(1)}, u32[]{:S(2)}, u32[]{:S(2)}) %collective-permute-start.14) | collective-permute-done | bytes 270368 | tf_op jit(solution)/shard_map/ppermute | solution.py:470
  32.4 1.2 %collective-permute-start.15 = (bf16[4,264,128]{2,1,0:T(8,128)(2,1)S(1)}, bf16[4,264,128]{2,1,0:T(8,128)(2,1)S(1)}, u32[]{:S(2)}, u32[]{:S(2)}) collective-permute-start(bf16[4,264,128]{2,1,0:T(8,128)(2,1)S(1)} %collective-permute-done.14.refs_2_), channel_id=1, source_target_pairs={{0,8},{2,10},{4,0},{6,2},{8,16},{10,18},{12,4},{14,6},{16,24},{18,... | collective-permute-start | bytes 811016 | tf_op jit(solution)/shard_map/ppermute | solution.py:470
  33.9 3.1 %shard_map.88.refs_4_ = f32[32,136,128]{2,1,0:T(8,128)S(1)} custom-call(s32[1088]{0:T(1024)S(4)} %get-tuple-element.31.list_ref, s32[8]{0:T(128)S(4)} %get-tuple-element.32.count_ref, s32[160,4,128]{2,1,0:T(4,128)S(1)} %shard_map.85.masks_ref, f32[16,8,128]{2,1,0:T(8,128)S(1)} %get-tuple-element.39.own_sc, ...), custom_call_target="tpu_custom_call" | custom-call | flops 8000000000 | tf_op jit(solution)/shard_map/pallas_call | solution.py:352
  37.0 7.0 %collective-permute-done.15.refs_0_ = bf16[4,264,128]{2,1,0:T(8,128)(2,1)S(1)} collective-permute-done((bf16[4,264,128]{2,1,0:T(8,128)(2,1)S(1)}, bf16[4,264,128]{2,1,0:T(8,128)(2,1)S(1)}, u32[]{:S(2)}, u32[]{:S(2)}) %collective-permute-start.15) | collective-permute-done | bytes 270368 | tf_op jit(solution)/shard_map/ppermute | solution.py:470
  44.0 1.2 %collective-permute-start.16 = (bf16[4,264,128]{2,1,0:T(8,128)(2,1)S(1)}, bf16[4,264,128]{2,1,0:T(8,128)(2,1)S(1)}, u32[]{:S(2)}, u32[]{:S(2)}) collective-permute-start(bf16[4,264,128]{2,1,0:T(8,128)(2,1)S(1)} %collective-permute-done.15.refs_0_), channel_id=1, source_target_pairs={{0,8},{2,10},{4,0},{6,2},{8,16},{10,18},{12,4},{14,6},{16,24},{18,... | collective-permute-start | bytes 811016 | tf_op jit(solution)/shard_map/ppermute | solution.py:470
  45.5 0.9 %collective-permute-start.12 = (bf16[4,264,128]{2,1,0:T(8,128)(2,1)S(1)}, bf16[4,264,128]{2,1,0:T(8,128)(2,1)S(1)}, u32[]{:S(2)}, u32[]{:S(2)}) collective-permute-start(bf16[4,264,128]{2,1,0:T(8,128)(2,1)S(1)} %collective-permute-done.11.refs_3_), channel_id=1, source_target_pairs={{0,4},{2,6},{4,12},{6,14},{8,0},{10,2},{12,20},{14,22},{16,8},{18,... | collective-permute-start | bytes 811016 | tf_op jit(solution)/shard_map/ppermute | solution.py:470
  46.3 0.6 collective-permute-start.8
  47.0 2.0 %shard_map.89.refs_2_ = f32[32,136,128]{2,1,0:T(8,128)S(1)} custom-call(s32[1088]{0:T(1024)S(4)} %get-tuple-element.31.list_ref, s32[8]{0:T(128)S(4)} %get-tuple-element.32.count_ref, s32[160,4,128]{2,1,0:T(4,128)S(1)} %shard_map.85.masks_ref, f32[16,8,128]{2,1,0:T(8,128)S(1)} %get-tuple-element.39.own_sc, ...), custom_call_target="tpu_custom_call", output_to_operand_aliasing={{}: (10, {})} | custom-call | flops 8000000000 | tf_op jit(solution)/shard_map/pallas_call | solution.py:352
  49.0 1.8 %collective-permute-done.16.refs_0_ = bf16[4,264,128]{2,1,0:T(8,128)(2,1)S(1)} collective-permute-done((bf16[4,264,128]{2,1,0:T(8,128)(2,1)S(1)}, bf16[4,264,128]{2,1,0:T(8,128)(2,1)S(1)}, u32[]{:S(2)}, u32[]{:S(2)}) %collective-permute-start.16) | collective-permute-done | bytes 270368 | tf_op jit(solution)/shard_map/ppermute | solution.py:470
  50.8 1.3 %collective-permute-start.17 = (bf16[2,264,128]{2,1,0:T(8,128)(2,1)S(1)}, bf16[2,264,128]{2,1,0:T(8,128)(2,1)S(1)}, u32[]{:S(2)}, u32[]{:S(2)}) collective-permute-start(bf16[2,264,128]{2,1,0:T(8,128)(2,1)S(1)} %slice.28), channel_id=1, source_target_pairs={{0,8},{2,10},{4,0},{6,2},{8,16},{10,18},{12,4},{14,6},{16,24},{18,... | collective-permute-start | bytes 405512 | tf_op jit(solution)/shard_map/ppermute | solution.py:479
  52.4 5.6 %collective-permute-done.12.refs_1_ = bf16[4,264,128]{2,1,0:T(8,128)(2,1)S(1)} collective-permute-done((bf16[4,264,128]{2,1,0:T(8,128)(2,1)S(1)}, bf16[4,264,128]{2,1,0:T(8,128)(2,1)S(1)}, u32[]{:S(2)}, u32[]{:S(2)}) %collective-permute-start.12) | collective-permute-done | bytes 270368 | tf_op jit(solution)/shard_map/ppermute | solution.py:470
  58.1 1.6 %collective-permute-start.9 = (bf16[2,264,128]{2,1,0:T(8,128)(2,1)S(1)}, bf16[2,264,128]{2,1,0:T(8,128)(2,1)S(1)}, u32[]{:S(2)}, u32[]{:S(2)}) collective-permute-start(bf16[2,264,128]{2,1,0:T(8,128)(2,1)S(1)} %slice.26), channel_id=1, source_target_pairs={{0,8},{2,10},{4,0},{6,2},{8,16},{10,18},{12,4},{14,6},{16,24},{18,... | collective-permute-start | bytes 405512 | tf_op jit(solution)/shard_map/ppermute | solution.py:479
  59.7 2.0 %shard_map.90.refs_2_ = f32[32,136,128]{2,1,0:T(8,128)S(1)} custom-call(s32[1088]{0:T(1024)S(4)} %get-tuple-element.31.list_ref, s32[8]{0:T(128)S(4)} %get-tuple-element.32.count_ref, s32[160,4,128]{2,1,0:T(4,128)S(1)} %shard_map.85.masks_ref, f32[16,8,128]{2,1,0:T(8,128)S(1)} %get-tuple-element.39.own_sc, ...), custom_call_target="tpu_custom_call", output_to_operand_aliasing={{}: (8, {})} | custom-call | flops 8000000000 | tf_op jit(solution)/shard_map/pallas_call | solution.py:352
  61.7 1.1 %shard_map.91.refs_2_ = f32[32,136,128]{2,1,0:T(8,128)S(1)} custom-call(s32[1088]{0:T(1024)S(4)} %get-tuple-element.31.list_ref, s32[8]{0:T(128)S(4)} %get-tuple-element.32.count_ref, s32[160,4,128]{2,1,0:T(4,128)S(1)} %shard_map.85.masks_ref, f32[16,8,128]{2,1,0:T(8,128)S(1)} %get-tuple-element.39.own_sc, ...), custom_call_target="tpu_custom_call", output_to_operand_aliasing={{}: (8, {})} | custom-call | flops 8000000000 | tf_op jit(solution)/shard_map/pallas_call | solution.py:352
  62.8 1.7 %shard_map.92.refs_2_ = f32[32,136,128]{2,1,0:T(8,128)S(1)} custom-call(s32[1088]{0:T(1024)S(4)} %get-tuple-element.31.list_ref, s32[8]{0:T(128)S(4)} %get-tuple-element.32.count_ref, s32[160,4,128]{2,1,0:T(4,128)S(1)} %shard_map.85.masks_ref, f32[16,8,128]{2,1,0:T(8,128)S(1)} %get-tuple-element.39.own_sc, ...), custom_call_target="tpu_custom_call", output_to_operand_aliasing={{}: (8, {})} | custom-call | flops 8000000000 | tf_op jit(solution)/shard_map/pallas_call | solution.py:352
  64.7 7.1 %collective-permute-start.22 = (bf16[16,128,128]{2,1,0:T(8,128)(2,1)S(1)}, bf16[16,128,128]{2,1,0:T(8,128)(2,1)S(1)}, u32[]{:S(2)}, u32[]{:S(2)}) collective-permute-start(bf16[16,128,128]{2,1,0:T(8,128)(2,1)S(1)} %get-tuple-element.49), channel_id=1, source_target_pairs={{0,2},{2,0},{4,6},{6,4},{8,10},{10,8},{12,14},{14,12},{16,18},{18,... | collective-permute-start | bytes 1572872 | tf_op jit(solution)/shard_map/ppermute | solution.py:537
  72.1 1.4 %collective-permute-done.23.levels_ref = f32[16,8,128]{2,1,0:T(8,128)S(1)} collective-permute-done((f32[16,8,128]{2,1,0:T(8,128)S(1)}, f32[16,8,128]{2,1,0:T(8,128)S(1)}, u32[]{:S(2)}, u32[]{:S(2)}) %collective-permute-start.23) | collective-permute-done | bytes 65568 | tf_op jit(solution)/shard_map/ppermute | solution.py:537
  73.5 1.4 %shard_map.95 = bf16[128,2048]{1,0:T(8,128)(2,1)} custom-call(f32[32,136,128]{2,1,0:T(8,128)S(1)} %shard_map.94.state_ref, bf16[16,128,128]{2,1,0:T(8,128)(2,1)S(1)} %collective-permute-done.22.sums_ref, f32[16,8,128]{2,1,0:T(8,128)S(1)} %collective-permute-done.23.levels_ref, bf16[128,2048]{1,0:T(8,128)(2,1)S(1)} %copy-done, f32[1,128]{1,0:T(1,128)S(1)} %bitcast.16), custom_call_target="tpu_custom_call" | custom-call | flops 1000000 | tf_op jit(solution)/shard_map/pallas_call | solution.py:352
  (43 shorter events, 3.5 us)
Async XLA Ops:
  1.1 16.3 %collective-permute-start.4 = (bf16[128,1024]{1,0:T(8,128)(2,1)S(1)}, bf16[128,1024]{1,0:T(8,128)(2,1)S(1)}, u32[]{:S(2)}, u32[]{:S(2)}) collective-permute-start(bf16[128,1024]{1,0:T(8,128)(2,1)S(1)} %get-tuple-element.37.refs_0_), channel_id=1, source_target_pairs={{0,1},{1,0},{2,3},{3,2},{4,5},{5,4},{6,7},{7,6},{8,9},{9,8},{10,11... | collective-permute-start | bytes 786440 | tf_op jit(solution)/shard_map/ppermute | solution.py:424
  2.4 15.5 %collective-permute-start.3 = (bf16[128,1024]{1,0:T(8,128)(2,1)S(1)}, bf16[128,1024]{1,0:T(8,128)(2,1)S(1)}, u32[]{:S(2)}, u32[]{:S(2)}) collective-permute-start(bf16[128,1024]{1,0:T(8,128)(2,1)S(1)} %get-tuple-element.36.refs_0_), channel_id=1, source_target_pairs={{0,1},{1,0},{2,3},{3,2},{4,5},{5,4},{6,7},{7,6},{8,9},{9,8},{10,11... | collective-permute-start | bytes 786440 | tf_op jit(solution)/shard_map/ppermute | solution.py:424
  15.6 5.8 %collective-permute-start.1 = (s32[80,2,128]{2,1,0:T(2,128)S(1)}, s32[80,2,128]{2,1,0:T(2,128)S(1)}, u32[]{:S(2)}, u32[]{:S(2)}) collective-permute-start(s32[80,2,128]{2,1,0:T(2,128)S(1)} %bitcast.12), channel_id=1, source_target_pairs={{0,1},{1,0},{2,3},{3,2},{4,5},{5,4},{6,7},{7,6},{8,9},{9,8},{10,11... | collective-permute-start | bytes 245768 | tf_op jit(solution)/shard_map/ppermute | solution.py:444
  16.8 4.7 %collective-permute-start = (s32[80,2,128]{2,1,0:T(2,128)S(1)}, s32[80,2,128]{2,1,0:T(2,128)S(1)}, u32[]{:S(2)}, u32[]{:S(2)}) collective-permute-start(s32[80,2,128]{2,1,0:T(2,128)S(1)} %bitcast.13), channel_id=1, source_target_pairs={{0,2},{2,0},{4,6},{6,4},{8,10},{10,8},{12,14},{14,12},{16,18},{18,... | collective-permute-start | bytes 245768 | tf_op jit(solution)/shard_map/ppermute | solution.py:445
  18.5 8.1 %collective-permute-start.10 = (bf16[4,264,128]{2,1,0:T(8,128)(2,1)S(1)}, bf16[4,264,128]{2,1,0:T(8,128)(2,1)S(1)}, u32[]{:S(2)}, u32[]{:S(2)}) collective-permute-start(bf16[4,264,128]{2,1,0:T(8,128)(2,1)S(1)} %get-tuple-element.40.refs_1_), channel_id=1, source_target_pairs={{0,4},{2,6},{4,12},{6,14},{8,0},{10,2},{12,20},{14,22},{16,8},{18,... | collective-permute-start | bytes 811016 | tf_op jit(solution)/shard_map/ppermute | solution.py:470
  19.0 7.9 %collective-permute-start.6 = (bf16[4,264,128]{2,1,0:T(8,128)(2,1)S(1)}, bf16[4,264,128]{2,1,0:T(8,128)(2,1)S(1)}, u32[]{:S(2)}, u32[]{:S(2)}) collective-permute-start(bf16[4,264,128]{2,1,0:T(8,128)(2,1)S(1)} %get-tuple-element.40.refs_1_), channel_id=1, source_target_pairs={{0,8},{2,10},{4,0},{6,2},{8,16},{10,18},{12,4},{14,6},{16,24},{18,... | collective-permute-start | bytes 811016 | tf_op jit(solution)/shard_map/ppermute | solution.py:470
  20.0 12.4 %collective-permute-start.14 = (bf16[4,264,128]{2,1,0:T(8,128)(2,1)S(1)}, bf16[4,264,128]{2,1,0:T(8,128)(2,1)S(1)}, u32[]{:S(2)}, u32[]{:S(2)}) collective-permute-start(bf16[4,264,128]{2,1,0:T(8,128)(2,1)S(1)} %get-tuple-element.41.refs_0_), channel_id=1, source_target_pairs={{0,8},{2,10},{4,0},{6,2},{8,16},{10,18},{12,4},{14,6},{16,24},{18,... | collective-permute-start | bytes 811016 | tf_op jit(solution)/shard_map/ppermute | solution.py:470
  21.4 12.1 %collective-permute-start.18 = (bf16[4,264,128]{2,1,0:T(8,128)(2,1)S(1)}, bf16[4,264,128]{2,1,0:T(8,128)(2,1)S(1)}, u32[]{:S(2)}, u32[]{:S(2)}) collective-permute-start(bf16[4,264,128]{2,1,0:T(8,128)(2,1)S(1)} %get-tuple-element.41.refs_0_), channel_id=1, source_target_pairs={{0,4},{2,6},{4,12},{6,14},{8,0},{10,2},{12,20},{14,22},{16,8},{18,... | collective-permute-start | bytes 811016 | tf_op jit(solution)/shard_map/ppermute | solution.py:470
  21.5 2.0 %collective-permute-start.2 = (s32[80,2,128]{2,1,0:T(2,128)S(1)}, s32[80,2,128]{2,1,0:T(2,128)S(1)}, u32[]{:S(2)}, u32[]{:S(2)}) collective-permute-start(s32[80,2,128]{2,1,0:T(2,128)S(1)} %collective-permute-done.1.refs_1_), channel_id=1, source_target_pairs={{0,2},{2,0},{4,6},{6,4},{8,10},{10,8},{12,14},{14,12},{16,18},{18,... | collective-permute-start | bytes 245768 | tf_op jit(solution)/shard_map/ppermute | solution.py:445
  23.5 10.3 %collective-permute-start.5 = (f32[16,8,128]{2,1,0:T(8,128)S(1)}, f32[16,8,128]{2,1,0:T(8,128)S(1)}, u32[]{:S(2)}, u32[]{:S(2)}) collective-permute-start(f32[16,8,128]{2,1,0:T(8,128)S(1)} %get-tuple-element.39.own_sc), channel_id=1, source_target_pairs={{0,2},{2,0},{4,6},{6,4},{8,10},{10,8},{12,14},{14,12},{16,18},{18,... | collective-permute-start | bytes 196616 | tf_op jit(solution)/shard_map/ppermute | solution.py:464
  26.6 18.9 %collective-permute-start.11 = (bf16[4,264,128]{2,1,0:T(8,128)(2,1)S(1)}, bf16[4,264,128]{2,1,0:T(8,128)(2,1)S(1)}, u32[]{:S(2)}, u32[]{:S(2)}) collective-permute-start(bf16[4,264,128]{2,1,0:T(8,128)(2,1)S(1)} %collective-permute-done.10.refs_5_), channel_id=1, source_target_pairs={{0,4},{2,6},{4,12},{6,14},{8,0},{10,2},{12,20},{14,22},{16,8},{18,... | collective-permute-start | bytes 811016 | tf_op jit(solution)/shard_map/ppermute | solution.py:470
  26.9 19.5 %collective-permute-start.7 = (bf16[4,264,128]{2,1,0:T(8,128)(2,1)S(1)}, bf16[4,264,128]{2,1,0:T(8,128)(2,1)S(1)}, u32[]{:S(2)}, u32[]{:S(2)}) collective-permute-start(bf16[4,264,128]{2,1,0:T(8,128)(2,1)S(1)} %collective-permute-done.6.refs_3_), channel_id=1, source_target_pairs={{0,8},{2,10},{4,0},{6,2},{8,16},{10,18},{12,4},{14,6},{16,24},{18,... | collective-permute-start | bytes 811016 | tf_op jit(solution)/shard_map/ppermute | solution.py:470
  32.4 11.6 %collective-permute-start.15 = (bf16[4,264,128]{2,1,0:T(8,128)(2,1)S(1)}, bf16[4,264,128]{2,1,0:T(8,128)(2,1)S(1)}, u32[]{:S(2)}, u32[]{:S(2)}) collective-permute-start(bf16[4,264,128]{2,1,0:T(8,128)(2,1)S(1)} %collective-permute-done.14.refs_2_), channel_id=1, source_target_pairs={{0,8},{2,10},{4,0},{6,2},{8,16},{10,18},{12,4},{14,6},{16,24},{18,... | collective-permute-start | bytes 811016 | tf_op jit(solution)/shard_map/ppermute | solution.py:470
  33.6 11.6 %collective-permute-start.19 = (bf16[4,264,128]{2,1,0:T(8,128)(2,1)S(1)}, bf16[4,264,128]{2,1,0:T(8,128)(2,1)S(1)}, u32[]{:S(2)}, u32[]{:S(2)}) collective-permute-start(bf16[4,264,128]{2,1,0:T(8,128)(2,1)S(1)} %collective-permute-done.18.refs_4_), channel_id=1, source_target_pairs={{0,4},{2,6},{4,12},{6,14},{8,0},{10,2},{12,20},{14,22},{16,8},{18,... | collective-permute-start | bytes 811016 | tf_op jit(solution)/shard_map/ppermute | solution.py:470
  44.0 6.8 %collective-permute-start.16 = (bf16[4,264,128]{2,1,0:T(8,128)(2,1)S(1)}, bf16[4,264,128]{2,1,0:T(8,128)(2,1)S(1)}, u32[]{:S(2)}, u32[]{:S(2)}) collective-permute-start(bf16[4,264,128]{2,1,0:T(8,128)(2,1)S(1)} %collective-permute-done.15.refs_0_), channel_id=1, source_target_pairs={{0,8},{2,10},{4,0},{6,2},{8,16},{10,18},{12,4},{14,6},{16,24},{18,... | collective-permute-start | bytes 811016 | tf_op jit(solution)/shard_map/ppermute | solution.py:470
  45.2 7.1 %collective-permute-start.20 = (bf16[4,264,128]{2,1,0:T(8,128)(2,1)S(1)}, bf16[4,264,128]{2,1,0:T(8,128)(2,1)S(1)}, u32[]{:S(2)}, u32[]{:S(2)}) collective-permute-start(bf16[4,264,128]{2,1,0:T(8,128)(2,1)S(1)} %collective-permute-done.19.refs_2_), channel_id=1, source_target_pairs={{0,4},{2,6},{4,12},{6,14},{8,0},{10,2},{12,20},{14,22},{16,8},{18,... | collective-permute-start | bytes 811016 | tf_op jit(solution)/shard_map/ppermute | solution.py:470
  45.5 12.6 %collective-permute-start.12 = (bf16[4,264,128]{2,1,0:T(8,128)(2,1)S(1)}, bf16[4,264,128]{2,1,0:T(8,128)(2,1)S(1)}, u32[]{:S(2)}, u32[]{:S(2)}) collective-permute-start(bf16[4,264,128]{2,1,0:T(8,128)(2,1)S(1)} %collective-permute-done.11.refs_3_), channel_id=1, source_target_pairs={{0,4},{2,6},{4,12},{6,14},{8,0},{10,2},{12,20},{14,22},{16,8},{18,... | collective-permute-start | bytes 811016 | tf_op jit(solution)/shard_map/ppermute | solution.py:470
  46.3 11.8 %collective-permute-start.8 = (bf16[4,264,128]{2,1,0:T(8,128)(2,1)S(1)}, bf16[4,264,128]{2,1,0:T(8,128)(2,1)S(1)}, u32[]{:S(2)}, u32[]{:S(2)}) collective-permute-start(bf16[4,264,128]{2,1,0:T(8,128)(2,1)S(1)} %collective-permute-done.7.refs_1_), channel_id=1, source_target_pairs={{0,8},{2,10},{4,0},{6,2},{8,16},{10,18},{12,4},{14,6},{16,24},{18,... | collective-permute-start | bytes 811016 | tf_op jit(solution)/shard_map/ppermute | solution.py:470
  50.8 12.0 %collective-permute-start.17 = (bf16[2,264,128]{2,1,0:T(8,128)(2,1)S(1)}, bf16[2,264,128]{2,1,0:T(8,128)(2,1)S(1)}, u32[]{:S(2)}, u32[]{:S(2)}) collective-permute-start(bf16[2,264,128]{2,1,0:T(8,128)(2,1)S(1)} %slice.28), channel_id=1, source_target_pairs={{0,8},{2,10},{4,0},{6,2},{8,16},{10,18},{12,4},{14,6},{16,24},{18,... | collective-permute-start | bytes 405512 | tf_op jit(solution)/shard_map/ppermute | solution.py:479
  52.2 10.6 %collective-permute-start.21 = (bf16[2,264,128]{2,1,0:T(8,128)(2,1)S(1)}, bf16[2,264,128]{2,1,0:T(8,128)(2,1)S(1)}, u32[]{:S(2)}, u32[]{:S(2)}) collective-permute-start(bf16[2,264,128]{2,1,0:T(8,128)(2,1)S(1)} %slice.29), channel_id=1, source_target_pairs={{0,4},{2,6},{4,12},{6,14},{8,0},{10,2},{12,20},{14,22},{16,8},{18,... | collective-permute-start | bytes 405512 | tf_op jit(solution)/shard_map/ppermute | solution.py:479
  58.0 6.5 %collective-permute-start.13 = (bf16[2,264,128]{2,1,0:T(8,128)(2,1)S(1)}, bf16[2,264,128]{2,1,0:T(8,128)(2,1)S(1)}, u32[]{:S(2)}, u32[]{:S(2)}) collective-permute-start(bf16[2,264,128]{2,1,0:T(8,128)(2,1)S(1)} %slice.27), channel_id=1, source_target_pairs={{0,4},{2,6},{4,12},{6,14},{8,0},{10,2},{12,20},{14,22},{16,8},{18,... | collective-permute-start | bytes 405512 | tf_op jit(solution)/shard_map/ppermute | solution.py:479
  58.1 6.4 %collective-permute-start.9 = (bf16[2,264,128]{2,1,0:T(8,128)(2,1)S(1)}, bf16[2,264,128]{2,1,0:T(8,128)(2,1)S(1)}, u32[]{:S(2)}, u32[]{:S(2)}) collective-permute-start(bf16[2,264,128]{2,1,0:T(8,128)(2,1)S(1)} %slice.26), channel_id=1, source_target_pairs={{0,8},{2,10},{4,0},{6,2},{8,16},{10,18},{12,4},{14,6},{16,24},{18,... | collective-permute-start | bytes 405512 | tf_op jit(solution)/shard_map/ppermute | solution.py:479
  64.7 8.8 %collective-permute-start.22 = (bf16[16,128,128]{2,1,0:T(8,128)(2,1)S(1)}, bf16[16,128,128]{2,1,0:T(8,128)(2,1)S(1)}, u32[]{:S(2)}, u32[]{:S(2)}) collective-permute-start(bf16[16,128,128]{2,1,0:T(8,128)(2,1)S(1)} %get-tuple-element.49), channel_id=1, source_target_pairs={{0,2},{2,0},{4,6},{6,4},{8,10},{10,8},{12,14},{14,12},{16,18},{18,... | collective-permute-start | bytes 1572872 | tf_op jit(solution)/shard_map/ppermute | solution.py:537
  71.9 1.6 %collective-permute-start.23 = (f32[16,8,128]{2,1,0:T(8,128)S(1)}, f32[16,8,128]{2,1,0:T(8,128)S(1)}, u32[]{:S(2)}, u32[]{:S(2)}) collective-permute-start(f32[16,8,128]{2,1,0:T(8,128)S(1)} %get-tuple-element.50), channel_id=1, source_target_pairs={{0,2},{2,0},{4,6},{6,4},{8,10},{10,8},{12,14},{14,12},{16,18},{18,... | collective-permute-start | bytes 196616 | tf_op jit(solution)/shard_map/ppermute | solution.py:537
  72.0 1.6 %copy-start = (bf16[128,2048]{1,0:T(8,128)(2,1)S(1)}, bf16[128,2048]{1,0:T(8,128)(2,1)}, u32[]{:S(2)}) copy-start(bf16[128,2048]{1,0:T(8,128)(2,1)} %x_ref.1) | copy-start | bytes 1572868
  72.0 1.6 %copy-start.1 = (f32[128]{0:T(128)S(1)}, f32[128]{0:T(128)}, u32[]{:S(2)}) copy-start(f32[128]{0:T(128)} %param.12) | copy-start | bytes 1540

commit v5 on v4

--- a/solution.py
+++ b/solution.py
@@ -115,8 +115,6 @@
     for d in range(devices):
         count[2 * d] = 0
         count[2 * d + 1] = 0
-        for n in range(slots):
-            codes[d * width + n] = 0
 
     def body(t, carry):
         row, col = rows_ref[t], cols_ref[t]
@@ -140,7 +138,7 @@
         codes[owner * width + at] = (row_at * (4 * blocks) + spot) * groups + group
         return carry
 
-    lax.fori_loop(0, rows_ref.shape[0], body, 0)
+    lax.fori_loop(0, rows_ref.shape[0], body, 0, unroll=4)
     lane = lax.broadcasted_iota(jnp.int32, words, 1)
     for d in range(devices):
         here = jnp.zeros(words, jnp.int32)
@@ -339,7 +337,7 @@
         mixed = mixed + sums_ref[b].astype(F32).reshape(heads, HD, tile) * c2
         at = slice(b * tile, (b + 1) * tile)
         v = mixed.reshape(dims, tile) + x_ref[:, at].astype(F32) + bias
-        out_ref[:, at] = jnp.where(v > 0, v, jnp.exp(jnp.minimum(v, 0.0)) - 1.0).astype(BF16)
+        out_ref[:, at] = jnp.where(v > 0, v, jnp.exp(v) - 1.0).astype(BF16)
         if (b + 1) % share == 0:
             at = slice((b + 1 - share) * tile, (b + 1) * tile)
             copies.append(pltpu.make_async_copy(out_ref.at[:, at], whole_ref.at[:, at], sems.at[b // share]))
@@ -542,7 +540,7 @@
         jax.ShapeDtypeStruct((dims, nodes), BF16),
         (near(state), *[near(v) for v in back], node_feats, out_bias.reshape(1, dims)),
         out_specs=anywhere,
-        scratch=[pltpu.VMEM((dims, nodes), BF16), pltpu.SemaphoreType.DMA((math.gcd(blocks, 4),))],
+        scratch=[pltpu.VMEM((dims, nodes), BF16), pltpu.SemaphoreType.DMA((math.gcd(blocks, 8),))],
     )
 
 

time: 76.3 us -> 76 us (level)
  no operation moved by 1% of the time
where the time goes in v5:
time: 76 us; the launch traced here: 74.7 us
  starting transfers between devices  24.3 us (32%)
  waiting for transfers between devices  21.9 us (29%)
  Pallas kernels  16.5 us (22%)
  blocking collectives  11.5 us (15%)
    ppermute x12, waiting for transfers between devices, local(): lax.ppermute(going[way], 'dp', right if way[0] == 'r' else left)  19.5 us
    pallas_call x14, Pallas kernels, call(): pl.pallas_call(kernel, out_shape=outs, in_specs=in_specs or [VMEM] * len(...  16.5 us
    all_to_all x1, blocking collectives, local(): got = lax.all_to_all(packed, 'dp', split_axis=0, concat_axis=0, tiled=True)  11.5 us
    ppermute x12, starting transfers between devices, local(): lax.ppermute(going[way], 'dp', right if way[0] == 'r' else left)  9.07 us
    ppermute x2, starting transfers between devices, local(): back = (lax.ppermute(sums, 'dp', swap), lax.ppermute(levels, 'dp', swap))  7.21 us
    ppermute x4, starting transfers between devices, local(): both.append(lax.ppermute(going[w + p][cut], 'dp', pairs))  3.11 us
    ppermute x2, starting transfers between devices, local(): got_other = [lax.ppermute(v, 'dp', swap) for v in got]  1.76 us
    ppermute x2, starting transfers between devices, local(): inputs = [[x, lax.ppermute(x, 'mp', flip)] for x in cuts]  1.53 us
  transfers between devices with their start and end apart: 24, of which 8 were waited for; matrix products, arithmetic and copies ran while one was open for 0% of the time, Pallas kernels for 19%

profile of v5, /device:TPU:11, one launch (start us, length us, event | category | flops | bytes accessed | tf_op | source)
XLA Modules:
  0.0 74.7 jit_solution(6902826087691789917)
XLA Ops:
  0.0 1.1 %shard_map.82 = (bf16[128,1024]{1,0:T(8,128)(2,1)S(1)}, bf16[128,1024]{1,0:T(8,128)(2,1)S(1)}, bf16[128,256]{1,0:T(8,128)(2,1)S(1)}, f32[1,128]{1,0:T(1,128)S(1)...) custom-call(bf16[128,2048]{1,0:T(8,128)(2,1)} %x_ref.1, ...), custom_call_target="tpu_custom_call" | custom-call | flops 1000000 | tf_op jit(solution)/shard_map/pallas_call | solution.py:350
  1.1 1.3 %collective-permute-start.4 = (bf16[128,1024]{1,0:T(8,128)(2,1)S(1)}, bf16[128,1024]{1,0:T(8,128)(2,1)S(1)}, u32[]{:S(2)}, u32[]{:S(2)}) collective-permute-start(bf16[128,1024]{1,0:T(8,128)(2,1)S(1)} %get-tuple-element.37.refs_0_), channel_id=1, source_target_pairs={{0,1},{1,0},{2,3},{3,2},{4,5},{5,4},{6,7},{7,6},{8,9},{9,8},{10,11... | collective-permute-start | bytes 786440 | tf_op jit(solution)/shard_map/ppermute | solution.py:422
  2.7 1.2 %shard_map.83 = s32[16,5,2,128]{3,2,1,0:T(2,128)} custom-call(s32[1]{0:T(128)} %bitcast.1.mp_ref, s32[32]{0:T(128)S(4)} %get-tuple-element.28.rows_ref, s32[32]{0:T(128)S(4)} %get-tuple-element.29.cols_ref, s32[32,4,128]{2,1,0:T(4,128)S(1)} %get-tuple-element.30.masks_ref), custom_call_target="tpu_custom_call" | custom-call | flops 1000000 | tf_op jit(solution)/shard_map/pallas_call | solution.py:350
  3.9 11.5 %all_to_all.5 = s32[16,5,2,128]{3,2,1,0:T(2,128)S(1)} all-to-all(s32[16,5,2,128]{3,2,1,0:T(2,128)} %shard_map.83), channel_id=1, replica_groups=mesh['dp'=16,'mp'=2] {'dp'}, dimensions={0} | all-to-all | bytes 163840 | tf_op jit(solution)/shard_map/all_to_all | solution.py:439
  15.4 1.2 %collective-permute-start.1 = (s32[80,2,128]{2,1,0:T(2,128)S(1)}, s32[80,2,128]{2,1,0:T(2,128)S(1)}, u32[]{:S(2)}, u32[]{:S(2)}) collective-permute-start(s32[80,2,128]{2,1,0:T(2,128)S(1)} %bitcast.12), channel_id=1, source_target_pairs={{0,1},{1,0},{2,3},{3,2},{4,5},{5,4},{6,7},{7,6},{8,9},{9,8},{10,11... | collective-permute-start | bytes 245768 | tf_op jit(solution)/shard_map/ppermute | solution.py:442
  16.6 0.6 collective-permute-start
  17.8 0.5 shard_map.87
  18.8 1.1 %collective-permute-start.6 = (bf16[4,264,128]{2,1,0:T(8,128)(2,1)S(1)}, bf16[4,264,128]{2,1,0:T(8,128)(2,1)S(1)}, u32[]{:S(2)}, u32[]{:S(2)}) collective-permute-start(bf16[4,264,128]{2,1,0:T(8,128)(2,1)S(1)} %get-tuple-element.40.refs_1_), channel_id=1, source_target_pairs={{0,8},{2,10},{4,0},{6,2},{8,16},{10,18},{12,4},{14,6},{16,24},{18,... | collective-permute-start | bytes 811016 | tf_op jit(solution)/shard_map/ppermute | solution.py:468
  19.8 1.4 %collective-permute-start.14 = (bf16[4,264,128]{2,1,0:T(8,128)(2,1)S(1)}, bf16[4,264,128]{2,1,0:T(8,128)(2,1)S(1)}, u32[]{:S(2)}, u32[]{:S(2)}) collective-permute-start(bf16[4,264,128]{2,1,0:T(8,128)(2,1)S(1)} %get-tuple-element.41.refs_0_), channel_id=1, source_target_pairs={{0,8},{2,10},{4,0},{6,2},{8,16},{10,18},{12,4},{14,6},{16,24},{18,... | collective-permute-start | bytes 811016 | tf_op jit(solution)/shard_map/ppermute | solution.py:468
  21.3 1.1 %collective-permute-start.2 = (s32[80,2,128]{2,1,0:T(2,128)S(1)}, s32[80,2,128]{2,1,0:T(2,128)S(1)}, u32[]{:S(2)}, u32[]{:S(2)}) collective-permute-start(s32[80,2,128]{2,1,0:T(2,128)S(1)} %collective-permute-done.1.refs_1_), channel_id=1, source_target_pairs={{0,2},{2,0},{4,6},{6,4},{8,10},{10,8},{12,14},{14,12},{16,18},{18,... | collective-permute-start | bytes 245768 | tf_op jit(solution)/shard_map/ppermute | solution.py:443
  22.4 0.9 %collective-permute-done.2.refs_3_ = s32[80,2,128]{2,1,0:T(2,128)S(1)} collective-permute-done((s32[80,2,128]{2,1,0:T(2,128)S(1)}, s32[80,2,128]{2,1,0:T(2,128)S(1)}, u32[]{:S(2)}, u32[]{:S(2)}) %collective-permute-start.2) | collective-permute-done | bytes 81952 | tf_op jit(solution)/shard_map/ppermute | solution.py:443
  23.9 1.5 %shard_map.84 = (s32[1088]{0:T(1024)S(4)}, s32[8]{0:T(128)S(4)}) custom-call(s32[1]{0:T(128)} %bitcast.core_ref, s32[96]{0:T(128)S(1)} %reshape_squeeze.6.own_ids, s32[96]{0:T(128)S(1)} %reshape_squeeze.7.other_ids), custom_call_target="tpu_custom_call" | custom-call | flops 1000000 | tf_op jit(solution)/shard_map/pallas_call | solution.py:350
  25.5 0.9 %collective-permute-done.10.refs_5_ = bf16[4,264,128]{2,1,0:T(8,128)(2,1)S(1)} collective-permute-done((bf16[4,264,128]{2,1,0:T(8,128)(2,1)S(1)}, bf16[4,264,128]{2,1,0:T(8,128)(2,1)S(1)}, u32[]{:S(2)}, u32[]{:S(2)}) %collective-permute-start.10) | collective-permute-done | bytes 270368 | tf_op jit(solution)/shard_map/ppermute | solution.py:468
  26.7 1.3 %collective-permute-start.7 = (bf16[4,264,128]{2,1,0:T(8,128)(2,1)S(1)}, bf16[4,264,128]{2,1,0:T(8,128)(2,1)S(1)}, u32[]{:S(2)}, u32[]{:S(2)}) collective-permute-start(bf16[4,264,128]{2,1,0:T(8,128)(2,1)S(1)} %collective-permute-done.6.refs_3_), channel_id=1, source_target_pairs={{0,8},{2,10},{4,0},{6,2},{8,16},{10,18},{12,4},{14,6},{16,24},{18,... | collective-permute-start | bytes 811016 | tf_op jit(solution)/shard_map/ppermute | solution.py:468
  28.0 4.2 %collective-permute-done.14.refs_2_ = bf16[4,264,128]{2,1,0:T(8,128)(2,1)S(1)} collective-permute-done((bf16[4,264,128]{2,1,0:T(8,128)(2,1)S(1)}, bf16[4,264,128]{2,1,0:T(8,128)(2,1)S(1)}, u32[]{:S(2)}, u32[]{:S(2)}) %collective-permute-start.14) | collective-permute-done | bytes 270368 | tf_op jit(solution)/shard_map/ppermute | solution.py:468
  32.2 1.2 %collective-permute-start.15 = (bf16[4,264,128]{2,1,0:T(8,128)(2,1)S(1)}, bf16[4,264,128]{2,1,0:T(8,128)(2,1)S(1)}, u32[]{:S(2)}, u32[]{:S(2)}) collective-permute-start(bf16[4,264,128]{2,1,0:T(8,128)(2,1)S(1)} %collective-permute-done.14.refs_2_), channel_id=1, source_target_pairs={{0,8},{2,10},{4,0},{6,2},{8,16},{10,18},{12,4},{14,6},{16,24},{18,... | collective-permute-start | bytes 811016 | tf_op jit(solution)/shard_map/ppermute | solution.py:468
  33.7 3.1 %shard_map.88.refs_4_ = f32[32,136,128]{2,1,0:T(8,128)S(1)} custom-call(s32[1088]{0:T(1024)S(4)} %get-tuple-element.31.list_ref, s32[8]{0:T(128)S(4)} %get-tuple-element.32.count_ref, s32[160,4,128]{2,1,0:T(4,128)S(1)} %shard_map.85.masks_ref, f32[16,8,128]{2,1,0:T(8,128)S(1)} %get-tuple-element.39.own_sc, ...), custom_call_target="tpu_custom_call" | custom-call | flops 8000000000 | tf_op jit(solution)/shard_map/pallas_call | solution.py:350
  36.8 7.0 %collective-permute-done.15.refs_0_ = bf16[4,264,128]{2,1,0:T(8,128)(2,1)S(1)} collective-permute-done((bf16[4,264,128]{2,1,0:T(8,128)(2,1)S(1)}, bf16[4,264,128]{2,1,0:T(8,128)(2,1)S(1)}, u32[]{:S(2)}, u32[]{:S(2)}) %collective-permute-start.15) | collective-permute-done | bytes 270368 | tf_op jit(solution)/shard_map/ppermute | solution.py:468
  43.8 1.2 %collective-permute-start.16 = (bf16[4,264,128]{2,1,0:T(8,128)(2,1)S(1)}, bf16[4,264,128]{2,1,0:T(8,128)(2,1)S(1)}, u32[]{:S(2)}, u32[]{:S(2)}) collective-permute-start(bf16[4,264,128]{2,1,0:T(8,128)(2,1)S(1)} %collective-permute-done.15.refs_0_), channel_id=1, source_target_pairs={{0,8},{2,10},{4,0},{6,2},{8,16},{10,18},{12,4},{14,6},{16,24},{18,... | collective-permute-start | bytes 811016 | tf_op jit(solution)/shard_map/ppermute | solution.py:468
  45.3 0.9 %collective-permute-start.12 = (bf16[4,264,128]{2,1,0:T(8,128)(2,1)S(1)}, bf16[4,264,128]{2,1,0:T(8,128)(2,1)S(1)}, u32[]{:S(2)}, u32[]{:S(2)}) collective-permute-start(bf16[4,264,128]{2,1,0:T(8,128)(2,1)S(1)} %collective-permute-done.11.refs_3_), channel_id=1, source_target_pairs={{0,4},{2,6},{4,12},{6,14},{8,0},{10,2},{12,20},{14,22},{16,8},{18,... | collective-permute-start | bytes 811016 | tf_op jit(solution)/shard_map/ppermute | solution.py:468
  46.1 0.6 collective-permute-start.8
  46.8 2.0 %shard_map.89.refs_2_ = f32[32,136,128]{2,1,0:T(8,128)S(1)} custom-call(s32[1088]{0:T(1024)S(4)} %get-tuple-element.31.list_ref, s32[8]{0:T(128)S(4)} %get-tuple-element.32.count_ref, s32[160,4,128]{2,1,0:T(4,128)S(1)} %shard_map.85.masks_ref, f32[16,8,128]{2,1,0:T(8,128)S(1)} %get-tuple-element.39.own_sc, ...), custom_call_target="tpu_custom_call", output_to_operand_aliasing={{}: (10, {})} | custom-call | flops 8000000000 | tf_op jit(solution)/shard_map/pallas_call | solution.py:350
  48.8 1.8 %collective-permute-done.16.refs_0_ = bf16[4,264,128]{2,1,0:T(8,128)(2,1)S(1)} collective-permute-done((bf16[4,264,128]{2,1,0:T(8,128)(2,1)S(1)}, bf16[4,264,128]{2,1,0:T(8,128)(2,1)S(1)}, u32[]{:S(2)}, u32[]{:S(2)}) %collective-permute-start.16) | collective-permute-done | bytes 270368 | tf_op jit(solution)/shard_map/ppermute | solution.py:468
  50.6 1.3 %collective-permute-start.17 = (bf16[2,264,128]{2,1,0:T(8,128)(2,1)S(1)}, bf16[2,264,128]{2,1,0:T(8,128)(2,1)S(1)}, u32[]{:S(2)}, u32[]{:S(2)}) collective-permute-start(bf16[2,264,128]{2,1,0:T(8,128)(2,1)S(1)} %slice.28), channel_id=1, source_target_pairs={{0,8},{2,10},{4,0},{6,2},{8,16},{10,18},{12,4},{14,6},{16,24},{18,... | collective-permute-start | bytes 405512 | tf_op jit(solution)/shard_map/ppermute | solution.py:477
  52.2 5.6 %collective-permute-done.12.refs_1_ = bf16[4,264,128]{2,1,0:T(8,128)(2,1)S(1)} collective-permute-done((bf16[4,264,128]{2,1,0:T(8,128)(2,1)S(1)}, bf16[4,264,128]{2,1,0:T(8,128)(2,1)S(1)}, u32[]{:S(2)}, u32[]{:S(2)}) %collective-permute-start.12) | collective-permute-done | bytes 270368 | tf_op jit(solution)/shard_map/ppermute | solution.py:468
  57.9 1.6 %collective-permute-start.9 = (bf16[2,264,128]{2,1,0:T(8,128)(2,1)S(1)}, bf16[2,264,128]{2,1,0:T(8,128)(2,1)S(1)}, u32[]{:S(2)}, u32[]{:S(2)}) collective-permute-start(bf16[2,264,128]{2,1,0:T(8,128)(2,1)S(1)} %slice.26), channel_id=1, source_target_pairs={{0,8},{2,10},{4,0},{6,2},{8,16},{10,18},{12,4},{14,6},{16,24},{18,... | collective-permute-start | bytes 405512 | tf_op jit(solution)/shard_map/ppermute | solution.py:477
  59.5 2.0 %shard_map.90.refs_2_ = f32[32,136,128]{2,1,0:T(8,128)S(1)} custom-call(s32[1088]{0:T(1024)S(4)} %get-tuple-element.31.list_ref, s32[8]{0:T(128)S(4)} %get-tuple-element.32.count_ref, s32[160,4,128]{2,1,0:T(4,128)S(1)} %shard_map.85.masks_ref, f32[16,8,128]{2,1,0:T(8,128)S(1)} %get-tuple-element.39.own_sc, ...), custom_call_target="tpu_custom_call", output_to_operand_aliasing={{}: (8, {})} | custom-call | flops 8000000000 | tf_op jit(solution)/shard_map/pallas_call | solution.py:350
  61.5 1.1 %shard_map.91.refs_2_ = f32[32,136,128]{2,1,0:T(8,128)S(1)} custom-call(s32[1088]{0:T(1024)S(4)} %get-tuple-element.31.list_ref, s32[8]{0:T(128)S(4)} %get-tuple-element.32.count_ref, s32[160,4,128]{2,1,0:T(4,128)S(1)} %shard_map.85.masks_ref, f32[16,8,128]{2,1,0:T(8,128)S(1)} %get-tuple-element.39.own_sc, ...), custom_call_target="tpu_custom_call", output_to_operand_aliasing={{}: (8, {})} | custom-call | flops 8000000000 | tf_op jit(solution)/shard_map/pallas_call | solution.py:350
  62.7 1.7 %shard_map.92.refs_2_ = f32[32,136,128]{2,1,0:T(8,128)S(1)} custom-call(s32[1088]{0:T(1024)S(4)} %get-tuple-element.31.list_ref, s32[8]{0:T(128)S(4)} %get-tuple-element.32.count_ref, s32[160,4,128]{2,1,0:T(4,128)S(1)} %shard_map.85.masks_ref, f32[16,8,128]{2,1,0:T(8,128)S(1)} %get-tuple-element.39.own_sc, ...), custom_call_target="tpu_custom_call", output_to_operand_aliasing={{}: (8, {})} | custom-call | flops 8000000000 | tf_op jit(solution)/shard_map/pallas_call | solution.py:350
  64.6 7.1 %collective-permute-start.22 = (bf16[16,128,128]{2,1,0:T(8,128)(2,1)S(1)}, bf16[16,128,128]{2,1,0:T(8,128)(2,1)S(1)}, u32[]{:S(2)}, u32[]{:S(2)}) collective-permute-start(bf16[16,128,128]{2,1,0:T(8,128)(2,1)S(1)} %get-tuple-element.49), channel_id=1, source_target_pairs={{0,2},{2,0},{4,6},{6,4},{8,10},{10,8},{12,14},{14,12},{16,18},{18,... | collective-permute-start | bytes 1572872 | tf_op jit(solution)/shard_map/ppermute | solution.py:535
  71.9 1.4 %collective-permute-done.23.levels_ref = f32[16,8,128]{2,1,0:T(8,128)S(1)} collective-permute-done((f32[16,8,128]{2,1,0:T(8,128)S(1)}, f32[16,8,128]{2,1,0:T(8,128)S(1)}, u32[]{:S(2)}, u32[]{:S(2)}) %collective-permute-start.23) | collective-permute-done | bytes 65568 | tf_op jit(solution)/shard_map/ppermute | solution.py:535
  73.3 1.4 %shard_map.95 = bf16[128,2048]{1,0:T(8,128)(2,1)} custom-call(f32[32,136,128]{2,1,0:T(8,128)S(1)} %shard_map.94.state_ref, bf16[16,128,128]{2,1,0:T(8,128)(2,1)S(1)} %collective-permute-done.22.sums_ref, f32[16,8,128]{2,1,0:T(8,128)S(1)} %collective-permute-done.23.levels_ref, bf16[128,2048]{1,0:T(8,128)(2,1)S(1)} %copy-done, f32[1,128]{1,0:T(1,128)S(1)} %bitcast.16), custom_call_target="tpu_custom_call" | custom-call | flops 1000000 | tf_op jit(solution)/shard_map/pallas_call | solution.py:350
  (43 shorter events, 3.5 us)
Async XLA Ops:
  1.1 16.1 %collective-permute-start.4 = (bf16[128,1024]{1,0:T(8,128)(2,1)S(1)}, bf16[128,1024]{1,0:T(8,128)(2,1)S(1)}, u32[]{:S(2)}, u32[]{:S(2)}) collective-permute-start(bf16[128,1024]{1,0:T(8,128)(2,1)S(1)} %get-tuple-element.37.refs_0_), channel_id=1, source_target_pairs={{0,1},{1,0},{2,3},{3,2},{4,5},{5,4},{6,7},{7,6},{8,9},{9,8},{10,11... | collective-permute-start | bytes 786440 | tf_op jit(solution)/shard_map/ppermute | solution.py:422
  2.4 15.4 %collective-permute-start.3 = (bf16[128,1024]{1,0:T(8,128)(2,1)S(1)}, bf16[128,1024]{1,0:T(8,128)(2,1)S(1)}, u32[]{:S(2)}, u32[]{:S(2)}) collective-permute-start(bf16[128,1024]{1,0:T(8,128)(2,1)S(1)} %get-tuple-element.36.refs_0_), channel_id=1, source_target_pairs={{0,1},{1,0},{2,3},{3,2},{4,5},{5,4},{6,7},{7,6},{8,9},{9,8},{10,11... | collective-permute-start | bytes 786440 | tf_op jit(solution)/shard_map/ppermute | solution.py:422
  15.4 5.8 %collective-permute-start.1 = (s32[80,2,128]{2,1,0:T(2,128)S(1)}, s32[80,2,128]{2,1,0:T(2,128)S(1)}, u32[]{:S(2)}, u32[]{:S(2)}) collective-permute-start(s32[80,2,128]{2,1,0:T(2,128)S(1)} %bitcast.12), channel_id=1, source_target_pairs={{0,1},{1,0},{2,3},{3,2},{4,5},{5,4},{6,7},{7,6},{8,9},{9,8},{10,11... | collective-permute-start | bytes 245768 | tf_op jit(solution)/shard_map/ppermute | solution.py:442
  16.6 4.7 %collective-permute-start = (s32[80,2,128]{2,1,0:T(2,128)S(1)}, s32[80,2,128]{2,1,0:T(2,128)S(1)}, u32[]{:S(2)}, u32[]{:S(2)}) collective-permute-start(s32[80,2,128]{2,1,0:T(2,128)S(1)} %bitcast.13), channel_id=1, source_target_pairs={{0,2},{2,0},{4,6},{6,4},{8,10},{10,8},{12,14},{14,12},{16,18},{18,... | collective-permute-start | bytes 245768 | tf_op jit(solution)/shard_map/ppermute | solution.py:443
  18.3 8.1 %collective-permute-start.10 = (bf16[4,264,128]{2,1,0:T(8,128)(2,1)S(1)}, bf16[4,264,128]{2,1,0:T(8,128)(2,1)S(1)}, u32[]{:S(2)}, u32[]{:S(2)}) collective-permute-start(bf16[4,264,128]{2,1,0:T(8,128)(2,1)S(1)} %get-tuple-element.40.refs_1_), channel_id=1, source_target_pairs={{0,4},{2,6},{4,12},{6,14},{8,0},{10,2},{12,20},{14,22},{16,8},{18,... | collective-permute-start | bytes 811016 | tf_op jit(solution)/shard_map/ppermute | solution.py:468
  18.8 7.9 %collective-permute-start.6 = (bf16[4,264,128]{2,1,0:T(8,128)(2,1)S(1)}, bf16[4,264,128]{2,1,0:T(8,128)(2,1)S(1)}, u32[]{:S(2)}, u32[]{:S(2)}) collective-permute-start(bf16[4,264,128]{2,1,0:T(8,128)(2,1)S(1)} %get-tuple-element.40.refs_1_), channel_id=1, source_target_pairs={{0,8},{2,10},{4,0},{6,2},{8,16},{10,18},{12,4},{14,6},{16,24},{18,... | collective-permute-start | bytes 811016 | tf_op jit(solution)/shard_map/ppermute | solution.py:468
  19.8 12.4 %collective-permute-start.14 = (bf16[4,264,128]{2,1,0:T(8,128)(2,1)S(1)}, bf16[4,264,128]{2,1,0:T(8,128)(2,1)S(1)}, u32[]{:S(2)}, u32[]{:S(2)}) collective-permute-start(bf16[4,264,128]{2,1,0:T(8,128)(2,1)S(1)} %get-tuple-element.41.refs_0_), channel_id=1, source_target_pairs={{0,8},{2,10},{4,0},{6,2},{8,16},{10,18},{12,4},{14,6},{16,24},{18,... | collective-permute-start | bytes 811016 | tf_op jit(solution)/shard_map/ppermute | solution.py:468
  21.2 12.1 %collective-permute-start.18 = (bf16[4,264,128]{2,1,0:T(8,128)(2,1)S(1)}, bf16[4,264,128]{2,1,0:T(8,128)(2,1)S(1)}, u32[]{:S(2)}, u32[]{:S(2)}) collective-permute-start(bf16[4,264,128]{2,1,0:T(8,128)(2,1)S(1)} %get-tuple-element.41.refs_0_), channel_id=1, source_target_pairs={{0,4},{2,6},{4,12},{6,14},{8,0},{10,2},{12,20},{14,22},{16,8},{18,... | collective-permute-start | bytes 811016 | tf_op jit(solution)/shard_map/ppermute | solution.py:468
  21.3 2.0 %collective-permute-start.2 = (s32[80,2,128]{2,1,0:T(2,128)S(1)}, s32[80,2,128]{2,1,0:T(2,128)S(1)}, u32[]{:S(2)}, u32[]{:S(2)}) collective-permute-start(s32[80,2,128]{2,1,0:T(2,128)S(1)} %collective-permute-done.1.refs_1_), channel_id=1, source_target_pairs={{0,2},{2,0},{4,6},{6,4},{8,10},{10,8},{12,14},{14,12},{16,18},{18,... | collective-permute-start | bytes 245768 | tf_op jit(solution)/shard_map/ppermute | solution.py:443
  23.4 10.3 %collective-permute-start.5 = (f32[16,8,128]{2,1,0:T(8,128)S(1)}, f32[16,8,128]{2,1,0:T(8,128)S(1)}, u32[]{:S(2)}, u32[]{:S(2)}) collective-permute-start(f32[16,8,128]{2,1,0:T(8,128)S(1)} %get-tuple-element.39.own_sc), channel_id=1, source_target_pairs={{0,2},{2,0},{4,6},{6,4},{8,10},{10,8},{12,14},{14,12},{16,18},{18,... | collective-permute-start | bytes 196616 | tf_op jit(solution)/shard_map/ppermute | solution.py:462
  26.4 18.9 %collective-permute-start.11 = (bf16[4,264,128]{2,1,0:T(8,128)(2,1)S(1)}, bf16[4,264,128]{2,1,0:T(8,128)(2,1)S(1)}, u32[]{:S(2)}, u32[]{:S(2)}) collective-permute-start(bf16[4,264,128]{2,1,0:T(8,128)(2,1)S(1)} %collective-permute-done.10.refs_5_), channel_id=1, source_target_pairs={{0,4},{2,6},{4,12},{6,14},{8,0},{10,2},{12,20},{14,22},{16,8},{18,... | collective-permute-start | bytes 811016 | tf_op jit(solution)/shard_map/ppermute | solution.py:468
  26.7 19.5 %collective-permute-start.7 = (bf16[4,264,128]{2,1,0:T(8,128)(2,1)S(1)}, bf16[4,264,128]{2,1,0:T(8,128)(2,1)S(1)}, u32[]{:S(2)}, u32[]{:S(2)}) collective-permute-start(bf16[4,264,128]{2,1,0:T(8,128)(2,1)S(1)} %collective-permute-done.6.refs_3_), channel_id=1, source_target_pairs={{0,8},{2,10},{4,0},{6,2},{8,16},{10,18},{12,4},{14,6},{16,24},{18,... | collective-permute-start | bytes 811016 | tf_op jit(solution)/shard_map/ppermute | solution.py:468
  32.2 11.6 %collective-permute-start.15 = (bf16[4,264,128]{2,1,0:T(8,128)(2,1)S(1)}, bf16[4,264,128]{2,1,0:T(8,128)(2,1)S(1)}, u32[]{:S(2)}, u32[]{:S(2)}) collective-permute-start(bf16[4,264,128]{2,1,0:T(8,128)(2,1)S(1)} %collective-permute-done.14.refs_2_), channel_id=1, source_target_pairs={{0,8},{2,10},{4,0},{6,2},{8,16},{10,18},{12,4},{14,6},{16,24},{18,... | collective-permute-start | bytes 811016 | tf_op jit(solution)/shard_map/ppermute | solution.py:468
  33.4 11.6 %collective-permute-start.19 = (bf16[4,264,128]{2,1,0:T(8,128)(2,1)S(1)}, bf16[4,264,128]{2,1,0:T(8,128)(2,1)S(1)}, u32[]{:S(2)}, u32[]{:S(2)}) collective-permute-start(bf16[4,264,128]{2,1,0:T(8,128)(2,1)S(1)} %collective-permute-done.18.refs_4_), channel_id=1, source_target_pairs={{0,4},{2,6},{4,12},{6,14},{8,0},{10,2},{12,20},{14,22},{16,8},{18,... | collective-permute-start | bytes 811016 | tf_op jit(solution)/shard_map/ppermute | solution.py:468
  43.8 6.8 %collective-permute-start.16 = (bf16[4,264,128]{2,1,0:T(8,128)(2,1)S(1)}, bf16[4,264,128]{2,1,0:T(8,128)(2,1)S(1)}, u32[]{:S(2)}, u32[]{:S(2)}) collective-permute-start(bf16[4,264,128]{2,1,0:T(8,128)(2,1)S(1)} %collective-permute-done.15.refs_0_), channel_id=1, source_target_pairs={{0,8},{2,10},{4,0},{6,2},{8,16},{10,18},{12,4},{14,6},{16,24},{18,... | collective-permute-start | bytes 811016 | tf_op jit(solution)/shard_map/ppermute | solution.py:468
  45.0 7.1 %collective-permute-start.20 = (bf16[4,264,128]{2,1,0:T(8,128)(2,1)S(1)}, bf16[4,264,128]{2,1,0:T(8,128)(2,1)S(1)}, u32[]{:S(2)}, u32[]{:S(2)}) collective-permute-start(bf16[4,264,128]{2,1,0:T(8,128)(2,1)S(1)} %collective-permute-done.19.refs_2_), channel_id=1, source_target_pairs={{0,4},{2,6},{4,12},{6,14},{8,0},{10,2},{12,20},{14,22},{16,8},{18,... | collective-permute-start | bytes 811016 | tf_op jit(solution)/shard_map/ppermute | solution.py:468
  45.3 12.6 %collective-permute-start.12 = (bf16[4,264,128]{2,1,0:T(8,128)(2,1)S(1)}, bf16[4,264,128]{2,1,0:T(8,128)(2,1)S(1)}, u32[]{:S(2)}, u32[]{:S(2)}) collective-permute-start(bf16[4,264,128]{2,1,0:T(8,128)(2,1)S(1)} %collective-permute-done.11.refs_3_), channel_id=1, source_target_pairs={{0,4},{2,6},{4,12},{6,14},{8,0},{10,2},{12,20},{14,22},{16,8},{18,... | collective-permute-start | bytes 811016 | tf_op jit(solution)/shard_map/ppermute | solution.py:468
  46.1 11.8 %collective-permute-start.8 = (bf16[4,264,128]{2,1,0:T(8,128)(2,1)S(1)}, bf16[4,264,128]{2,1,0:T(8,128)(2,1)S(1)}, u32[]{:S(2)}, u32[]{:S(2)}) collective-permute-start(bf16[4,264,128]{2,1,0:T(8,128)(2,1)S(1)} %collective-permute-done.7.refs_1_), channel_id=1, source_target_pairs={{0,8},{2,10},{4,0},{6,2},{8,16},{10,18},{12,4},{14,6},{16,24},{18,... | collective-permute-start | bytes 811016 | tf_op jit(solution)/shard_map/ppermute | solution.py:468
  50.6 12.0 %collective-permute-start.17 = (bf16[2,264,128]{2,1,0:T(8,128)(2,1)S(1)}, bf16[2,264,128]{2,1,0:T(8,128)(2,1)S(1)}, u32[]{:S(2)}, u32[]{:S(2)}) collective-permute-start(bf16[2,264,128]{2,1,0:T(8,128)(2,1)S(1)} %slice.28), channel_id=1, source_target_pairs={{0,8},{2,10},{4,0},{6,2},{8,16},{10,18},{12,4},{14,6},{16,24},{18,... | collective-permute-start | bytes 405512 | tf_op jit(solution)/shard_map/ppermute | solution.py:477
  52.0 10.6 %collective-permute-start.21 = (bf16[2,264,128]{2,1,0:T(8,128)(2,1)S(1)}, bf16[2,264,128]{2,1,0:T(8,128)(2,1)S(1)}, u32[]{:S(2)}, u32[]{:S(2)}) collective-permute-start(bf16[2,264,128]{2,1,0:T(8,128)(2,1)S(1)} %slice.29), channel_id=1, source_target_pairs={{0,4},{2,6},{4,12},{6,14},{8,0},{10,2},{12,20},{14,22},{16,8},{18,... | collective-permute-start | bytes 405512 | tf_op jit(solution)/shard_map/ppermute | solution.py:477
  57.8 6.5 %collective-permute-start.13 = (bf16[2,264,128]{2,1,0:T(8,128)(2,1)S(1)}, bf16[2,264,128]{2,1,0:T(8,128)(2,1)S(1)}, u32[]{:S(2)}, u32[]{:S(2)}) collective-permute-start(bf16[2,264,128]{2,1,0:T(8,128)(2,1)S(1)} %slice.27), channel_id=1, source_target_pairs={{0,4},{2,6},{4,12},{6,14},{8,0},{10,2},{12,20},{14,22},{16,8},{18,... | collective-permute-start | bytes 405512 | tf_op jit(solution)/shard_map/ppermute | solution.py:477
  57.9 6.4 %collective-permute-start.9 = (bf16[2,264,128]{2,1,0:T(8,128)(2,1)S(1)}, bf16[2,264,128]{2,1,0:T(8,128)(2,1)S(1)}, u32[]{:S(2)}, u32[]{:S(2)}) collective-permute-start(bf16[2,264,128]{2,1,0:T(8,128)(2,1)S(1)} %slice.26), channel_id=1, source_target_pairs={{0,8},{2,10},{4,0},{6,2},{8,16},{10,18},{12,4},{14,6},{16,24},{18,... | collective-permute-start | bytes 405512 | tf_op jit(solution)/shard_map/ppermute | solution.py:477
  64.6 8.8 %collective-permute-start.22 = (bf16[16,128,128]{2,1,0:T(8,128)(2,1)S(1)}, bf16[16,128,128]{2,1,0:T(8,128)(2,1)S(1)}, u32[]{:S(2)}, u32[]{:S(2)}) collective-permute-start(bf16[16,128,128]{2,1,0:T(8,128)(2,1)S(1)} %get-tuple-element.49), channel_id=1, source_target_pairs={{0,2},{2,0},{4,6},{6,4},{8,10},{10,8},{12,14},{14,12},{16,18},{18,... | collective-permute-start | bytes 1572872 | tf_op jit(solution)/shard_map/ppermute | solution.py:535
  71.7 1.6 %collective-permute-start.23 = (f32[16,8,128]{2,1,0:T(8,128)S(1)}, f32[16,8,128]{2,1,0:T(8,128)S(1)}, u32[]{:S(2)}, u32[]{:S(2)}) collective-permute-start(f32[16,8,128]{2,1,0:T(8,128)S(1)} %get-tuple-element.50), channel_id=1, source_target_pairs={{0,2},{2,0},{4,6},{6,4},{8,10},{10,8},{12,14},{14,12},{16,18},{18,... | collective-permute-start | bytes 196616 | tf_op jit(solution)/shard_map/ppermute | solution.py:535
  71.8 1.6 %copy-start = (bf16[128,2048]{1,0:T(8,128)(2,1)S(1)}, bf16[128,2048]{1,0:T(8,128)(2,1)}, u32[]{:S(2)}) copy-start(bf16[128,2048]{1,0:T(8,128)(2,1)} %x_ref.1) | copy-start | bytes 1572868
  71.8 1.6 %copy-start.1 = (f32[128]{0:T(128)S(1)}, f32[128]{0:T(128)}, u32[]{:S(2)}) copy-start(f32[128]{0:T(128)} %param.12) | copy-start | bytes 1540

commit v6 on v5

--- a/solution.py
+++ b/solution.py
@@ -306,14 +306,17 @@
         take(i, 0)
         return carry
 
+    least = 2 if short else 1
     if short:
-        lax.fori_loop(0, number, plain, 0)
-    else:
-
-        @pl.when(number > 0)
+
+        @pl.when(number == 1)
         def _():
-            ready(0, 0)
-            lax.fori_loop(0, (number + 1) >> 1, body, 0)
+            plain(0, 0)
+
+    @pl.when(number >= least)
+    def _():
+        ready(0, 0)
+        lax.fori_loop(0, (number + 1) >> 1, body, 0)
 
     if len(outs) > 1:
         outs[1][...] = state[blocks:, :dims].astype(BF16)

time: 76 us -> 76.4 us (level)
  the two profiles are of different devices: /device:TPU:11 before, /device:TPU:0 now
where the time goes in v6:
time: 76.4 us; the launch traced here: 76.2 us
  starting transfers between devices  21.8 us (29%)
  Pallas kernels  20.5 us (27%)
  waiting for transfers between devices  19.8 us (26%)
  blocking collectives  13.4 us (18%)
    pallas_call x14, Pallas kernels, call(): pl.pallas_call(kernel, out_shape=outs, in_specs=in_specs or [VMEM] * len(...  20.5 us
    ppermute x12, waiting for transfers between devices, local(): lax.ppermute(going[way], 'dp', right if way[0] == 'r' else left)  18 us
    all_to_all x1, blocking collectives, local(): got = lax.all_to_all(packed, 'dp', split_axis=0, concat_axis=0, tiled=True)  13.4 us
    ppermute x12, starting transfers between devices, local(): lax.ppermute(going[way], 'dp', right if way[0] == 'r' else left)  12.2 us
    ppermute x4, starting transfers between devices, local(): both.append(lax.ppermute(going[w + p][cut], 'dp', pairs))  4.26 us
    ppermute x2, starting transfers between devices, local(): inputs = [[x, lax.ppermute(x, 'mp', flip)] for x in cuts]  3.14 us
  transfers between devices with their start and end apart: 24, of which 8 were waited for; matrix products, arithmetic and copies ran while one was open for 0% of the time, Pallas kernels for 22%

profile of v6, /device:TPU:0, one launch (start us, length us, event | category | flops | bytes accessed | tf_op | source)
XLA Modules:
  0.0 76.2 jit_solution(3754483689837529160)
XLA Ops:
  0.0 1.1 %shard_map.82 = (bf16[128,1024]{1,0:T(8,128)(2,1)S(1)}, bf16[128,1024]{1,0:T(8,128)(2,1)S(1)}, bf16[128,256]{1,0:T(8,128)(2,1)S(1)}, f32[1,128]{1,0:T(1,128)S(1)...) custom-call(bf16[128,2048]{1,0:T(8,128)(2,1)} %x_ref.1, ...), custom_call_target="tpu_custom_call" | custom-call | flops 1000000 | tf_op jit(solution)/shard_map/pallas_call | solution.py:353
  1.1 3.1 %collective-permute-start.4 = (bf16[128,1024]{1,0:T(8,128)(2,1)S(1)}, bf16[128,1024]{1,0:T(8,128)(2,1)S(1)}, u32[]{:S(2)}, u32[]{:S(2)}) collective-permute-start(bf16[128,1024]{1,0:T(8,128)(2,1)S(1)} %get-tuple-element.37.refs_0_), channel_id=1, source_target_pairs={{0,1},{1,0},{2,3},{3,2},{4,5},{5,4},{6,7},{7,6},{8,9},{9,8},{10,11... | collective-permute-start | bytes 786440 | tf_op jit(solution)/shard_map/ppermute | solution.py:425
  4.3 1.2 %shard_map.83 = s32[16,5,2,128]{3,2,1,0:T(2,128)} custom-call(s32[1]{0:T(128)} %bitcast.1.mp_ref, s32[32]{0:T(128)S(4)} %get-tuple-element.28.rows_ref, s32[32]{0:T(128)S(4)} %get-tuple-element.29.cols_ref, s32[32,4,128]{2,1,0:T(4,128)S(1)} %get-tuple-element.30.masks_ref), custom_call_target="tpu_custom_call" | custom-call | flops 1000000 | tf_op jit(solution)/shard_map/pallas_call | solution.py:353
  5.5 13.4 %all_to_all.5 = s32[16,5,2,128]{3,2,1,0:T(2,128)S(1)} all-to-all(s32[16,5,2,128]{3,2,1,0:T(2,128)} %shard_map.83), channel_id=1, replica_groups=mesh['dp'=16,'mp'=2] {'dp'}, dimensions={0} | all-to-all | bytes 163840 | tf_op jit(solution)/shard_map/all_to_all | solution.py:442
  18.9 1.5 %collective-permute-start.1 = (s32[80,2,128]{2,1,0:T(2,128)S(1)}, s32[80,2,128]{2,1,0:T(2,128)S(1)}, u32[]{:S(2)}, u32[]{:S(2)}) collective-permute-start(s32[80,2,128]{2,1,0:T(2,128)S(1)} %bitcast.12), channel_id=1, source_target_pairs={{0,1},{1,0},{2,3},{3,2},{4,5},{5,4},{6,7},{7,6},{8,9},{9,8},{10,11... | collective-permute-start | bytes 245768 | tf_op jit(solution)/shard_map/ppermute | solution.py:445
  20.5 0.5 shard_map.86
  21.0 0.5 shard_map.87
  21.6 2.0 %collective-permute-start.6 = (bf16[4,264,128]{2,1,0:T(8,128)(2,1)S(1)}, bf16[4,264,128]{2,1,0:T(8,128)(2,1)S(1)}, u32[]{:S(2)}, u32[]{:S(2)}) collective-permute-start(bf16[4,264,128]{2,1,0:T(8,128)(2,1)S(1)} %get-tuple-element.40.refs_1_), channel_id=1, source_target_pairs={{0,8},{2,10},{4,0},{6,2},{8,16},{10,18},{12,4},{14,6},{16,24},{18,... | collective-permute-start | bytes 811016 | tf_op jit(solution)/shard_map/ppermute | solution.py:471
  23.6 2.0 %collective-permute-start.18 = (bf16[4,264,128]{2,1,0:T(8,128)(2,1)S(1)}, bf16[4,264,128]{2,1,0:T(8,128)(2,1)S(1)}, u32[]{:S(2)}, u32[]{:S(2)}) collective-permute-start(bf16[4,264,128]{2,1,0:T(8,128)(2,1)S(1)} %get-tuple-element.41.refs_0_), channel_id=1, source_target_pairs={{0,4},{2,6},{4,12},{6,14},{8,0},{10,2},{12,20},{14,22},{16,8},{18,... | collective-permute-start | bytes 811016 | tf_op jit(solution)/shard_map/ppermute | solution.py:471
  25.6 1.3 %collective-permute-done.2.refs_3_ = s32[80,2,128]{2,1,0:T(2,128)S(1)} collective-permute-done((s32[80,2,128]{2,1,0:T(2,128)S(1)}, s32[80,2,128]{2,1,0:T(2,128)S(1)}, u32[]{:S(2)}, u32[]{:S(2)}) %collective-permute-start.2) | collective-permute-done | bytes 81952 | tf_op jit(solution)/shard_map/ppermute | solution.py:446
  27.3 1.6 %shard_map.84 = (s32[1088]{0:T(1024)S(4)}, s32[8]{0:T(128)S(4)}) custom-call(s32[1]{0:T(128)} %bitcast.core_ref, s32[96]{0:T(128)S(1)} %reshape_squeeze.6.own_ids, s32[96]{0:T(128)S(1)} %reshape_squeeze.7.other_ids), custom_call_target="tpu_custom_call" | custom-call | flops 1000000 | tf_op jit(solution)/shard_map/pallas_call | solution.py:353
  29.0 1.9 %collective-permute-done.10.refs_5_ = bf16[4,264,128]{2,1,0:T(8,128)(2,1)S(1)} collective-permute-done((bf16[4,264,128]{2,1,0:T(8,128)(2,1)S(1)}, bf16[4,264,128]{2,1,0:T(8,128)(2,1)S(1)}, u32[]{:S(2)}, u32[]{:S(2)}) %collective-permute-start.10) | collective-permute-done | bytes 270368 | tf_op jit(solution)/shard_map/ppermute | solution.py:471
  31.0 2.0 %collective-permute-start.7 = (bf16[4,264,128]{2,1,0:T(8,128)(2,1)S(1)}, bf16[4,264,128]{2,1,0:T(8,128)(2,1)S(1)}, u32[]{:S(2)}, u32[]{:S(2)}) collective-permute-start(bf16[4,264,128]{2,1,0:T(8,128)(2,1)S(1)} %collective-permute-done.6.refs_3_), channel_id=1, source_target_pairs={{0,8},{2,10},{4,0},{6,2},{8,16},{10,18},{12,4},{14,6},{16,24},{18,... | collective-permute-start | bytes 811016 | tf_op jit(solution)/shard_map/ppermute | solution.py:471
  32.9 3.8 %collective-permute-done.14.refs_2_ = bf16[4,264,128]{2,1,0:T(8,128)(2,1)S(1)} collective-permute-done((bf16[4,264,128]{2,1,0:T(8,128)(2,1)S(1)}, bf16[4,264,128]{2,1,0:T(8,128)(2,1)S(1)}, u32[]{:S(2)}, u32[]{:S(2)}) %collective-permute-start.14) | collective-permute-done | bytes 270368 | tf_op jit(solution)/shard_map/ppermute | solution.py:471
  36.8 2.0 %collective-permute-start.15 = (bf16[4,264,128]{2,1,0:T(8,128)(2,1)S(1)}, bf16[4,264,128]{2,1,0:T(8,128)(2,1)S(1)}, u32[]{:S(2)}, u32[]{:S(2)}) collective-permute-start(bf16[4,264,128]{2,1,0:T(8,128)(2,1)S(1)} %collective-permute-done.14.refs_2_), channel_id=1, source_target_pairs={{0,8},{2,10},{4,0},{6,2},{8,16},{10,18},{12,4},{14,6},{16,24},{18,... | collective-permute-start | bytes 811016 | tf_op jit(solution)/shard_map/ppermute | solution.py:471
  38.8 4.5 %shard_map.88.refs_4_ = f32[32,136,128]{2,1,0:T(8,128)S(1)} custom-call(s32[1088]{0:T(1024)S(4)} %get-tuple-element.31.list_ref, s32[8]{0:T(128)S(4)} %get-tuple-element.32.count_ref, s32[160,4,128]{2,1,0:T(4,128)S(1)} %shard_map.85.masks_ref, f32[16,8,128]{2,1,0:T(8,128)S(1)} %get-tuple-element.39.own_sc, ...), custom_call_target="tpu_custom_call" | custom-call | flops 8000000000 | tf_op jit(solution)/shard_map/pallas_call | solution.py:353
  43.4 4.5 %collective-permute-done.15.refs_0_ = bf16[4,264,128]{2,1,0:T(8,128)(2,1)S(1)} collective-permute-done((bf16[4,264,128]{2,1,0:T(8,128)(2,1)S(1)}, bf16[4,264,128]{2,1,0:T(8,128)(2,1)S(1)}, u32[]{:S(2)}, u32[]{:S(2)}) %collective-permute-start.15) | collective-permute-done | bytes 270368 | tf_op jit(solution)/shard_map/ppermute | solution.py:471
  47.9 1.7 %collective-permute-start.16 = (bf16[4,264,128]{2,1,0:T(8,128)(2,1)S(1)}, bf16[4,264,128]{2,1,0:T(8,128)(2,1)S(1)}, u32[]{:S(2)}, u32[]{:S(2)}) collective-permute-start(bf16[4,264,128]{2,1,0:T(8,128)(2,1)S(1)} %collective-permute-done.15.refs_0_), channel_id=1, source_target_pairs={{0,8},{2,10},{4,0},{6,2},{8,16},{10,18},{12,4},{14,6},{16,24},{18,... | collective-permute-start | bytes 811016 | tf_op jit(solution)/shard_map/ppermute | solution.py:471
  50.3 1.7 %collective-permute-start.8 = (bf16[4,264,128]{2,1,0:T(8,128)(2,1)S(1)}, bf16[4,264,128]{2,1,0:T(8,128)(2,1)S(1)}, u32[]{:S(2)}, u32[]{:S(2)}) collective-permute-start(bf16[4,264,128]{2,1,0:T(8,128)(2,1)S(1)} %collective-permute-done.7.refs_1_), channel_id=1, source_target_pairs={{0,8},{2,10},{4,0},{6,2},{8,16},{10,18},{12,4},{14,6},{16,24},{18,... | collective-permute-start | bytes 811016 | tf_op jit(solution)/shard_map/ppermute | solution.py:471
  52.0 3.0 %shard_map.89.refs_2_ = f32[32,136,128]{2,1,0:T(8,128)S(1)} custom-call(s32[1088]{0:T(1024)S(4)} %get-tuple-element.31.list_ref, s32[8]{0:T(128)S(4)} %get-tuple-element.32.count_ref, s32[160,4,128]{2,1,0:T(4,128)S(1)} %shard_map.85.masks_ref, f32[16,8,128]{2,1,0:T(8,128)S(1)} %get-tuple-element.39.own_sc, ...), custom_call_target="tpu_custom_call", output_to_operand_aliasing={{}: (10, {})} | custom-call | flops 8000000000 | tf_op jit(solution)/shard_map/pallas_call | solution.py:353
  54.9 2.3 %collective-permute-done.16.refs_0_ = bf16[4,264,128]{2,1,0:T(8,128)(2,1)S(1)} collective-permute-done((bf16[4,264,128]{2,1,0:T(8,128)(2,1)S(1)}, bf16[4,264,128]{2,1,0:T(8,128)(2,1)S(1)}, u32[]{:S(2)}, u32[]{:S(2)}) %collective-permute-start.16) | collective-permute-done | bytes 270368 | tf_op jit(solution)/shard_map/ppermute | solution.py:471
  57.3 1.7 %collective-permute-start.17 = (bf16[2,264,128]{2,1,0:T(8,128)(2,1)S(1)}, bf16[2,264,128]{2,1,0:T(8,128)(2,1)S(1)}, u32[]{:S(2)}, u32[]{:S(2)}) collective-permute-start(bf16[2,264,128]{2,1,0:T(8,128)(2,1)S(1)} %slice.28), channel_id=1, source_target_pairs={{0,8},{2,10},{4,0},{6,2},{8,16},{10,18},{12,4},{14,6},{16,24},{18,... | collective-permute-start | bytes 405512 | tf_op jit(solution)/shard_map/ppermute | solution.py:480
  59.4 5.3 %collective-permute-done.12.refs_1_ = bf16[4,264,128]{2,1,0:T(8,128)(2,1)S(1)} collective-permute-done((bf16[4,264,128]{2,1,0:T(8,128)(2,1)S(1)}, bf16[4,264,128]{2,1,0:T(8,128)(2,1)S(1)}, u32[]{:S(2)}, u32[]{:S(2)}) %collective-permute-start.12) | collective-permute-done | bytes 270368 | tf_op jit(solution)/shard_map/ppermute | solution.py:471
  65.1 1.7 %collective-permute-start.9 = (bf16[2,264,128]{2,1,0:T(8,128)(2,1)S(1)}, bf16[2,264,128]{2,1,0:T(8,128)(2,1)S(1)}, u32[]{:S(2)}, u32[]{:S(2)}) collective-permute-start(bf16[2,264,128]{2,1,0:T(8,128)(2,1)S(1)} %slice.26), channel_id=1, source_target_pairs={{0,8},{2,10},{4,0},{6,2},{8,16},{10,18},{12,4},{14,6},{16,24},{18,... | collective-permute-start | bytes 405512 | tf_op jit(solution)/shard_map/ppermute | solution.py:480
  66.9 2.0 %shard_map.90.refs_2_ = f32[32,136,128]{2,1,0:T(8,128)S(1)} custom-call(s32[1088]{0:T(1024)S(4)} %get-tuple-element.31.list_ref, s32[8]{0:T(128)S(4)} %get-tuple-element.32.count_ref, s32[160,4,128]{2,1,0:T(4,128)S(1)} %shard_map.85.masks_ref, f32[16,8,128]{2,1,0:T(8,128)S(1)} %get-tuple-element.39.own_sc, ...), custom_call_target="tpu_custom_call", output_to_operand_aliasing={{}: (8, {})} | custom-call | flops 8000000000 | tf_op jit(solution)/shard_map/pallas_call | solution.py:353
  68.9 1.6 %shard_map.91.refs_2_ = f32[32,136,128]{2,1,0:T(8,128)S(1)} custom-call(s32[1088]{0:T(1024)S(4)} %get-tuple-element.31.list_ref, s32[8]{0:T(128)S(4)} %get-tuple-element.32.count_ref, s32[160,4,128]{2,1,0:T(4,128)S(1)} %shard_map.85.masks_ref, f32[16,8,128]{2,1,0:T(8,128)S(1)} %get-tuple-element.39.own_sc, ...), custom_call_target="tpu_custom_call", output_to_operand_aliasing={{}: (8, {})} | custom-call | flops 8000000000 | tf_op jit(solution)/shard_map/pallas_call | solution.py:353
  70.5 0.9 %shard_map.92.refs_2_ = f32[32,136,128]{2,1,0:T(8,128)S(1)} custom-call(s32[1088]{0:T(1024)S(4)} %get-tuple-element.31.list_ref, s32[8]{0:T(128)S(4)} %get-tuple-element.32.count_ref, s32[160,4,128]{2,1,0:T(4,128)S(1)} %shard_map.85.masks_ref, f32[16,8,128]{2,1,0:T(8,128)S(1)} %get-tuple-element.39.own_sc, ...), custom_call_target="tpu_custom_call", output_to_operand_aliasing={{}: (8, {})} | custom-call | flops 8000000000 | tf_op jit(solution)/shard_map/pallas_call | solution.py:353
  71.4 1.2 %shard_map.93 = (f32[32,136,128]{2,1,0:T(8,128)S(1)}, bf16[16,128,128]{2,1,0:T(8,128)(2,1)S(1)}, f32[16,8,128]{2,1,0:T(8,128)S(1)}, s32[160,4,128]{2,1,0:T(4,128...) custom-call(s32[1088]{0:T(1024)S(4)} %get-tuple-element.31.list_ref,, ...), custom_call_target="tpu_custom_call", output_to_operand_aliasing={{0}: (8, {}), {3}: (2, {}), {4}: (3, {}), {5}: (4, {}), {6}... | custom-call | flops 8000000000 | tf_op jit(solution)/shard_map/pallas_call | solution.py:353
  72.7 0.5 collective-permute-start.23
  73.2 0.9 %shard_map.94.state_ref = f32[32,136,128]{2,1,0:T(8,128)S(1)} custom-call(s32[1088]{0:T(1024)S(4)} %get-tuple-element.31.list_ref, s32[8]{0:T(128)S(4)} %get-tuple-element.32.count_ref, s32[160,4,128]{2,1,0:T(4,128)S(1)} %get-tuple-element.42.masks_ref, f32[16,8,128]{2,1,0:T(8,128)S(1)} %get-tuple-element.43.own_sc, ...), custom_call_target="tpu_custom_call", output_to_operand_aliasing={{}: (8, {})} | custom-call | flops 8000000000 | tf_op jit(solution)/shard_map/pallas_call | solution.py:353
  74.1 0.6 collective-permute-done.23.levels_ref
  74.7 1.4 %shard_map.95 = bf16[128,2048]{1,0:T(8,128)(2,1)} custom-call(f32[32,136,128]{2,1,0:T(8,128)S(1)} %shard_map.94.state_ref, bf16[16,128,128]{2,1,0:T(8,128)(2,1)S(1)} %collective-permute-done.22.sums_ref, f32[16,8,128]{2,1,0:T(8,128)S(1)} %collective-permute-done.23.levels_ref, bf16[128,2048]{1,0:T(8,128)(2,1)S(1)} %copy-done, f32[1,128]{1,0:T(1,128)S(1)} %bitcast.16), custom_call_target="tpu_custom_call" | custom-call | flops 1000000 | tf_op jit(solution)/shard_map/pallas_call | solution.py:353
  (43 shorter events, 2.4 us)
Async XLA Ops:
  1.1 19.3 %collective-permute-start.4 = (bf16[128,1024]{1,0:T(8,128)(2,1)S(1)}, bf16[128,1024]{1,0:T(8,128)(2,1)S(1)}, u32[]{:S(2)}, u32[]{:S(2)}) collective-permute-start(bf16[128,1024]{1,0:T(8,128)(2,1)S(1)} %get-tuple-element.37.refs_0_), channel_id=1, source_target_pairs={{0,1},{1,0},{2,3},{3,2},{4,5},{5,4},{6,7},{7,6},{8,9},{9,8},{10,11... | collective-permute-start | bytes 786440 | tf_op jit(solution)/shard_map/ppermute | solution.py:425
  4.2 16.8 %collective-permute-start.3 = (bf16[128,1024]{1,0:T(8,128)(2,1)S(1)}, bf16[128,1024]{1,0:T(8,128)(2,1)S(1)}, u32[]{:S(2)}, u32[]{:S(2)}) collective-permute-start(bf16[128,1024]{1,0:T(8,128)(2,1)S(1)} %get-tuple-element.36.refs_0_), channel_id=1, source_target_pairs={{0,1},{1,0},{2,3},{3,2},{4,5},{5,4},{6,7},{7,6},{8,9},{9,8},{10,11... | collective-permute-start | bytes 786440 | tf_op jit(solution)/shard_map/ppermute | solution.py:425
  18.9 4.7 %collective-permute-start.1 = (s32[80,2,128]{2,1,0:T(2,128)S(1)}, s32[80,2,128]{2,1,0:T(2,128)S(1)}, u32[]{:S(2)}, u32[]{:S(2)}) collective-permute-start(s32[80,2,128]{2,1,0:T(2,128)S(1)} %bitcast.12), channel_id=1, source_target_pairs={{0,1},{1,0},{2,3},{3,2},{4,5},{5,4},{6,7},{7,6},{8,9},{9,8},{10,11... | collective-permute-start | bytes 245768 | tf_op jit(solution)/shard_map/ppermute | solution.py:445
  20.5 5.1 %collective-permute-start = (s32[80,2,128]{2,1,0:T(2,128)S(1)}, s32[80,2,128]{2,1,0:T(2,128)S(1)}, u32[]{:S(2)}, u32[]{:S(2)}) collective-permute-start(s32[80,2,128]{2,1,0:T(2,128)S(1)} %bitcast.13), channel_id=1, source_target_pairs={{0,2},{2,0},{4,6},{6,4},{8,10},{10,8},{12,14},{14,12},{16,18},{18,... | collective-permute-start | bytes 245768 | tf_op jit(solution)/shard_map/ppermute | solution.py:446
  21.5 9.4 %collective-permute-start.10 = (bf16[4,264,128]{2,1,0:T(8,128)(2,1)S(1)}, bf16[4,264,128]{2,1,0:T(8,128)(2,1)S(1)}, u32[]{:S(2)}, u32[]{:S(2)}) collective-permute-start(bf16[4,264,128]{2,1,0:T(8,128)(2,1)S(1)} %get-tuple-element.40.refs_1_), channel_id=1, source_target_pairs={{0,4},{2,6},{4,12},{6,14},{8,0},{10,2},{12,20},{14,22},{16,8},{18,... | collective-permute-start | bytes 811016 | tf_op jit(solution)/shard_map/ppermute | solution.py:471
  21.6 9.4 %collective-permute-start.6 = (bf16[4,264,128]{2,1,0:T(8,128)(2,1)S(1)}, bf16[4,264,128]{2,1,0:T(8,128)(2,1)S(1)}, u32[]{:S(2)}, u32[]{:S(2)}) collective-permute-start(bf16[4,264,128]{2,1,0:T(8,128)(2,1)S(1)} %get-tuple-element.40.refs_1_), channel_id=1, source_target_pairs={{0,8},{2,10},{4,0},{6,2},{8,16},{10,18},{12,4},{14,6},{16,24},{18,... | collective-permute-start | bytes 811016 | tf_op jit(solution)/shard_map/ppermute | solution.py:471
  23.6 13.2 %collective-permute-start.14 = (bf16[4,264,128]{2,1,0:T(8,128)(2,1)S(1)}, bf16[4,264,128]{2,1,0:T(8,128)(2,1)S(1)}, u32[]{:S(2)}, u32[]{:S(2)}) collective-permute-start(bf16[4,264,128]{2,1,0:T(8,128)(2,1)S(1)} %get-tuple-element.41.refs_0_), channel_id=1, source_target_pairs={{0,8},{2,10},{4,0},{6,2},{8,16},{10,18},{12,4},{14,6},{16,24},{18,... | collective-permute-start | bytes 811016 | tf_op jit(solution)/shard_map/ppermute | solution.py:471
  23.6 15.1 %collective-permute-start.18 = (bf16[4,264,128]{2,1,0:T(8,128)(2,1)S(1)}, bf16[4,264,128]{2,1,0:T(8,128)(2,1)S(1)}, u32[]{:S(2)}, u32[]{:S(2)}) collective-permute-start(bf16[4,264,128]{2,1,0:T(8,128)(2,1)S(1)} %get-tuple-element.41.refs_0_), channel_id=1, source_target_pairs={{0,4},{2,6},{4,12},{6,14},{8,0},{10,2},{12,20},{14,22},{16,8},{18,... | collective-permute-start | bytes 811016 | tf_op jit(solution)/shard_map/ppermute | solution.py:471
  25.6 1.3 %collective-permute-start.2 = (s32[80,2,128]{2,1,0:T(2,128)S(1)}, s32[80,2,128]{2,1,0:T(2,128)S(1)}, u32[]{:S(2)}, u32[]{:S(2)}) collective-permute-start(s32[80,2,128]{2,1,0:T(2,128)S(1)} %collective-permute-done.1.refs_1_), channel_id=1, source_target_pairs={{0,2},{2,0},{4,6},{6,4},{8,10},{10,8},{12,14},{14,12},{16,18},{18,... | collective-permute-start | bytes 245768 | tf_op jit(solution)/shard_map/ppermute | solution.py:446
  26.9 11.9 %collective-permute-start.5 = (f32[16,8,128]{2,1,0:T(8,128)S(1)}, f32[16,8,128]{2,1,0:T(8,128)S(1)}, u32[]{:S(2)}, u32[]{:S(2)}) collective-permute-start(f32[16,8,128]{2,1,0:T(8,128)S(1)} %get-tuple-element.39.own_sc), channel_id=1, source_target_pairs={{0,2},{2,0},{4,6},{6,4},{8,10},{10,8},{12,14},{14,12},{16,18},{18,... | collective-permute-start | bytes 196616 | tf_op jit(solution)/shard_map/ppermute | solution.py:465
  30.9 19.0 %collective-permute-start.11 = (bf16[4,264,128]{2,1,0:T(8,128)(2,1)S(1)}, bf16[4,264,128]{2,1,0:T(8,128)(2,1)S(1)}, u32[]{:S(2)}, u32[]{:S(2)}) collective-permute-start(bf16[4,264,128]{2,1,0:T(8,128)(2,1)S(1)} %collective-permute-done.10.refs_5_), channel_id=1, source_target_pairs={{0,4},{2,6},{4,12},{6,14},{8,0},{10,2},{12,20},{14,22},{16,8},{18,... | collective-permute-start | bytes 811016 | tf_op jit(solution)/shard_map/ppermute | solution.py:471
  31.0 19.3 %collective-permute-start.7 = (bf16[4,264,128]{2,1,0:T(8,128)(2,1)S(1)}, bf16[4,264,128]{2,1,0:T(8,128)(2,1)S(1)}, u32[]{:S(2)}, u32[]{:S(2)}) collective-permute-start(bf16[4,264,128]{2,1,0:T(8,128)(2,1)S(1)} %collective-permute-done.6.refs_3_), channel_id=1, source_target_pairs={{0,8},{2,10},{4,0},{6,2},{8,16},{10,18},{12,4},{14,6},{16,24},{18,... | collective-permute-start | bytes 811016 | tf_op jit(solution)/shard_map/ppermute | solution.py:471
  36.8 11.1 %collective-permute-start.15 = (bf16[4,264,128]{2,1,0:T(8,128)(2,1)S(1)}, bf16[4,264,128]{2,1,0:T(8,128)(2,1)S(1)}, u32[]{:S(2)}, u32[]{:S(2)}) collective-permute-start(bf16[4,264,128]{2,1,0:T(8,128)(2,1)S(1)} %collective-permute-done.14.refs_2_), channel_id=1, source_target_pairs={{0,8},{2,10},{4,0},{6,2},{8,16},{10,18},{12,4},{14,6},{16,24},{18,... | collective-permute-start | bytes 811016 | tf_op jit(solution)/shard_map/ppermute | solution.py:471
  38.7 10.8 %collective-permute-start.19 = (bf16[4,264,128]{2,1,0:T(8,128)(2,1)S(1)}, bf16[4,264,128]{2,1,0:T(8,128)(2,1)S(1)}, u32[]{:S(2)}, u32[]{:S(2)}) collective-permute-start(bf16[4,264,128]{2,1,0:T(8,128)(2,1)S(1)} %collective-permute-done.18.refs_4_), channel_id=1, source_target_pairs={{0,4},{2,6},{4,12},{6,14},{8,0},{10,2},{12,20},{14,22},{16,8},{18,... | collective-permute-start | bytes 811016 | tf_op jit(solution)/shard_map/ppermute | solution.py:471
  47.9 9.4 %collective-permute-start.16 = (bf16[4,264,128]{2,1,0:T(8,128)(2,1)S(1)}, bf16[4,264,128]{2,1,0:T(8,128)(2,1)S(1)}, u32[]{:S(2)}, u32[]{:S(2)}) collective-permute-start(bf16[4,264,128]{2,1,0:T(8,128)(2,1)S(1)} %collective-permute-done.15.refs_0_), channel_id=1, source_target_pairs={{0,8},{2,10},{4,0},{6,2},{8,16},{10,18},{12,4},{14,6},{16,24},{18,... | collective-permute-start | bytes 811016 | tf_op jit(solution)/shard_map/ppermute | solution.py:471
  49.6 9.4 %collective-permute-start.20 = (bf16[4,264,128]{2,1,0:T(8,128)(2,1)S(1)}, bf16[4,264,128]{2,1,0:T(8,128)(2,1)S(1)}, u32[]{:S(2)}, u32[]{:S(2)}) collective-permute-start(bf16[4,264,128]{2,1,0:T(8,128)(2,1)S(1)} %collective-permute-done.19.refs_2_), channel_id=1, source_target_pairs={{0,4},{2,6},{4,12},{6,14},{8,0},{10,2},{12,20},{14,22},{16,8},{18,... | collective-permute-start | bytes 811016 | tf_op jit(solution)/shard_map/ppermute | solution.py:471
  49.9 14.8 %collective-permute-start.12 = (bf16[4,264,128]{2,1,0:T(8,128)(2,1)S(1)}, bf16[4,264,128]{2,1,0:T(8,128)(2,1)S(1)}, u32[]{:S(2)}, u32[]{:S(2)}) collective-permute-start(bf16[4,264,128]{2,1,0:T(8,128)(2,1)S(1)} %collective-permute-done.11.refs_3_), channel_id=1, source_target_pairs={{0,4},{2,6},{4,12},{6,14},{8,0},{10,2},{12,20},{14,22},{16,8},{18,... | collective-permute-start | bytes 811016 | tf_op jit(solution)/shard_map/ppermute | solution.py:471
  50.3 14.9 %collective-permute-start.8 = (bf16[4,264,128]{2,1,0:T(8,128)(2,1)S(1)}, bf16[4,264,128]{2,1,0:T(8,128)(2,1)S(1)}, u32[]{:S(2)}, u32[]{:S(2)}) collective-permute-start(bf16[4,264,128]{2,1,0:T(8,128)(2,1)S(1)} %collective-permute-done.7.refs_1_), channel_id=1, source_target_pairs={{0,8},{2,10},{4,0},{6,2},{8,16},{10,18},{12,4},{14,6},{16,24},{18,... | collective-permute-start | bytes 811016 | tf_op jit(solution)/shard_map/ppermute | solution.py:471
  57.3 13.2 %collective-permute-start.17 = (bf16[2,264,128]{2,1,0:T(8,128)(2,1)S(1)}, bf16[2,264,128]{2,1,0:T(8,128)(2,1)S(1)}, u32[]{:S(2)}, u32[]{:S(2)}) collective-permute-start(bf16[2,264,128]{2,1,0:T(8,128)(2,1)S(1)} %slice.28), channel_id=1, source_target_pairs={{0,8},{2,10},{4,0},{6,2},{8,16},{10,18},{12,4},{14,6},{16,24},{18,... | collective-permute-start | bytes 405512 | tf_op jit(solution)/shard_map/ppermute | solution.py:480
  59.0 11.5 %collective-permute-start.21 = (bf16[2,264,128]{2,1,0:T(8,128)(2,1)S(1)}, bf16[2,264,128]{2,1,0:T(8,128)(2,1)S(1)}, u32[]{:S(2)}, u32[]{:S(2)}) collective-permute-start(bf16[2,264,128]{2,1,0:T(8,128)(2,1)S(1)} %slice.29), channel_id=1, source_target_pairs={{0,4},{2,6},{4,12},{6,14},{8,0},{10,2},{12,20},{14,22},{16,8},{18,... | collective-permute-start | bytes 405512 | tf_op jit(solution)/shard_map/ppermute | solution.py:480
  64.7 6.7 %collective-permute-start.13 = (bf16[2,264,128]{2,1,0:T(8,128)(2,1)S(1)}, bf16[2,264,128]{2,1,0:T(8,128)(2,1)S(1)}, u32[]{:S(2)}, u32[]{:S(2)}) collective-permute-start(bf16[2,264,128]{2,1,0:T(8,128)(2,1)S(1)} %slice.27), channel_id=1, source_target_pairs={{0,4},{2,6},{4,12},{6,14},{8,0},{10,2},{12,20},{14,22},{16,8},{18,... | collective-permute-start | bytes 405512 | tf_op jit(solution)/shard_map/ppermute | solution.py:480
  65.1 6.3 %collective-permute-start.9 = (bf16[2,264,128]{2,1,0:T(8,128)(2,1)S(1)}, bf16[2,264,128]{2,1,0:T(8,128)(2,1)S(1)}, u32[]{:S(2)}, u32[]{:S(2)}) collective-permute-start(bf16[2,264,128]{2,1,0:T(8,128)(2,1)S(1)} %slice.26), channel_id=1, source_target_pairs={{0,8},{2,10},{4,0},{6,2},{8,16},{10,18},{12,4},{14,6},{16,24},{18,... | collective-permute-start | bytes 405512 | tf_op jit(solution)/shard_map/ppermute | solution.py:480
  72.6 2.1 %collective-permute-start.22 = (bf16[16,128,128]{2,1,0:T(8,128)(2,1)S(1)}, bf16[16,128,128]{2,1,0:T(8,128)(2,1)S(1)}, u32[]{:S(2)}, u32[]{:S(2)}) collective-permute-start(bf16[16,128,128]{2,1,0:T(8,128)(2,1)S(1)} %get-tuple-element.49), channel_id=1, source_target_pairs={{0,2},{2,0},{4,6},{6,4},{8,10},{10,8},{12,14},{14,12},{16,18},{18,... | collective-permute-start | bytes 1572872 | tf_op jit(solution)/shard_map/ppermute | solution.py:538
  72.7 2.0 %collective-permute-start.23 = (f32[16,8,128]{2,1,0:T(8,128)S(1)}, f32[16,8,128]{2,1,0:T(8,128)S(1)}, u32[]{:S(2)}, u32[]{:S(2)}) collective-permute-start(f32[16,8,128]{2,1,0:T(8,128)S(1)} %get-tuple-element.50), channel_id=1, source_target_pairs={{0,2},{2,0},{4,6},{6,4},{8,10},{10,8},{12,14},{14,12},{16,18},{18,... | collective-permute-start | bytes 196616 | tf_op jit(solution)/shard_map/ppermute | solution.py:538
  73.2 1.5 %copy-start = (bf16[128,2048]{1,0:T(8,128)(2,1)S(1)}, bf16[128,2048]{1,0:T(8,128)(2,1)}, u32[]{:S(2)}) copy-start(bf16[128,2048]{1,0:T(8,128)(2,1)} %x_ref.1) | copy-start | bytes 1572868
  73.2 1.5 %copy-start.1 = (f32[128]{0:T(128)S(1)}, f32[128]{0:T(128)}, u32[]{:S(2)}) copy-start(f32[128]{0:T(128)} %param.12) | copy-start | bytes 1540

commit v7 on v5

--- a/solution.py
+++ b/solution.py
@@ -405,11 +405,11 @@
     core = jnp.full((1,), lax.axis_index("dp") & 1, jnp.int32)
     parts = 2 if n_mp == 2 else 1
     moved = [node_feats, proj_weight, att_src.reshape(1, dims), att_dst.reshape(1, dims)]
-    moved += [tile_masks, tile_rows, tile_cols]
+    moved += [out_bias.reshape(1, dims), tile_masks, tile_rows, tile_cols]
     shapes = [((node_feats.shape[0], nodes // parts), BF16)] * parts + [(v.shape, v.dtype) for v in moved[1:]]
     spaces = [pltpu.VMEM] * (len(shapes) - 2) + [pltpu.SMEM] * 2
     anywhere = pl.BlockSpec(memory_space=pl.ANY)
-    *cuts, weight, a_src, a_dst, near_masks, near_rows, near_cols = call(
+    *cuts, weight, a_src, a_dst, near_bias, near_masks, near_rows, near_cols = call(
         functools.partial(open_kernel, parts),
         [space(*v) for space, v in zip(spaces, shapes)],
         [far(v) for v in moved],
@@ -538,7 +538,7 @@
     return call(
         merge_kernel,
         jax.ShapeDtypeStruct((dims, nodes), BF16),
-        (near(state), *[near(v) for v in back], node_feats, out_bias.reshape(1, dims)),
+        (near(state), *[near(v) for v in back], near(node_feats), near(near_bias)),
         out_specs=anywhere,
         scratch=[pltpu.VMEM((dims, nodes), BF16), pltpu.SemaphoreType.DMA((math.gcd(blocks, 8),))],
     )

time: 76 us -> 76.1 us (level)
  no operation moved by 1% of the time
where the time goes in v7:
time: 76.1 us; the launch traced here: 74.7 us
  starting transfers between devices  24.3 us (32%)
  waiting for transfers between devices  21.9 us (29%)
  Pallas kernels  16.6 us (22%)
  blocking collectives  11.5 us (15%)
    ppermute x12, waiting for transfers between devices, local(): lax.ppermute(going[way], 'dp', right if way[0] == 'r' else left)  19.5 us
    pallas_call x14, Pallas kernels, call(): pl.pallas_call(kernel, out_shape=outs, in_specs=in_specs or [VMEM] * len(...  16.6 us
    all_to_all x1, blocking collectives, local(): got = lax.all_to_all(packed, 'dp', split_axis=0, concat_axis=0, tiled=True)  11.5 us
    ppermute x12, starting transfers between devices, local(): lax.ppermute(going[way], 'dp', right if way[0] == 'r' else left)  9.07 us
    ppermute x2, starting transfers between devices, local(): back = (lax.ppermute(sums, 'dp', swap), lax.ppermute(levels, 'dp', swap))  7.21 us
    ppermute x4, starting transfers between devices, local(): both.append(lax.ppermute(going[w + p][cut], 'dp', pairs))  3.11 us
    ppermute x2, starting transfers between devices, local(): got_other = [lax.ppermute(v, 'dp', swap) for v in got]  1.76 us
    ppermute x2, starting transfers between devices, local(): inputs = [[x, lax.ppermute(x, 'mp', flip)] for x in cuts]  1.53 us
  transfers between devices with their start and end apart: 24, of which 8 were waited for; matrix products, arithmetic and copies ran while one was open for 0% of the time, Pallas kernels for 19%

profile of v7, /device:TPU:11, one launch (start us, length us, event | category | flops | bytes accessed | tf_op | source)
XLA Modules:
  0.0 74.7 jit_solution(7607507246650704948)
XLA Ops:
  0.0 1.2 %shard_map.82 = (bf16[128,1024]{1,0:T(8,128)(2,1)S(1)}, bf16[128,1024]{1,0:T(8,128)(2,1)S(1)}, bf16[128,256]{1,0:T(8,128)(2,1)S(1)}, f32[1,128]{1,0:T(1,128)S(1)...) custom-call(bf16[128,2048]{1,0:T(8,128)(2,1)} %x_ref.1, ...), custom_call_target="tpu_custom_call" | custom-call | flops 1000000 | tf_op jit(solution)/shard_map/pallas_call | solution.py:350
  1.2 1.3 %collective-permute-start.4 = (bf16[128,1024]{1,0:T(8,128)(2,1)S(1)}, bf16[128,1024]{1,0:T(8,128)(2,1)S(1)}, u32[]{:S(2)}, u32[]{:S(2)}) collective-permute-start(bf16[128,1024]{1,0:T(8,128)(2,1)S(1)} %get-tuple-element.38.refs_0_), channel_id=1, source_target_pairs={{0,1},{1,0},{2,3},{3,2},{4,5},{5,4},{6,7},{7,6},{8,9},{9,8},{10,11... | collective-permute-start | bytes 786440 | tf_op jit(solution)/shard_map/ppermute | solution.py:422
  2.7 1.2 %shard_map.83 = s32[16,5,2,128]{3,2,1,0:T(2,128)} custom-call(s32[1]{0:T(128)} %bitcast.1.mp_ref, s32[32]{0:T(128)S(4)} %get-tuple-element.29.rows_ref, s32[32]{0:T(128)S(4)} %get-tuple-element.30.cols_ref, s32[32,4,128]{2,1,0:T(4,128)S(1)} %get-tuple-element.31.masks_ref), custom_call_target="tpu_custom_call" | custom-call | flops 1000000 | tf_op jit(solution)/shard_map/pallas_call | solution.py:350
  3.9 11.5 %all_to_all.5 = s32[16,5,2,128]{3,2,1,0:T(2,128)S(1)} all-to-all(s32[16,5,2,128]{3,2,1,0:T(2,128)} %shard_map.83), channel_id=1, replica_groups=mesh['dp'=16,'mp'=2] {'dp'}, dimensions={0} | all-to-all | bytes 163840 | tf_op jit(solution)/shard_map/all_to_all | solution.py:439
  15.4 1.2 %collective-permute-start.1 = (s32[80,2,128]{2,1,0:T(2,128)S(1)}, s32[80,2,128]{2,1,0:T(2,128)S(1)}, u32[]{:S(2)}, u32[]{:S(2)}) collective-permute-start(s32[80,2,128]{2,1,0:T(2,128)S(1)} %bitcast.12), channel_id=1, source_target_pairs={{0,1},{1,0},{2,3},{3,2},{4,5},{5,4},{6,7},{7,6},{8,9},{9,8},{10,11... | collective-permute-start | bytes 245768 | tf_op jit(solution)/shard_map/ppermute | solution.py:442
  16.7 0.6 collective-permute-start
  17.8 0.5 shard_map.87
  18.8 1.1 %collective-permute-start.6 = (bf16[4,264,128]{2,1,0:T(8,128)(2,1)S(1)}, bf16[4,264,128]{2,1,0:T(8,128)(2,1)S(1)}, u32[]{:S(2)}, u32[]{:S(2)}) collective-permute-start(bf16[4,264,128]{2,1,0:T(8,128)(2,1)S(1)} %get-tuple-element.41.refs_1_), channel_id=1, source_target_pairs={{0,8},{2,10},{4,0},{6,2},{8,16},{10,18},{12,4},{14,6},{16,24},{18,... | collective-permute-start | bytes 811016 | tf_op jit(solution)/shard_map/ppermute | solution.py:468
  19.9 1.4 %collective-permute-start.14 = (bf16[4,264,128]{2,1,0:T(8,128)(2,1)S(1)}, bf16[4,264,128]{2,1,0:T(8,128)(2,1)S(1)}, u32[]{:S(2)}, u32[]{:S(2)}) collective-permute-start(bf16[4,264,128]{2,1,0:T(8,128)(2,1)S(1)} %get-tuple-element.42.refs_0_), channel_id=1, source_target_pairs={{0,8},{2,10},{4,0},{6,2},{8,16},{10,18},{12,4},{14,6},{16,24},{18,... | collective-permute-start | bytes 811016 | tf_op jit(solution)/shard_map/ppermute | solution.py:468
  21.3 1.1 %collective-permute-start.2 = (s32[80,2,128]{2,1,0:T(2,128)S(1)}, s32[80,2,128]{2,1,0:T(2,128)S(1)}, u32[]{:S(2)}, u32[]{:S(2)}) collective-permute-start(s32[80,2,128]{2,1,0:T(2,128)S(1)} %collective-permute-done.1.refs_1_), channel_id=1, source_target_pairs={{0,2},{2,0},{4,6},{6,4},{8,10},{10,8},{12,14},{14,12},{16,18},{18,... | collective-permute-start | bytes 245768 | tf_op jit(solution)/shard_map/ppermute | solution.py:443
  22.5 0.9 %collective-permute-done.2.refs_3_ = s32[80,2,128]{2,1,0:T(2,128)S(1)} collective-permute-done((s32[80,2,128]{2,1,0:T(2,128)S(1)}, s32[80,2,128]{2,1,0:T(2,128)S(1)}, u32[]{:S(2)}, u32[]{:S(2)}) %collective-permute-start.2) | collective-permute-done | bytes 81952 | tf_op jit(solution)/shard_map/ppermute | solution.py:443
  24.0 1.5 %shard_map.84 = (s32[1088]{0:T(1024)S(4)}, s32[8]{0:T(128)S(4)}) custom-call(s32[1]{0:T(128)} %bitcast.core_ref, s32[96]{0:T(128)S(1)} %reshape_squeeze.6.own_ids, s32[96]{0:T(128)S(1)} %reshape_squeeze.7.other_ids), custom_call_target="tpu_custom_call" | custom-call | flops 1000000 | tf_op jit(solution)/shard_map/pallas_call | solution.py:350
  25.6 0.9 %collective-permute-done.10.refs_5_ = bf16[4,264,128]{2,1,0:T(8,128)(2,1)S(1)} collective-permute-done((bf16[4,264,128]{2,1,0:T(8,128)(2,1)S(1)}, bf16[4,264,128]{2,1,0:T(8,128)(2,1)S(1)}, u32[]{:S(2)}, u32[]{:S(2)}) %collective-permute-start.10) | collective-permute-done | bytes 270368 | tf_op jit(solution)/shard_map/ppermute | solution.py:468
  26.7 1.3 %collective-permute-start.7 = (bf16[4,264,128]{2,1,0:T(8,128)(2,1)S(1)}, bf16[4,264,128]{2,1,0:T(8,128)(2,1)S(1)}, u32[]{:S(2)}, u32[]{:S(2)}) collective-permute-start(bf16[4,264,128]{2,1,0:T(8,128)(2,1)S(1)} %collective-permute-done.6.refs_3_), channel_id=1, source_target_pairs={{0,8},{2,10},{4,0},{6,2},{8,16},{10,18},{12,4},{14,6},{16,24},{18,... | collective-permute-start | bytes 811016 | tf_op jit(solution)/shard_map/ppermute | solution.py:468
  28.1 4.2 %collective-permute-done.14.refs_2_ = bf16[4,264,128]{2,1,0:T(8,128)(2,1)S(1)} collective-permute-done((bf16[4,264,128]{2,1,0:T(8,128)(2,1)S(1)}, bf16[4,264,128]{2,1,0:T(8,128)(2,1)S(1)}, u32[]{:S(2)}, u32[]{:S(2)}) %collective-permute-start.14) | collective-permute-done | bytes 270368 | tf_op jit(solution)/shard_map/ppermute | solution.py:468
  32.2 1.2 %collective-permute-start.15 = (bf16[4,264,128]{2,1,0:T(8,128)(2,1)S(1)}, bf16[4,264,128]{2,1,0:T(8,128)(2,1)S(1)}, u32[]{:S(2)}, u32[]{:S(2)}) collective-permute-start(bf16[4,264,128]{2,1,0:T(8,128)(2,1)S(1)} %collective-permute-done.14.refs_2_), channel_id=1, source_target_pairs={{0,8},{2,10},{4,0},{6,2},{8,16},{10,18},{12,4},{14,6},{16,24},{18,... | collective-permute-start | bytes 811016 | tf_op jit(solution)/shard_map/ppermute | solution.py:468
  33.7 3.1 %shard_map.88.refs_4_ = f32[32,136,128]{2,1,0:T(8,128)S(1)} custom-call(s32[1088]{0:T(1024)S(4)} %get-tuple-element.32.list_ref, s32[8]{0:T(128)S(4)} %get-tuple-element.33.count_ref, s32[160,4,128]{2,1,0:T(4,128)S(1)} %shard_map.85.masks_ref, f32[16,8,128]{2,1,0:T(8,128)S(1)} %get-tuple-element.40.own_sc, ...), custom_call_target="tpu_custom_call" | custom-call | flops 8000000000 | tf_op jit(solution)/shard_map/pallas_call | solution.py:350
  36.8 7.0 %collective-permute-done.15.refs_0_ = bf16[4,264,128]{2,1,0:T(8,128)(2,1)S(1)} collective-permute-done((bf16[4,264,128]{2,1,0:T(8,128)(2,1)S(1)}, bf16[4,264,128]{2,1,0:T(8,128)(2,1)S(1)}, u32[]{:S(2)}, u32[]{:S(2)}) %collective-permute-start.15) | collective-permute-done | bytes 270368 | tf_op jit(solution)/shard_map/ppermute | solution.py:468
  43.8 1.2 %collective-permute-start.16 = (bf16[4,264,128]{2,1,0:T(8,128)(2,1)S(1)}, bf16[4,264,128]{2,1,0:T(8,128)(2,1)S(1)}, u32[]{:S(2)}, u32[]{:S(2)}) collective-permute-start(bf16[4,264,128]{2,1,0:T(8,128)(2,1)S(1)} %collective-permute-done.15.refs_0_), channel_id=1, source_target_pairs={{0,8},{2,10},{4,0},{6,2},{8,16},{10,18},{12,4},{14,6},{16,24},{18,... | collective-permute-start | bytes 811016 | tf_op jit(solution)/shard_map/ppermute | solution.py:468
  45.3 0.9 %collective-permute-start.12 = (bf16[4,264,128]{2,1,0:T(8,128)(2,1)S(1)}, bf16[4,264,128]{2,1,0:T(8,128)(2,1)S(1)}, u32[]{:S(2)}, u32[]{:S(2)}) collective-permute-start(bf16[4,264,128]{2,1,0:T(8,128)(2,1)S(1)} %collective-permute-done.11.refs_3_), channel_id=1, source_target_pairs={{0,4},{2,6},{4,12},{6,14},{8,0},{10,2},{12,20},{14,22},{16,8},{18,... | collective-permute-start | bytes 811016 | tf_op jit(solution)/shard_map/ppermute | solution.py:468
  46.2 0.6 collective-permute-start.8
  46.8 2.0 %shard_map.89.refs_2_ = f32[32,136,128]{2,1,0:T(8,128)S(1)} custom-call(s32[1088]{0:T(1024)S(4)} %get-tuple-element.32.list_ref, s32[8]{0:T(128)S(4)} %get-tuple-element.33.count_ref, s32[160,4,128]{2,1,0:T(4,128)S(1)} %shard_map.85.masks_ref, f32[16,8,128]{2,1,0:T(8,128)S(1)} %get-tuple-element.40.own_sc, ...), custom_call_target="tpu_custom_call", output_to_operand_aliasing={{}: (10, {})} | custom-call | flops 8000000000 | tf_op jit(solution)/shard_map/pallas_call | solution.py:350
  48.9 1.8 %collective-permute-done.16.refs_0_ = bf16[4,264,128]{2,1,0:T(8,128)(2,1)S(1)} collective-permute-done((bf16[4,264,128]{2,1,0:T(8,128)(2,1)S(1)}, bf16[4,264,128]{2,1,0:T(8,128)(2,1)S(1)}, u32[]{:S(2)}, u32[]{:S(2)}) %collective-permute-start.16) | collective-permute-done | bytes 270368 | tf_op jit(solution)/shard_map/ppermute | solution.py:468
  50.6 1.3 %collective-permute-start.17 = (bf16[2,264,128]{2,1,0:T(8,128)(2,1)S(1)}, bf16[2,264,128]{2,1,0:T(8,128)(2,1)S(1)}, u32[]{:S(2)}, u32[]{:S(2)}) collective-permute-start(bf16[2,264,128]{2,1,0:T(8,128)(2,1)S(1)} %slice.28), channel_id=1, source_target_pairs={{0,8},{2,10},{4,0},{6,2},{8,16},{10,18},{12,4},{14,6},{16,24},{18,... | collective-permute-start | bytes 405512 | tf_op jit(solution)/shard_map/ppermute | solution.py:477
  52.2 5.6 %collective-permute-done.12.refs_1_ = bf16[4,264,128]{2,1,0:T(8,128)(2,1)S(1)} collective-permute-done((bf16[4,264,128]{2,1,0:T(8,128)(2,1)S(1)}, bf16[4,264,128]{2,1,0:T(8,128)(2,1)S(1)}, u32[]{:S(2)}, u32[]{:S(2)}) %collective-permute-start.12) | collective-permute-done | bytes 270368 | tf_op jit(solution)/shard_map/ppermute | solution.py:468
  58.0 1.6 %collective-permute-start.9 = (bf16[2,264,128]{2,1,0:T(8,128)(2,1)S(1)}, bf16[2,264,128]{2,1,0:T(8,128)(2,1)S(1)}, u32[]{:S(2)}, u32[]{:S(2)}) collective-permute-start(bf16[2,264,128]{2,1,0:T(8,128)(2,1)S(1)} %slice.26), channel_id=1, source_target_pairs={{0,8},{2,10},{4,0},{6,2},{8,16},{10,18},{12,4},{14,6},{16,24},{18,... | collective-permute-start | bytes 405512 | tf_op jit(solution)/shard_map/ppermute | solution.py:477
  59.5 2.0 %shard_map.90.refs_2_ = f32[32,136,128]{2,1,0:T(8,128)S(1)} custom-call(s32[1088]{0:T(1024)S(4)} %get-tuple-element.32.list_ref, s32[8]{0:T(128)S(4)} %get-tuple-element.33.count_ref, s32[160,4,128]{2,1,0:T(4,128)S(1)} %shard_map.85.masks_ref, f32[16,8,128]{2,1,0:T(8,128)S(1)} %get-tuple-element.40.own_sc, ...), custom_call_target="tpu_custom_call", output_to_operand_aliasing={{}: (8, {})} | custom-call | flops 8000000000 | tf_op jit(solution)/shard_map/pallas_call | solution.py:350
  61.6 1.1 %shard_map.91.refs_2_ = f32[32,136,128]{2,1,0:T(8,128)S(1)} custom-call(s32[1088]{0:T(1024)S(4)} %get-tuple-element.32.list_ref, s32[8]{0:T(128)S(4)} %get-tuple-element.33.count_ref, s32[160,4,128]{2,1,0:T(4,128)S(1)} %shard_map.85.masks_ref, f32[16,8,128]{2,1,0:T(8,128)S(1)} %get-tuple-element.40.own_sc, ...), custom_call_target="tpu_custom_call", output_to_operand_aliasing={{}: (8, {})} | custom-call | flops 8000000000 | tf_op jit(solution)/shard_map/pallas_call | solution.py:350
  62.7 1.7 %shard_map.92.refs_2_ = f32[32,136,128]{2,1,0:T(8,128)S(1)} custom-call(s32[1088]{0:T(1024)S(4)} %get-tuple-element.32.list_ref, s32[8]{0:T(128)S(4)} %get-tuple-element.33.count_ref, s32[160,4,128]{2,1,0:T(4,128)S(1)} %shard_map.85.masks_ref, f32[16,8,128]{2,1,0:T(8,128)S(1)} %get-tuple-element.40.own_sc, ...), custom_call_target="tpu_custom_call", output_to_operand_aliasing={{}: (8, {})} | custom-call | flops 8000000000 | tf_op jit(solution)/shard_map/pallas_call | solution.py:350
  64.6 7.1 %collective-permute-start.22 = (bf16[16,128,128]{2,1,0:T(8,128)(2,1)S(1)}, bf16[16,128,128]{2,1,0:T(8,128)(2,1)S(1)}, u32[]{:S(2)}, u32[]{:S(2)}) collective-permute-start(bf16[16,128,128]{2,1,0:T(8,128)(2,1)S(1)} %get-tuple-element.50), channel_id=1, source_target_pairs={{0,2},{2,0},{4,6},{6,4},{8,10},{10,8},{12,14},{14,12},{16,18},{18,... | collective-permute-start | bytes 1572872 | tf_op jit(solution)/shard_map/ppermute | solution.py:535
  71.9 1.4 %collective-permute-done.23.levels_ref = f32[16,8,128]{2,1,0:T(8,128)S(1)} collective-permute-done((f32[16,8,128]{2,1,0:T(8,128)S(1)}, f32[16,8,128]{2,1,0:T(8,128)S(1)}, u32[]{:S(2)}, u32[]{:S(2)}) %collective-permute-start.23) | collective-permute-done | bytes 65568 | tf_op jit(solution)/shard_map/ppermute | solution.py:535
  73.4 1.4 %shard_map.95 = bf16[128,2048]{1,0:T(8,128)(2,1)} custom-call(f32[32,136,128]{2,1,0:T(8,128)S(1)} %shard_map.94.state_ref, bf16[16,128,128]{2,1,0:T(8,128)(2,1)S(1)} %collective-permute-done.22.sums_ref, f32[16,8,128]{2,1,0:T(8,128)S(1)} %collective-permute-done.23.levels_ref, bf16[128,2048]{1,0:T(8,128)(2,1)S(1)} %copy-done, ...), custom_call_target="tpu_custom_call" | custom-call | flops 1000000 | tf_op jit(solution)/shard_map/pallas_call | solution.py:350
  (41 shorter events, 3.5 us)
Async XLA Ops:
  1.2 16.1 %collective-permute-start.4 = (bf16[128,1024]{1,0:T(8,128)(2,1)S(1)}, bf16[128,1024]{1,0:T(8,128)(2,1)S(1)}, u32[]{:S(2)}, u32[]{:S(2)}) collective-permute-start(bf16[128,1024]{1,0:T(8,128)(2,1)S(1)} %get-tuple-element.38.refs_0_), channel_id=1, source_target_pairs={{0,1},{1,0},{2,3},{3,2},{4,5},{5,4},{6,7},{7,6},{8,9},{9,8},{10,11... | collective-permute-start | bytes 786440 | tf_op jit(solution)/shard_map/ppermute | solution.py:422
  2.5 15.4 %collective-permute-start.3 = (bf16[128,1024]{1,0:T(8,128)(2,1)S(1)}, bf16[128,1024]{1,0:T(8,128)(2,1)S(1)}, u32[]{:S(2)}, u32[]{:S(2)}) collective-permute-start(bf16[128,1024]{1,0:T(8,128)(2,1)S(1)} %get-tuple-element.37.refs_0_), channel_id=1, source_target_pairs={{0,1},{1,0},{2,3},{3,2},{4,5},{5,4},{6,7},{7,6},{8,9},{9,8},{10,11... | collective-permute-start | bytes 786440 | tf_op jit(solution)/shard_map/ppermute | solution.py:422
  15.4 5.8 %collective-permute-start.1 = (s32[80,2,128]{2,1,0:T(2,128)S(1)}, s32[80,2,128]{2,1,0:T(2,128)S(1)}, u32[]{:S(2)}, u32[]{:S(2)}) collective-permute-start(s32[80,2,128]{2,1,0:T(2,128)S(1)} %bitcast.12), channel_id=1, source_target_pairs={{0,1},{1,0},{2,3},{3,2},{4,5},{5,4},{6,7},{7,6},{8,9},{9,8},{10,11... | collective-permute-start | bytes 245768 | tf_op jit(solution)/shard_map/ppermute | solution.py:442
  16.7 4.7 %collective-permute-start = (s32[80,2,128]{2,1,0:T(2,128)S(1)}, s32[80,2,128]{2,1,0:T(2,128)S(1)}, u32[]{:S(2)}, u32[]{:S(2)}) collective-permute-start(s32[80,2,128]{2,1,0:T(2,128)S(1)} %bitcast.13), channel_id=1, source_target_pairs={{0,2},{2,0},{4,6},{6,4},{8,10},{10,8},{12,14},{14,12},{16,18},{18,... | collective-permute-start | bytes 245768 | tf_op jit(solution)/shard_map/ppermute | solution.py:443
  18.3 8.1 %collective-permute-start.10 = (bf16[4,264,128]{2,1,0:T(8,128)(2,1)S(1)}, bf16[4,264,128]{2,1,0:T(8,128)(2,1)S(1)}, u32[]{:S(2)}, u32[]{:S(2)}) collective-permute-start(bf16[4,264,128]{2,1,0:T(8,128)(2,1)S(1)} %get-tuple-element.41.refs_1_), channel_id=1, source_target_pairs={{0,4},{2,6},{4,12},{6,14},{8,0},{10,2},{12,20},{14,22},{16,8},{18,... | collective-permute-start | bytes 811016 | tf_op jit(solution)/shard_map/ppermute | solution.py:468
  18.8 7.9 %collective-permute-start.6 = (bf16[4,264,128]{2,1,0:T(8,128)(2,1)S(1)}, bf16[4,264,128]{2,1,0:T(8,128)(2,1)S(1)}, u32[]{:S(2)}, u32[]{:S(2)}) collective-permute-start(bf16[4,264,128]{2,1,0:T(8,128)(2,1)S(1)} %get-tuple-element.41.refs_1_), channel_id=1, source_target_pairs={{0,8},{2,10},{4,0},{6,2},{8,16},{10,18},{12,4},{14,6},{16,24},{18,... | collective-permute-start | bytes 811016 | tf_op jit(solution)/shard_map/ppermute | solution.py:468
  19.9 12.4 %collective-permute-start.14 = (bf16[4,264,128]{2,1,0:T(8,128)(2,1)S(1)}, bf16[4,264,128]{2,1,0:T(8,128)(2,1)S(1)}, u32[]{:S(2)}, u32[]{:S(2)}) collective-permute-start(bf16[4,264,128]{2,1,0:T(8,128)(2,1)S(1)} %get-tuple-element.42.refs_0_), channel_id=1, source_target_pairs={{0,8},{2,10},{4,0},{6,2},{8,16},{10,18},{12,4},{14,6},{16,24},{18,... | collective-permute-start | bytes 811016 | tf_op jit(solution)/shard_map/ppermute | solution.py:468
  21.3 12.1 %collective-permute-start.18 = (bf16[4,264,128]{2,1,0:T(8,128)(2,1)S(1)}, bf16[4,264,128]{2,1,0:T(8,128)(2,1)S(1)}, u32[]{:S(2)}, u32[]{:S(2)}) collective-permute-start(bf16[4,264,128]{2,1,0:T(8,128)(2,1)S(1)} %get-tuple-element.42.refs_0_), channel_id=1, source_target_pairs={{0,4},{2,6},{4,12},{6,14},{8,0},{10,2},{12,20},{14,22},{16,8},{18,... | collective-permute-start | bytes 811016 | tf_op jit(solution)/shard_map/ppermute | solution.py:468
  21.3 2.0 %collective-permute-start.2 = (s32[80,2,128]{2,1,0:T(2,128)S(1)}, s32[80,2,128]{2,1,0:T(2,128)S(1)}, u32[]{:S(2)}, u32[]{:S(2)}) collective-permute-start(s32[80,2,128]{2,1,0:T(2,128)S(1)} %collective-permute-done.1.refs_1_), channel_id=1, source_target_pairs={{0,2},{2,0},{4,6},{6,4},{8,10},{10,8},{12,14},{14,12},{16,18},{18,... | collective-permute-start | bytes 245768 | tf_op jit(solution)/shard_map/ppermute | solution.py:443
  23.4 10.3 %collective-permute-start.5 = (f32[16,8,128]{2,1,0:T(8,128)S(1)}, f32[16,8,128]{2,1,0:T(8,128)S(1)}, u32[]{:S(2)}, u32[]{:S(2)}) collective-permute-start(f32[16,8,128]{2,1,0:T(8,128)S(1)} %get-tuple-element.40.own_sc), channel_id=1, source_target_pairs={{0,2},{2,0},{4,6},{6,4},{8,10},{10,8},{12,14},{14,12},{16,18},{18,... | collective-permute-start | bytes 196616 | tf_op jit(solution)/shard_map/ppermute | solution.py:462
  26.4 18.9 %collective-permute-start.11 = (bf16[4,264,128]{2,1,0:T(8,128)(2,1)S(1)}, bf16[4,264,128]{2,1,0:T(8,128)(2,1)S(1)}, u32[]{:S(2)}, u32[]{:S(2)}) collective-permute-start(bf16[4,264,128]{2,1,0:T(8,128)(2,1)S(1)} %collective-permute-done.10.refs_5_), channel_id=1, source_target_pairs={{0,4},{2,6},{4,12},{6,14},{8,0},{10,2},{12,20},{14,22},{16,8},{18,... | collective-permute-start | bytes 811016 | tf_op jit(solution)/shard_map/ppermute | solution.py:468
  26.7 19.5 %collective-permute-start.7 = (bf16[4,264,128]{2,1,0:T(8,128)(2,1)S(1)}, bf16[4,264,128]{2,1,0:T(8,128)(2,1)S(1)}, u32[]{:S(2)}, u32[]{:S(2)}) collective-permute-start(bf16[4,264,128]{2,1,0:T(8,128)(2,1)S(1)} %collective-permute-done.6.refs_3_), channel_id=1, source_target_pairs={{0,8},{2,10},{4,0},{6,2},{8,16},{10,18},{12,4},{14,6},{16,24},{18,... | collective-permute-start | bytes 811016 | tf_op jit(solution)/shard_map/ppermute | solution.py:468
  32.2 11.6 %collective-permute-start.15 = (bf16[4,264,128]{2,1,0:T(8,128)(2,1)S(1)}, bf16[4,264,128]{2,1,0:T(8,128)(2,1)S(1)}, u32[]{:S(2)}, u32[]{:S(2)}) collective-permute-start(bf16[4,264,128]{2,1,0:T(8,128)(2,1)S(1)} %collective-permute-done.14.refs_2_), channel_id=1, source_target_pairs={{0,8},{2,10},{4,0},{6,2},{8,16},{10,18},{12,4},{14,6},{16,24},{18,... | collective-permute-start | bytes 811016 | tf_op jit(solution)/shard_map/ppermute | solution.py:468
  33.4 11.6 %collective-permute-start.19 = (bf16[4,264,128]{2,1,0:T(8,128)(2,1)S(1)}, bf16[4,264,128]{2,1,0:T(8,128)(2,1)S(1)}, u32[]{:S(2)}, u32[]{:S(2)}) collective-permute-start(bf16[4,264,128]{2,1,0:T(8,128)(2,1)S(1)} %collective-permute-done.18.refs_4_), channel_id=1, source_target_pairs={{0,4},{2,6},{4,12},{6,14},{8,0},{10,2},{12,20},{14,22},{16,8},{18,... | collective-permute-start | bytes 811016 | tf_op jit(solution)/shard_map/ppermute | solution.py:468
  43.8 6.8 %collective-permute-start.16 = (bf16[4,264,128]{2,1,0:T(8,128)(2,1)S(1)}, bf16[4,264,128]{2,1,0:T(8,128)(2,1)S(1)}, u32[]{:S(2)}, u32[]{:S(2)}) collective-permute-start(bf16[4,264,128]{2,1,0:T(8,128)(2,1)S(1)} %collective-permute-done.15.refs_0_), channel_id=1, source_target_pairs={{0,8},{2,10},{4,0},{6,2},{8,16},{10,18},{12,4},{14,6},{16,24},{18,... | collective-permute-start | bytes 811016 | tf_op jit(solution)/shard_map/ppermute | solution.py:468
  45.0 7.1 %collective-permute-start.20 = (bf16[4,264,128]{2,1,0:T(8,128)(2,1)S(1)}, bf16[4,264,128]{2,1,0:T(8,128)(2,1)S(1)}, u32[]{:S(2)}, u32[]{:S(2)}) collective-permute-start(bf16[4,264,128]{2,1,0:T(8,128)(2,1)S(1)} %collective-permute-done.19.refs_2_), channel_id=1, source_target_pairs={{0,4},{2,6},{4,12},{6,14},{8,0},{10,2},{12,20},{14,22},{16,8},{18,... | collective-permute-start | bytes 811016 | tf_op jit(solution)/shard_map/ppermute | solution.py:468
  45.3 12.6 %collective-permute-start.12 = (bf16[4,264,128]{2,1,0:T(8,128)(2,1)S(1)}, bf16[4,264,128]{2,1,0:T(8,128)(2,1)S(1)}, u32[]{:S(2)}, u32[]{:S(2)}) collective-permute-start(bf16[4,264,128]{2,1,0:T(8,128)(2,1)S(1)} %collective-permute-done.11.refs_3_), channel_id=1, source_target_pairs={{0,4},{2,6},{4,12},{6,14},{8,0},{10,2},{12,20},{14,22},{16,8},{18,... | collective-permute-start | bytes 811016 | tf_op jit(solution)/shard_map/ppermute | solution.py:468
  46.2 11.8 %collective-permute-start.8 = (bf16[4,264,128]{2,1,0:T(8,128)(2,1)S(1)}, bf16[4,264,128]{2,1,0:T(8,128)(2,1)S(1)}, u32[]{:S(2)}, u32[]{:S(2)}) collective-permute-start(bf16[4,264,128]{2,1,0:T(8,128)(2,1)S(1)} %collective-permute-done.7.refs_1_), channel_id=1, source_target_pairs={{0,8},{2,10},{4,0},{6,2},{8,16},{10,18},{12,4},{14,6},{16,24},{18,... | collective-permute-start | bytes 811016 | tf_op jit(solution)/shard_map/ppermute | solution.py:468
  50.6 12.0 %collective-permute-start.17 = (bf16[2,264,128]{2,1,0:T(8,128)(2,1)S(1)}, bf16[2,264,128]{2,1,0:T(8,128)(2,1)S(1)}, u32[]{:S(2)}, u32[]{:S(2)}) collective-permute-start(bf16[2,264,128]{2,1,0:T(8,128)(2,1)S(1)} %slice.28), channel_id=1, source_target_pairs={{0,8},{2,10},{4,0},{6,2},{8,16},{10,18},{12,4},{14,6},{16,24},{18,... | collective-permute-start | bytes 405512 | tf_op jit(solution)/shard_map/ppermute | solution.py:477
  52.1 10.6 %collective-permute-start.21 = (bf16[2,264,128]{2,1,0:T(8,128)(2,1)S(1)}, bf16[2,264,128]{2,1,0:T(8,128)(2,1)S(1)}, u32[]{:S(2)}, u32[]{:S(2)}) collective-permute-start(bf16[2,264,128]{2,1,0:T(8,128)(2,1)S(1)} %slice.29), channel_id=1, source_target_pairs={{0,4},{2,6},{4,12},{6,14},{8,0},{10,2},{12,20},{14,22},{16,8},{18,... | collective-permute-start | bytes 405512 | tf_op jit(solution)/shard_map/ppermute | solution.py:477
  57.9 6.5 %collective-permute-start.13 = (bf16[2,264,128]{2,1,0:T(8,128)(2,1)S(1)}, bf16[2,264,128]{2,1,0:T(8,128)(2,1)S(1)}, u32[]{:S(2)}, u32[]{:S(2)}) collective-permute-start(bf16[2,264,128]{2,1,0:T(8,128)(2,1)S(1)} %slice.27), channel_id=1, source_target_pairs={{0,4},{2,6},{4,12},{6,14},{8,0},{10,2},{12,20},{14,22},{16,8},{18,... | collective-permute-start | bytes 405512 | tf_op jit(solution)/shard_map/ppermute | solution.py:477
  58.0 6.4 %collective-permute-start.9 = (bf16[2,264,128]{2,1,0:T(8,128)(2,1)S(1)}, bf16[2,264,128]{2,1,0:T(8,128)(2,1)S(1)}, u32[]{:S(2)}, u32[]{:S(2)}) collective-permute-start(bf16[2,264,128]{2,1,0:T(8,128)(2,1)S(1)} %slice.26), channel_id=1, source_target_pairs={{0,8},{2,10},{4,0},{6,2},{8,16},{10,18},{12,4},{14,6},{16,24},{18,... | collective-permute-start | bytes 405512 | tf_op jit(solution)/shard_map/ppermute | solution.py:477
  64.6 8.8 %collective-permute-start.22 = (bf16[16,128,128]{2,1,0:T(8,128)(2,1)S(1)}, bf16[16,128,128]{2,1,0:T(8,128)(2,1)S(1)}, u32[]{:S(2)}, u32[]{:S(2)}) collective-permute-start(bf16[16,128,128]{2,1,0:T(8,128)(2,1)S(1)} %get-tuple-element.50), channel_id=1, source_target_pairs={{0,2},{2,0},{4,6},{6,4},{8,10},{10,8},{12,14},{14,12},{16,18},{18,... | collective-permute-start | bytes 1572872 | tf_op jit(solution)/shard_map/ppermute | solution.py:535
  71.7 1.6 %collective-permute-start.23 = (f32[16,8,128]{2,1,0:T(8,128)S(1)}, f32[16,8,128]{2,1,0:T(8,128)S(1)}, u32[]{:S(2)}, u32[]{:S(2)}) collective-permute-start(f32[16,8,128]{2,1,0:T(8,128)S(1)} %get-tuple-element.51), channel_id=1, source_target_pairs={{0,2},{2,0},{4,6},{6,4},{8,10},{10,8},{12,14},{14,12},{16,18},{18,... | collective-permute-start | bytes 196616 | tf_op jit(solution)/shard_map/ppermute | solution.py:535
  71.8 1.6 %copy-start = (bf16[128,2048]{1,0:T(8,128)(2,1)S(1)}, bf16[128,2048]{1,0:T(8,128)(2,1)}, u32[]{:S(2)}) copy-start(bf16[128,2048]{1,0:T(8,128)(2,1)} %x_ref.1) | copy-start | bytes 1572868
